TPU v7x, 32 devices: a whole 2x2x4 slice. The times are simulated.
32 devices in a mesh: grp: 8 (over z, x), ep: 4 (over y, core).
Axes of the slice: x: 2, y: 2, z: 4, core: 2. Of those that a mesh axis runs over, the one named last changes fastest.
Arguments:
- out_grad: bfloat16 [256, 4096], P('grp', 'ep'), may hold values from -6 to 6
- expert_ids: int32 [256, 8], P('grp'), may hold values from 0 to 15, as said below
- router_logits: float32 [256, 16], P('grp'), may hold values from -5 to 5
- router_weight: bfloat16 [16, 4096], P(None, 'ep'), may hold values from -0.09375 to 0.09375
- expert_weight: bfloat16 [16, 4096, 1024], P('grp', 'ep'), may hold values from -0.1875 to 0.1875
- hidden_saved: bfloat16 [8, 512, 1024], P('grp'), may hold values from -6 to 6
Outputs:
- weight_grad: bfloat16 [16, 4096, 1024], P('grp', 'ep')
- hidden_grad: bfloat16 [8, 512, 1024], P('grp', 'ep')
- input_grad: bfloat16 [256, 4096], P('grp', 'ep')
Inputs may be any that keep to these rules, and one draw needn't show every extreme that they name: `expert_ids`: each row names 8 different experts, lying in at most 4 of the 4 groups of 4 consecutive experts. In each aligned block of 32 rows no expert is named by more than 32 rows, and some expert is named by exactly 32.
All inputs are finite; a program needn't handle non-finite values.
Results may differ from a plain program's by a relative error of at most 0.02.
Values may be sent and summed in bfloat16 or wider, within the bound.
No kernel may reach another device: no remote copies, remote signals or barrier semaphores. Data moves between devices by JAX's collectives and lax.ppermute only.
A program may use at most 64 MiB of HBM per device.

v0:
```python
import jax
import jax.numpy as jnp
from jax import lax
from jax.sharding import PartitionSpec as P

route_scale = 2.5


def body(out_grad, expert_ids, router_logits, router_weight, expert_weight, hidden_saved):
    group_rows, features = out_grad.shape
    top_count = expert_ids.shape[1]
    experts = router_logits.shape[1]
    group_count = lax.axis_size("grp")
    local_experts = expert_weight.shape[0]
    hidden_width = expert_weight.shape[2]
    slot_count = hidden_saved.shape[1]
    capacity = slot_count // (local_experts * group_count)
    expert_span = group_count * capacity
    pair_count = group_rows * top_count
    sig_values = jax.nn.sigmoid(router_logits)
    picked = expert_ids[:, :, None] == jnp.arange(experts, dtype=jnp.int32)[None, None, :]
    chosen = jnp.sum(jnp.where(picked, sig_values[:, None, :], 0.0), axis=2)
    route_probs = route_scale * chosen / jnp.sum(chosen, axis=1, keepdims=True)
    flat_ids = expert_ids.reshape(pair_count)
    onehot = picked.reshape(pair_count, experts).astype(jnp.int32)
    pair_ranks = jnp.sum((jnp.cumsum(onehot, axis=0) - 1) * onehot, axis=1)
    slot_place = (
        flat_ids % local_experts * group_count + flat_ids // local_experts
    ) * capacity + pair_ranks
    slot_match = slot_place[None, :] == jnp.arange(slot_count, dtype=jnp.int32)[:, None]
    token_pick = jnp.sum(
        slot_match.reshape(slot_count, group_rows, top_count).astype(jnp.float32), axis=2
    ).astype(jnp.bfloat16)
    send_rows = jnp.dot(token_pick, out_grad, preferred_element_type=jnp.float32).astype(
        jnp.bfloat16
    )
    send_prob = jnp.sum(
        jnp.where(slot_match, route_probs.reshape(1, pair_count), 0.0), axis=1
    ).astype(jnp.bfloat16)
    got_rows, got_prob = (
        lax.all_to_all(
            send_rows.reshape(local_experts, group_count, capacity, features),
            "grp",
            split_axis=1,
            concat_axis=1,
            tiled=True,
        ),
        lax.all_to_all(
            send_prob.reshape(local_experts, group_count, capacity),
            "grp",
            split_axis=1,
            concat_axis=1,
            tiled=True,
        ),
    )
    slot_grads = got_rows.reshape(local_experts, expert_span, features)
    prob_rows = got_prob.reshape(local_experts, expert_span).astype(jnp.float32)
    saved_rows = hidden_saved.reshape(local_experts, expert_span, hidden_width)
    scaled_rows = (prob_rows[:, :, None] * slot_grads.astype(jnp.float32)).astype(jnp.bfloat16)
    weight_grad = jnp.einsum(
        "lmd,lmf->ldf", scaled_rows, saved_rows, preferred_element_type=jnp.float32
    ).astype(jnp.bfloat16)
    owner_index = lax.axis_index("ep")
    share_rows = slot_count // lax.axis_size("ep")
    flat_prob = prob_rows.reshape(slot_count)
    flat_saved = hidden_saved.reshape(slot_count, hidden_width)
    partial_term = jnp.einsum(
        "lmd,ldf->lmf", slot_grads, expert_weight, preferred_element_type=jnp.float32
    ).reshape(slot_count, hidden_width)
    rounded_term = lax.optimization_barrier(partial_term.astype(jnp.bfloat16)).astype(jnp.float32)
    partial_score = jnp.sum(flat_saved.astype(jnp.float32) * rounded_term, axis=1)
    moved_scores = lax.all_to_all(
        partial_score.reshape(local_experts, group_count, capacity),
        "grp",
        split_axis=1,
        concat_axis=1,
        tiled=True,
    )
    returned = lax.psum(moved_scores, "ep")
    summed = lax.psum_scatter(
        partial_term.astype(jnp.bfloat16), "ep", scatter_dimension=0, tiled=True
    ).astype(jnp.float32)
    own_prob = lax.dynamic_slice_in_dim(flat_prob, owner_index * share_rows, share_rows, 0)
    hidden_grad = (own_prob[:, None] * summed).astype(jnp.bfloat16)[None]
    pair_score = jnp.sum(
        jnp.where(slot_match, returned.reshape(slot_count, 1), 0.0), axis=0
    ).reshape(group_rows, top_count)
    weighted_mean = jnp.sum(route_probs * pair_score, axis=1, keepdims=True) / route_scale
    logit_terms = route_probs * (1.0 - chosen) * (pair_score - weighted_mean)
    router_grad = jnp.sum(jnp.where(picked, logit_terms[:, :, None], 0.0), axis=1).astype(
        jnp.bfloat16
    )
    input_grad = jnp.dot(router_grad, router_weight, preferred_element_type=jnp.float32).astype(
        jnp.bfloat16
    )
    return (weight_grad, hidden_grad, input_grad)


def solution(mesh):
    in_specs = (
        P("grp", "ep"),
        P("grp", None),
        P("grp", None),
        P(None, "ep"),
        P("grp", "ep", None),
        P("grp", None, None),
    )
    out_specs = (P("grp", "ep", None), P("grp", "ep", None), P("grp", "ep"))
    return jax.shard_map(body, mesh=mesh, in_specs=in_specs, out_specs=out_specs, check_vma=False)
```

profile of v0, /device:TPU:0, one launch (start us, length us, event | category | flops | bytes accessed | tf_op | source)
XLA Modules:
  0.0 89.7 jit_solution(18396075402777026776)
XLA Ops:
  7.2 0.0 copy-start
  7.2 0.8 copy.70
  8.0 0.1 reshape.192
  8.1 0.1 eq.55
  8.2 0.6 reduce-window.6
  8.8 0.2 slice_reduce_fusion
  9.0 0.1 fusion.9
  9.1 0.1 reduce_sum.87
  9.2 0.2 convert_reduce_fusion
  9.4 0.0 copy-done
  9.4 0.4 convolution_convert_fusion.2
  9.9 0.0 copy-start.4
  9.9 0.0 copy-start.2
  9.9 1.1 %copy.80 = bf16[2,8,32,1024]{3,2,0,1:T(8,128)(2,1)} copy(bf16[2,8,32,1024]{3,2,1,0:T(8,128)(2,1)S(1)} %bitcast.33) | data formatting | bytes 2097152 | tf_op jit(solution)/shard_map/reshape | solution.py:42
  11.0 7.3 %all-to-all-start.1 = ((bf16[2,8,32,1024]{3,2,0,1:T(8,128)(2,1)}), bf16[2,8,32,1024]{3,2,0,1:T(8,128)(2,1)S(1)}, u32[]{:S(2)}, u32[]{:S(2)}) async-start(bf16[2,8,32,1024]{3,2,0,1:T(8,128)(2,1)} %copy.80), calls=%async_computation.1 | async-start | bytes 2097152 | tf_op jit(solution)/shard_map/all_to_all | solution.py:41
  18.3 0.0 reduce-scatter.2.cloned.1.call-start
  18.3 0.0 copy-done.4
  18.3 0.0 copy-done.2
  18.4 25.7 %all-to-all-done.1 = bf16[2,8,32,1024]{3,2,0,1:T(8,128)(2,1)S(1)} async-done(((bf16[2,8,32,1024]{3,2,0,1:T(8,128)(2,1)}), bf16[2,8,32,1024]{3,2,0,1:T(8,128)(2,1)S(1)}, u32[]{:S(2)}, u32[]{:S(2)}) %all-to-all-start.1) | async-done | bytes 1048608 | tf_op jit(solution)/shard_map/all_to_all | solution.py:41
  44.0 0.1 copy.81
  44.1 0.0 copy-start.1
  44.1 4.5 %convolution_convert_fusion.1 = bf16[2,256,1024]{2,1,0:T(8,128)(2,1)} fusion(bf16[2,256,1024]{2,1,0:T(8,128)(2,1)S(1)} %bitcast.35, bf16[2,1024,1024]{2,1,0:T(8,128)(2,1)} %param.10), kind=kOutput, calls=%fused_computation.4 | convolution fusion | flops 1074266112 | bytes 6291456 | tf_op jit(solution)/shard_map/lmd,ldf->lmf/dot_general | solution.py:67
  48.7 0.0 copy-start.3
  48.7 0.0 reduce-scatter.2.cloned.1.call-update
  48.7 0.0 copy-done.1
  48.7 1.6 %fusion = f32[512]{0:T(512)S(1)} fusion(bf16[512,1024]{1,0:T(8,128)(2,1)} %bitcast.32, bf16[1,512,1024]{2,1,0:T(8,128)(2,1)S(1)} %copy-done.1), kind=kLoop, calls=%fused_computation.2 | loop fusion | flops 2096640 | bytes 2099200 | tf_op jit(solution)/shard_map/reduce_sum | solution.py:71
  50.3 0.1 reshape.197
  50.4 0.6 copy.83
  51.0 3.6 %all-to-all-start.2 = ((f32[2,8,32]{2,0,1:T(2,128)}), f32[2,8,32]{2,0,1:T(2,128)S(1)}, u32[]{:S(2)}, u32[]{:S(2)}) async-start(f32[2,8,32]{2,0,1:T(2,128)} %copy.83), calls=%async_computation.3 | async-start | bytes 16384 | tf_op jit(solution)/shard_map/all_to_all | solution.py:72
  54.6 0.1 copy.73
  54.7 0.1 div.50
  54.8 6.3 %all-to-all-done.2 = f32[2,8,32]{2,0,1:T(2,128)S(1)} async-done(((f32[2,8,32]{2,0,1:T(2,128)}), f32[2,8,32]{2,0,1:T(2,128)S(1)}, u32[]{:S(2)}, u32[]{:S(2)}) %all-to-all-start.2) | async-done | bytes 2080 | tf_op jit(solution)/shard_map/all_to_all | solution.py:72
  61.1 0.1 broadcast_in_dim.64
  61.2 5.6 %psum.7 = f32[512]{0:T(512)S(1)} all-reduce(f32[512]{0:T(512)S(1)} %broadcast_in_dim.64), channel_id=1, replica_groups=mesh['grp'=8,'ep'=4] {'ep'}, use_global_device_ids=true, to_apply=%region_9.10 | all-reduce | flops 512 | bytes 4096 | tf_op jit(solution)/shard_map/psum | solution.py:79
  66.8 0.3 select_reduce_fusion
  67.1 0.1 convert_element_type.76
  67.2 0.6 copy.74
  67.8 3.3 %all-to-all-start = ((bf16[2,8,32]{2,0,1:T(2,128)(2,1)}), bf16[2,8,32]{2,0,1:T(2,128)(2,1)S(1)}, u32[]{:S(2)}, u32[]{:S(2)}) async-start(bf16[2,8,32]{2,0,1:T(2,128)(2,1)} %copy.74), calls=%async_computation | async-start | bytes 8192 | tf_op jit(solution)/shard_map/all_to_all | solution.py:48
  71.1 0.1 reshape.198
  71.2 0.1 copy.86
  71.3 0.0 copy-done.3
  71.3 0.8 convolution_convert_fusion.3
  72.1 5.3 %all-to-all-done = bf16[2,8,32]{2,0,1:T(2,128)(2,1)S(1)} async-done(((bf16[2,8,32]{2,0,1:T(2,128)(2,1)}), bf16[2,8,32]{2,0,1:T(2,128)(2,1)S(1)}, u32[]{:S(2)}, u32[]{:S(2)}) %all-to-all-start) | async-done | bytes 1056 | tf_op jit(solution)/shard_map/all_to_all | solution.py:48
  77.4 0.1 reshape.200
  77.5 0.1 reshape.199
  77.6 0.1 dynamic_slice.3
  77.7 3.4 %convolution_convert_fusion = bf16[2,1024,1024]{2,1,0:T(8,128)(2,1)} fusion(bf16[2,256,1024]{2,1,0:T(8,128)(2,1)S(1)} %bitcast.34, bf16[2,256,1024]{2,1,0:T(8,128)(2,1)S(1)} %bitcast.36, f32[2,256]{1,0:T(2,128)S(1)} %reshape.199), kind=kOutput, calls=%fused_computation | convolution fusion | flops 1077411840 | bytes 6293504 | tf_op jit(solution)/shard_map/lmd,lmf->ldf/dot_general | solution.py:60
  81.0 0.0 reduce-scatter.2.cloned.1.call-done
  81.0 1.8 %fusion.2 = bf16[1,128,1024]{2,1,0:T(8,128)(2,1)} fusion(bf16[128,1024]{1,0:T(8,128)(2,1)} %reduce-scatter.2.cloned.1.call-done, f32[128]{0:T(128)S(1)} %dynamic_slice.3), kind=kLoop, calls=%fused_computation.14 | loop fusion | flops 393216 | bytes 524800 | tf_op jit(solution)/shard_map/broadcast_in_dim | solution.py:84
  (14 shorter events, 0.2 us)
Async XLA Ops:
  7.2 2.3 %copy-start = (bf16[32,1024]{1,0:T(8,128)(2,1)S(1)}, bf16[32,1024]{1,0:T(8,128)(2,1)}, u32[]{:S(2)}) copy-start(bf16[32,1024]{1,0:T(8,128)(2,1)} %param.6) | copy-start | bytes 196612
  9.9 8.4 %copy-start.4 = (f32[32,16]{0,1:T(8,128)S(1)}, f32[32,16]{0,1:T(8,128)}, u32[]{:S(2)}) copy-start(f32[32,16]{0,1:T(8,128)} %param.8) | copy-start | bytes 6148
  9.9 8.4 %copy-start.2 = (s32[32,8]{0,1:T(8,128)S(1)}, s32[32,8]{0,1:T(8,128)}, u32[]{:S(2)}) copy-start(s32[32,8]{0,1:T(8,128)} %param.7) | copy-start | bytes 3076
  11.0 33.0 %all-to-all-start.1 = ((bf16[2,8,32,1024]{3,2,0,1:T(8,128)(2,1)}), bf16[2,8,32,1024]{3,2,0,1:T(8,128)(2,1)S(1)}, u32[]{:S(2)}, u32[]{:S(2)}) async-start(bf16[2,8,32,1024]{3,2,0,1:T(8,128)(2,1)} %copy.80), calls=%async_computation.1 | async-start | bytes 2097152 | tf_op jit(solution)/shard_map/all_to_all | solution.py:41
  18.3 62.8 %reduce-scatter.2.cloned.1.call-start = ((), (), s32[]{:S(2)}) async-start(), calls=%async_computation.4 | async-start | bytes 1310720 | tf_op jit(solution)/shard_map/reduce_scatter | solution.py:80
  44.1 4.6 %copy-start.1 = (bf16[1,512,1024]{2,1,0:T(8,128)(2,1)S(1)}, bf16[1,512,1024]{2,1,0:T(8,128)(2,1)}, u32[]{:S(2)}) copy-start(bf16[1,512,1024]{2,1,0:T(8,128)(2,1)} %param.11) | copy-start | bytes 3145732
  48.7 22.6 %copy-start.3 = (bf16[16,1024]{1,0:T(8,128)(2,1)S(1)}, bf16[16,1024]{1,0:T(8,128)(2,1)}, u32[]{:S(2)}) copy-start(bf16[16,1024]{1,0:T(8,128)(2,1)} %param.9) | copy-start | bytes 98308
  51.0 10.1 %all-to-all-start.2 = ((f32[2,8,32]{2,0,1:T(2,128)}), f32[2,8,32]{2,0,1:T(2,128)S(1)}, u32[]{:S(2)}, u32[]{:S(2)}) async-start(f32[2,8,32]{2,0,1:T(2,128)} %copy.83), calls=%async_computation.3 | async-start | bytes 16384 | tf_op jit(solution)/shard_map/all_to_all | solution.py:72
  67.8 9.7 %all-to-all-start = ((bf16[2,8,32]{2,0,1:T(2,128)(2,1)}), bf16[2,8,32]{2,0,1:T(2,128)(2,1)S(1)}, u32[]{:S(2)}, u32[]{:S(2)}) async-start(bf16[2,8,32]{2,0,1:T(2,128)(2,1)} %copy.74), calls=%async_computation | async-start | bytes 8192 | tf_op jit(solution)/shard_map/all_to_all | solution.py:48
Sparse Core Ops, SparseCore 0:
  48.8 23.8 reduce-scatter.1
where the time goes:
time: 90 us; the launch traced here: 89.7 us
  waiting for transfers between devices  37.3 us (41%)
  starting transfers between devices  14.2 us (16%)
  between operations  14.2 us (16%)
  matrix products  9.16 us (10%)
  blocking collectives  5.63 us (6%)
  other arithmetic  4.71 us (5%)
  local copies, waits for them, and re-layouts  4.43 us (5%)
    all_to_all x1, waiting for transfers between devices, body(): lax.all_to_all(send_rows.reshape(local_experts, group_count, capacity, fe...  25.7 us
    all_to_all x1, starting transfers between devices, body(): lax.all_to_all(send_rows.reshape(local_experts, group_count, capacity, fe...  7.28 us
    all_to_all x1, waiting for transfers between devices, body(): lax.all_to_all(partial_score.reshape(local_experts, group_count, capacity...  6.34 us
    psum x1, blocking collectives, body(): returned = lax.psum(moved_scores, 'ep')  5.63 us
    all_to_all x1, waiting for transfers between devices, body(): lax.all_to_all(send_prob.reshape(local_experts, group_count, capacity), '...  5.3 us
    dot_general x1, matrix products, body(): jnp.einsum('lmd,ldf->lmf', slot_grads, expert_weight, preferred_element_t...  4.52 us
    all_to_all x1, starting transfers between devices, body(): lax.all_to_all(partial_score.reshape(local_experts, group_count, capacity...  3.59 us
    dot_general x1, matrix products, body(): jnp.einsum('lmd,lmf->ldf', scaled_rows, saved_rows, preferred_element_typ...  3.38 us
  transfers between devices with their start and end apart: 4, of which 3 were waited for; matrix products, arithmetic and copies ran while one was open for 9% of the time, Pallas kernels for 0%

commit v1 on v0

--- a/solution.py
+++ b/solution.py
@@ -4,9 +4,10 @@
 from jax.sharding import PartitionSpec as P
 
 route_scale = 2.5
-
-
-def body(out_grad, expert_ids, router_logits, router_weight, expert_weight, hidden_saved):
+LANES = 128
+
+
+def slot_plan(out_grad, expert_ids, router_logits, router_weight, expert_weight, hidden_saved):
     group_rows, features = out_grad.shape
     top_count = expert_ids.shape[1]
     experts = router_logits.shape[1]
@@ -37,22 +38,10 @@
     send_prob = jnp.sum(
         jnp.where(slot_match, route_probs.reshape(1, pair_count), 0.0), axis=1
     ).astype(jnp.bfloat16)
-    got_rows, got_prob = (
-        lax.all_to_all(
-            send_rows.reshape(local_experts, group_count, capacity, features),
-            "grp",
-            split_axis=1,
-            concat_axis=1,
-            tiled=True,
-        ),
-        lax.all_to_all(
-            send_prob.reshape(local_experts, group_count, capacity),
-            "grp",
-            split_axis=1,
-            concat_axis=1,
-            tiled=True,
-        ),
-    )
+    swap = dict(split_axis=1, concat_axis=1, tiled=True)
+    shape = (local_experts, group_count, capacity)
+    got_rows = lax.all_to_all(send_rows.reshape(shape + (features,)), "grp", **swap)
+    got_prob = lax.all_to_all(send_prob.reshape(shape), "grp", **swap)
     slot_grads = got_rows.reshape(local_experts, expert_span, features)
     prob_rows = got_prob.reshape(local_experts, expert_span).astype(jnp.float32)
     saved_rows = hidden_saved.reshape(local_experts, expert_span, hidden_width)
@@ -69,13 +58,7 @@
     ).reshape(slot_count, hidden_width)
     rounded_term = lax.optimization_barrier(partial_term.astype(jnp.bfloat16)).astype(jnp.float32)
     partial_score = jnp.sum(flat_saved.astype(jnp.float32) * rounded_term, axis=1)
-    moved_scores = lax.all_to_all(
-        partial_score.reshape(local_experts, group_count, capacity),
-        "grp",
-        split_axis=1,
-        concat_axis=1,
-        tiled=True,
-    )
+    moved_scores = lax.all_to_all(partial_score.reshape(shape), "grp", **swap)
     returned = lax.psum(moved_scores, "ep")
     summed = lax.psum_scatter(
         partial_term.astype(jnp.bfloat16), "ep", scatter_dimension=0, tiled=True
@@ -96,6 +79,135 @@
     return (weight_grad, hidden_grad, input_grad)
 
 
+def exchange(x, distance):
+    count = lax.axis_size("grp")
+    return lax.ppermute(x, "grp", [(i, i ^ distance) for i in range(count)])
+
+
+def gather_blocks(x):
+    count = lax.axis_size("grp")
+    blocks = {0: x}
+    far = sorted(range(2, count, 2), key=lambda d: (d != count // 2, -d))
+    for distance in far:
+        blocks[distance] = exchange(x, distance)
+    for distance in [0] + far:
+        blocks[distance ^ 1] = exchange(blocks[distance], 1)
+    return [blocks[d] for d in range(count)]
+
+
+def token_plan(out_grad, expert_ids, router_logits, router_weight, expert_weight, hidden_saved):
+    group_rows, features = out_grad.shape
+    experts = router_logits.shape[1]
+    group_count, ep_count = lax.axis_size("grp"), lax.axis_size("ep")
+    local_experts, _, hidden_width = expert_weight.shape
+    slot_count = hidden_saved.shape[1]
+    capacity = slot_count // (local_experts * group_count)
+    expert_span = group_count * capacity
+    token_count = group_count * group_rows
+    own_group, own_ep = lax.axis_index("grp"), lax.axis_index("ep")
+
+    sig = jax.nn.sigmoid(router_logits).T
+    named = jnp.any(
+        expert_ids.T[None] == jnp.arange(experts, dtype=jnp.int32)[:, None, None], axis=1
+    )
+    chosen = jnp.where(named, sig, 0.0)
+    probs = route_scale * chosen / jnp.sum(chosen, axis=0, keepdims=True)
+    upto = jnp.arange(group_rows)[:, None] <= jnp.arange(group_rows)[None, :]
+    ranks = jnp.dot(
+        named.astype(jnp.bfloat16), upto.astype(jnp.bfloat16), preferred_element_type=jnp.float32
+    )
+    ranks = jnp.where(named, ranks, 0.0)
+
+    pad = -2 * experts % LANES
+    packed = jnp.concatenate(
+        [
+            out_grad,
+            probs.T.astype(jnp.bfloat16),
+            ranks.T.astype(jnp.bfloat16),
+            jnp.zeros((group_rows, pad), jnp.bfloat16),
+        ],
+        axis=1,
+    )
+    blocks = gather_blocks(packed)
+    rows = jnp.concatenate([b[:, :features] for b in blocks], axis=0)
+    aux = jnp.concatenate([b[:, features:] for b in blocks], axis=0)
+    own_experts = own_group * local_experts
+    slot_probs = lax.dynamic_slice_in_dim(aux, own_experts, local_experts, 1).T
+    slot_ranks = lax.dynamic_slice_in_dim(aux, experts + own_experts, local_experts, 1).T
+    source = (jnp.arange(token_count, dtype=jnp.int32) // group_rows) ^ own_group
+    place = jnp.where(
+        slot_ranks > 0, source[None] * capacity + slot_ranks.astype(jnp.int32) - 1, -1
+    )
+    pick = place[:, None, :] == jnp.arange(expert_span, dtype=jnp.int32)[None, :, None]
+    pick_rows = pick.astype(jnp.bfloat16)
+    slot_grads = jnp.einsum(
+        "lmt,td->lmd", pick_rows, rows, preferred_element_type=jnp.float32
+    ).astype(jnp.bfloat16)
+    prob_rows = jnp.sum(jnp.where(pick, slot_probs[:, None, :].astype(jnp.float32), 0.0), axis=2)
+    saved_rows = hidden_saved.reshape(local_experts, expert_span, hidden_width)
+    partial_term = jnp.einsum(
+        "lmd,ldf->lmf", slot_grads, expert_weight, preferred_element_type=jnp.float32
+    ).astype(jnp.bfloat16)
+    partial_term = lax.optimization_barrier(partial_term)
+    partial_score = jnp.sum(
+        saved_rows.astype(jnp.float32) * partial_term.astype(jnp.float32), axis=2
+    )
+    to_blocks = partial_score.reshape(local_experts, group_count, capacity).transpose(1, 0, 2)
+    to_all = jnp.broadcast_to(
+        to_blocks[:, None], (group_count, ep_count, local_experts, capacity)
+    ).reshape(group_count * ep_count, local_experts * capacity)
+    from_all = lax.all_to_all(to_all, ("grp", "ep"), 0, 0, tiled=True)
+
+    scaled_rows = (prob_rows[:, :, None] * slot_grads.astype(jnp.float32)).astype(jnp.bfloat16)
+    weight_grad = jnp.einsum(
+        "lmd,lmf->ldf", scaled_rows, saved_rows, preferred_element_type=jnp.float32
+    ).astype(jnp.bfloat16)
+
+    share_rows = slot_count // ep_count
+    held = partial_term.reshape(1, slot_count, hidden_width)
+    bit = 1
+    piece = partial_term.reshape(ep_count, share_rows, hidden_width)
+    while bit < ep_count:
+        pairs = [(i, i ^ bit) for i in range(ep_count)]
+        left = piece.shape[0] // 2
+        own_bit = (own_ep // bit) % 2
+        halves = piece.reshape(left, 2, share_rows, hidden_width)
+        keep = lax.dynamic_index_in_dim(halves, own_bit, 1, False)
+        send = lax.dynamic_index_in_dim(halves, 1 - own_bit, 1, False)
+        got = lax.ppermute(send, "ep", pairs)
+        total = keep.astype(jnp.float32) + got.astype(jnp.float32)
+        piece = total.astype(jnp.bfloat16) if left > 1 else total
+        bit *= 2
+    summed = piece.reshape(share_rows, hidden_width)
+    own_prob = lax.dynamic_slice_in_dim(
+        prob_rows.reshape(slot_count), own_ep * share_rows, share_rows, 0
+    )
+    hidden_grad = (own_prob[:, None] * summed).astype(jnp.bfloat16)[None]
+
+    returned = jnp.sum(
+        from_all.reshape(group_count, ep_count, local_experts, capacity), axis=1
+    ).reshape(experts, capacity)
+    at_rank = ranks[:, None, :] == jnp.arange(1, capacity + 1, dtype=jnp.float32)[None, :, None]
+    scores = jnp.sum(jnp.where(at_rank, returned[:, :, None], 0.0), axis=1)
+    mean = jnp.sum(probs * scores, axis=0, keepdims=True) / route_scale
+    router_grad = jnp.where(named, probs * (1.0 - sig) * (scores - mean), 0.0).astype(jnp.bfloat16)
+    input_grad = lax.dot_general(
+        router_grad, router_weight, (((0,), (0,)), ((), ())), preferred_element_type=jnp.float32
+    ).astype(jnp.bfloat16)
+    return (weight_grad, hidden_grad, input_grad)
+
+
+def body(out_grad, expert_ids, router_logits, router_weight, expert_weight, hidden_saved):
+    group_count, ep_count = lax.axis_size("grp"), lax.axis_size("ep")
+    tokens = out_grad.shape[0] * group_count
+    slots = hidden_saved.shape[1]
+    powers = group_count & (group_count - 1) == 0 and ep_count & (ep_count - 1) == 0
+    plan = token_plan if tokens <= slots and powers else slot_plan
+    return plan(
+        out_grad, expert_ids, router_logits, router_weight, expert_weight, hidden_saved
+    )
+
+
 def solution(mesh):
     in_specs = (
         P("grp", "ep"),

time: 90 us -> 50.7 us (0.56)
  waiting for transfers between devices: 37.3 us -> 14.7 us
  between operations: 14.2 us -> 0.85 us
  blocking collectives: 5.63 us -> 0 us
  starting transfers between devices: 14.2 us -> 15.9 us
    all_to_all x3 -> x1, waiting for transfers between devices: 37.3 us -> 2.55 us  [token_plan(): from_all = lax.all_to_all(to_all, ('grp', 'ep'), 0, 0, tiled=True)]
    ppermute x0 -> x9, waiting for transfers between devices: none -> 12.2 us  [the longest x2 6.71 us: token_plan(): got = lax.ppermute(send, 'ep', pairs)]
    ppermute x0 -> x9, starting transfers between devices: none -> 11.6 us  [the longest x7 10.8 us: exchange(): return lax.ppermute(x, 'grp', [(i, i ^ distance) for i in range(count)])]
    all_to_all x3 -> x1, starting transfers between devices: 14.2 us -> 4.26 us  [token_plan(): from_all = lax.all_to_all(to_all, ('grp', 'ep'), 0, 0, tiled=True)]
    psum x1 -> x0, blocking collectives: 5.63 us -> none  [body(): returned = lax.psum(moved_scores, 'ep')]
    convert_element_type x2 -> x5, other arithmetic: 0.01 us -> 2.86 us  [the longest x1 1.24 us: token_plan(): piece = total.astype(jnp.bfloat16) if left > 1 else total]
    reshape x6 -> x2, local copies, waits for them, and re-layouts: 1.99 us -> 0.17 us  [the longest x1 0.09 us: token_plan(): from_all.reshape(group_count, ep_count, local_experts, capacity)]
    broadcast_in_dim x1 -> x0, other arithmetic: 1.76 us -> none  [body(): hidden_grad = (own_prob[:, None] * summed).astype(jnp.bfloat16)[None]]
  transfers between devices with their start and end apart: 4 -> 10, of which waited for: 3 -> 4; matrix products, arithmetic and copies ran while one was open for 9% -> 15% of each run, Pallas kernels for 0% -> 0%
where the time goes in v1:
time: 50.7 us; the launch traced here: 50.2 us
  starting transfers between devices  15.9 us (31%)
  waiting for transfers between devices  14.7 us (29%)
  matrix products  9.02 us (18%)
  other arithmetic  5.2 us (10%)
  local copies, waits for them, and re-layouts  4.57 us (9%)
  between operations  0.85 us (2%)
    ppermute x7, starting transfers between devices, exchange(): return lax.ppermute(x, 'grp', [(i, i ^ distance) for i in range(count)])  10.8 us
    ppermute x2, waiting for transfers between devices, token_plan(): got = lax.ppermute(send, 'ep', pairs)  6.71 us
    ppermute x7, waiting for transfers between devices, exchange(): return lax.ppermute(x, 'grp', [(i, i ^ distance) for i in range(count)])  5.45 us
    all_to_all x1, starting transfers between devices, token_plan(): from_all = lax.all_to_all(to_all, ('grp', 'ep'), 0, 0, tiled=True)  4.26 us
    dot_general x1, matrix products, token_plan(): jnp.einsum('lmd,ldf->lmf', slot_grads, expert_weight, preferred_element_t...  3.53 us
    dot_general x1, matrix products, token_plan(): jnp.einsum('lmd,lmf->ldf', scaled_rows, saved_rows, preferred_element_typ...  3.38 us
    all_to_all x1, waiting for transfers between devices, token_plan(): from_all = lax.all_to_all(to_all, ('grp', 'ep'), 0, 0, tiled=True)  2.55 us
    convert_element_type x1, other arithmetic, token_plan(): piece = total.astype(jnp.bfloat16) if left > 1 else total  1.24 us
  transfers between devices with their start and end apart: 10, of which 4 were waited for; matrix products, arithmetic and copies ran while one was open for 15% of the time, Pallas kernels for 0%

profile of v1, /device:TPU:0, one launch (start us, length us, event | category | flops | bytes accessed | tf_op | source)
XLA Modules:
  0.0 50.2 jit_solution(12770678469617340093)
XLA Ops:
  0.6 0.0 copy-start
  0.6 0.7 %fusion.4 = pred[16,32]{1,0:T(8,128)(4,1)S(1)} fusion(s32[8,32]{1,0:T(8,128)} %bitcast.60), kind=kLoop, calls=%fused_computation.26 | loop fusion | flops 7680 | bytes 1536 | tf_op jit(solution)/shard_map/reduce_or | solution.py:110
  1.4 0.8 %broadcast_select_fusion = (f32[16,32]{1,0:T(8,128)S(1)}, f32[32]{0:T(128)S(1)}, bf16[16,32]{1,0:T(8,128)(2,1)S(1)}) fusion(pred[16,32]{1,0:T(8,128)(4,1)S(1)} %fusion.4, f32[32,16]{0,1:T(8,128)} %param.8), kind=kOutput, calls=%fused_computation.56 | convolution fusion | flops 37344 | bytes 5760 | tf_op jit(solution)/shard_map/dot_general | solution.py:116
  2.2 0.1 copy.36
  2.3 0.7 %divide_convert_fusion = bf16[32,16]{0,1:T(8,128)(2,1)S(1)} fusion(pred[16,32]{1,0:T(8,128)(4,1)S(1)} %fusion.4, f32[32]{0:T(128)S(1)} %get-tuple-element.4, f32[32,16]{0,1:T(8,128)} %param.8), kind=kLoop, calls=%fused_computation.48 | loop fusion | flops 3584 | bytes 3712 | tf_op jit(solution)/shard_map/convert_element_type | solution.py:125
  3.0 0.1 copy.35
  3.1 0.9 %concatenate.13 = bf16[32,1152]{1,0:T(8,128)(2,1)S(1)} concatenate(bf16[32,1024]{1,0:T(8,128)(2,1)} %param.6, bf16[32,16]{1,0:T(8,128)(2,1)S(1)} %copy.35, bf16[32,16]{1,0:T(8,128)(2,1)S(1)} %copy.36, bf16[32,96]{1,0:T(8,128)(2,1)S(1)} %broadcast_in_dim.62), dimensions={1} | concatenate | bytes 147456 | tf_op jit(solution)/shard_map/concatenate | solution.py:122
  4.0 5.1 %collective-permute-start.5 = (bf16[32,1152]{1,0:T(8,128)(2,1)S(1)}, bf16[32,1152]{1,0:T(8,128)(2,1)S(1)}, u32[]{:S(2)}, u32[]{:S(2)}) collective-permute-start(bf16[32,1152]{1,0:T(8,128)(2,1)S(1)} %concatenate.13), channel_id=1, source_target_pairs={{0,24},{4,28},{8,16},{12,20},{16,8},{20,12},{24,0},{28,4},{1,25},{... | collective-permute-start | bytes 221192 | tf_op jit(solution)/shard_map/ppermute | solution.py:84
  9.2 0.0 collective-permute-start.3
  9.2 0.6 %collective-permute-start.1 = (bf16[32,1152]{1,0:T(8,128)(2,1)S(1)}, bf16[32,1152]{1,0:T(8,128)(2,1)S(1)}, u32[]{:S(2)}, u32[]{:S(2)}) collective-permute-start(bf16[32,1152]{1,0:T(8,128)(2,1)S(1)} %concatenate.13), channel_id=1, source_target_pairs={{0,8},{4,12},{8,0},{12,4},{16,24},{20,28},{24,16},{28,20},{1,9},{5... | collective-permute-start | bytes 221192 | tf_op jit(solution)/shard_map/ppermute | solution.py:84
  9.8 1.6 %collective-permute-start = (bf16[32,1152]{1,0:T(8,128)(2,1)S(1)}, bf16[32,1152]{1,0:T(8,128)(2,1)S(1)}, u32[]{:S(2)}, u32[]{:S(2)}) collective-permute-start(bf16[32,1152]{1,0:T(8,128)(2,1)S(1)} %concatenate.13), channel_id=1, source_target_pairs={{0,4},{4,0},{8,12},{12,8},{16,20},{20,16},{24,28},{28,24},{1,5},{5... | collective-permute-start | bytes 221192 | tf_op jit(solution)/shard_map/ppermute | solution.py:84
  11.5 0.1 constant_dynamic-update-slice_fusion.7
  11.5 0.8 %constant_dynamic-update-slice_fusion.8 = bf16[256,1024]{1,0:T(8,128)(2,1)S(1)} fusion(bf16[32,1024]{1,0:T(8,128)(2,1)} %param.6), kind=kLoop, calls=%fused_computation.35 | loop fusion | bytes 131072
  12.4 0.0 collective-permute-done.5
  12.4 1.3 %collective-permute-start.6 = (bf16[32,1152]{1,0:T(8,128)(2,1)S(1)}, bf16[32,1152]{1,0:T(8,128)(2,1)S(1)}, u32[]{:S(2)}, u32[]{:S(2)}) collective-permute-start(bf16[32,1152]{1,0:T(8,128)(2,1)S(1)} %collective-permute-done.5), channel_id=1, source_target_pairs={{0,4},{4,0},{8,12},{12,8},{16,20},{20,16},{24,28},{28,24},{1,5},{5... | collective-permute-start | bytes 221192 | tf_op jit(solution)/shard_map/ppermute | solution.py:84
  13.7 1.7 %collective-permute-done.3 = bf16[32,1152]{1,0:T(8,128)(2,1)S(1)} collective-permute-done((bf16[32,1152]{1,0:T(8,128)(2,1)S(1)}, bf16[32,1152]{1,0:T(8,128)(2,1)S(1)}, u32[]{:S(2)}, u32[]{:S(2)}) %collective-permute-start.3) | collective-permute-done | bytes 73760 | tf_op jit(solution)/shard_map/ppermute | solution.py:84
  15.4 1.5 %collective-permute-start.4 = (bf16[32,1152]{1,0:T(8,128)(2,1)S(1)}, bf16[32,1152]{1,0:T(8,128)(2,1)S(1)}, u32[]{:S(2)}, u32[]{:S(2)}) collective-permute-start(bf16[32,1152]{1,0:T(8,128)(2,1)S(1)} %collective-permute-done.3), channel_id=1, source_target_pairs={{0,4},{4,0},{8,12},{12,8},{16,20},{20,16},{24,28},{28,24},{1,5},{5... | collective-permute-start | bytes 221192 | tf_op jit(solution)/shard_map/ppermute | solution.py:84
  16.9 0.0 collective-permute-done.1
  16.9 0.5 %collective-permute-start.2 = (bf16[32,1152]{1,0:T(8,128)(2,1)S(1)}, bf16[32,1152]{1,0:T(8,128)(2,1)S(1)}, u32[]{:S(2)}, u32[]{:S(2)}) collective-permute-start(bf16[32,1152]{1,0:T(8,128)(2,1)S(1)} %collective-permute-done.1), channel_id=1, source_target_pairs={{0,4},{4,0},{8,12},{12,8},{16,20},{20,16},{24,28},{28,24},{1,5},{5... | collective-permute-start | bytes 221192 | tf_op jit(solution)/shard_map/ppermute | solution.py:84
  17.4 0.0 collective-permute-done
  17.5 3.8 %collective-permute-done.2 = bf16[32,1152]{1,0:T(8,128)(2,1)S(1)} collective-permute-done((bf16[32,1152]{1,0:T(8,128)(2,1)S(1)}, bf16[32,1152]{1,0:T(8,128)(2,1)S(1)}, u32[]{:S(2)}, u32[]{:S(2)}) %collective-permute-start.2) | collective-permute-done | bytes 73760 | tf_op jit(solution)/shard_map/ppermute | solution.py:84
  21.3 0.0 collective-permute-done.4
  21.3 0.0 collective-permute-done.6
  21.3 0.1 select_bitcast_fusion
  21.4 0.1 copy.39
  21.5 0.1 convert_bitcast_fusion
  21.6 0.1 copy.40
  21.7 0.2 select_reduce_fusion
  21.9 0.4 convolution_convert_fusion.2
  22.4 0.0 copy-start.1
  22.4 3.5 %convolution_convert_fusion.1 = bf16[2,256,1024]{2,1,0:T(8,128)(2,1)S(1)} fusion(bf16[2,256,1024]{2,1,0:T(8,128)(2,1)S(1)} %convolution_convert_fusion.2, bf16[2,1024,1024]{2,1,0:T(8,128)(2,1)} %param.10), kind=kOutput, calls=%fused_computation.3 | convolution fusion | flops 1074266112 | bytes 6291456 | tf_op jit(solution)/shard_map/lmd,ldf->lmf/dot_general | solution.py:148
  25.9 0.0 copy-done.1
  25.9 0.3 multiply_reduce_fusion
  26.3 0.1 reshape.74
  26.4 0.7 %all_to_all.6 = f32[32,1,64]{2,1,0:T(1,128)} reshape(f32[8,4,2,32]{3,2,1,0:T(2,128)S(1)} %broadcast_in_dim.65) | data formatting | bytes 16384 | tf_op jit(solution)/shard_map/all_to_all | solution.py:159
  27.1 4.3 %all-to-all-start = ((f32[32,1,64]{2,1,0:T(1,128)}), f32[32,1,64]{2,1,0:T(1,128)S(1)}, u32[]{:S(2)}, u32[]{:S(2)}) async-start(f32[32,1,64]{2,1,0:T(1,128)} %all_to_all.6), calls=%async_computation | async-start | bytes 32768 | tf_op jit(solution)/shard_map/all_to_all | solution.py:159
  31.4 0.8 %dynamic-slice_bitcast_fusion = bf16[2,128,1024]{2,1,0:T(8,128)(2,1)} fusion(bf16[2,2,128,1024]{3,2,1,0:T(8,128)(2,1)S(1)} %bitcast.53, s32[]{:T(128)S(6)} %select_n.91), kind=kLoop, calls=%fused_computation.11 | loop fusion | bytes 1048580 | tf_op jit(solution)/shard_map/jit(dynamic_index_in_dim)/squeeze | solution.py:176
  32.2 0.0 copy-start.2
  32.2 0.3 collective-permute-start.7
  32.5 3.4 %convolution_convert_fusion = bf16[2,1024,1024]{2,1,0:T(8,128)(2,1)} fusion(bf16[2,256,1024]{2,1,0:T(8,128)(2,1)S(1)} %bitcast.56, bf16[2,256,1024]{2,1,0:T(8,128)(2,1)S(1)} %convolution_convert_fusion.2, f32[2,256]{1,0:T(2,128)S(1)} %select_reduce_fusion), kind=kOutput, calls=%fused_computation | convolution fusion | flops 1077411840 | bytes 6293504 | tf_op jit(solution)/shard_map/lmd,lmf->ldf/dot_general | solution.py:162
  35.8 0.1 dynamic_slice.21
  35.9 2.6 %all-to-all-done = f32[32,1,64]{2,1,0:T(1,128)S(1)} async-done(((f32[32,1,64]{2,1,0:T(1,128)}), f32[32,1,64]{2,1,0:T(1,128)S(1)}, u32[]{:S(2)}, u32[]{:S(2)}) %all-to-all-start) | async-done | bytes 8224 | tf_op jit(solution)/shard_map/all_to_all | solution.py:159
  38.5 0.5 %broadcast.99 = f32[]{:T(128)} broadcast(f32[]{:T(128)} %constant.182), dimensions={} | broadcast | bytes 8 | tf_op jit(solution)/shard_map/all_to_all | solution.py:159
  39.0 0.7 %reduce.3 = f32[32,64]{1,0:T(8,128)S(1)} reduce(f32[32,1,64]{2,1,0:T(1,128)S(1)} %all-to-all-done, f32[]{:T(128)} %broadcast.99), dimensions={1}, to_apply=%all_to_all.7.reduce_sub_computation.3 | reduce | bytes 16388 | tf_op jit(solution)/shard_map/all_to_all | solution.py:159
  39.7 0.1 reshape.75
  39.8 0.1 select_reduce_fusion.1
  39.9 0.0 copy-done.2
  40.0 0.0 collective-permute-done.7
  40.0 1.2 %fusion = bf16[2,128,1024]{2,1,0:T(8,128)(2,1)S(1)} fusion(bf16[2,128,1024]{2,1,0:T(8,128)(2,1)} %collective-permute-done.7, bf16[2,2,128,1024]{3,2,1,0:T(8,128)(2,1)S(1)} %bitcast.54, s32[]{:T(128)S(6)} %select_n.90), kind=kLoop, calls=%fused_computation.7 | loop fusion | flops 1048576 | bytes 1572868 | tf_op jit(solution)/shard_map/convert_element_type | solution.py:179
  41.3 0.6 %collective-permute-start.8 = (bf16[1,128,1024]{2,1,0:T(8,128)(2,1)S(1)}, bf16[1,128,1024]{2,1,0:T(8,128)(2,1)S(1)}, u32[]{:S(2)}, u32[]{:S(2)}) collective-permute-start(bf16[1,128,1024]{2,1,0:T(8,128)(2,1)S(1)} %constant_dynamic-slice_fusion), channel_id=1, source_target_pairs={{0,2},{1,3},{2,0},{3,1},{4,6},{5,7},{6,4},{7,5},{8,10},{9,11},{10,... | collective-permute-start | bytes 786440 | tf_op jit(solution)/shard_map/ppermute | solution.py:177
  41.9 0.0 copy-done
  41.9 0.8 %convolution_convert_fusion.3 = bf16[32,1024]{1,0:T(8,128)(2,1)} fusion(bf16[16,1024]{1,0:T(8,128)(2,1)S(1)} %copy-done, pred[16,32]{1,0:T(8,128)(4,1)S(1)} %fusion.4, f32[16,32]{1,0:T(8,128)S(1)} %select_reduce_fusion.1, f32[32]{0:T(128)S(1)} %broadcast_multiply_fusion, f32[32]{0:T(128)S(1)} %get-tuple-element.4, f32[32,16]{0,1:T(8,128)S(1)} %copy-done.2), kind=kOutput, calls=%fused_computation.5 | convolution fusion | flops 1087488 | bytes 103168 | tf_op jit(solution)/shard_map/dot_general | solution.py:194
  42.7 6.7 %collective-permute-done.8 = bf16[1,128,1024]{2,1,0:T(8,128)(2,1)S(1)} collective-permute-done((bf16[1,128,1024]{2,1,0:T(8,128)(2,1)S(1)}, bf16[1,128,1024]{2,1,0:T(8,128)(2,1)S(1)}, u32[]{:S(2)}, u32[]{:S(2)}) %collective-permute-start.8) | collective-permute-done | bytes 262176 | tf_op jit(solution)/shard_map/ppermute | solution.py:177
  49.4 0.8 %multiply_convert_fusion.2 = bf16[1,128,1024]{2,1,0:T(8,128)(2,1)} fusion(bf16[1,128,1024]{2,1,0:T(8,128)(2,1)S(1)} %collective-permute-done.8, bf16[2,128,1024]{2,1,0:T(8,128)(2,1)S(1)} %fusion, s32[]{:T(128)S(6)} %select_n.94, f32[128]{0:T(128)S(1)} %dynamic_slice.21), kind=kLoop, calls=%fused_computation.10 | loop fusion | flops 655360 | bytes 786948 | tf_op jit(solution)/shard_map/convert_element_type | solution.py:185
  (25 shorter events, 0.2 us)
Async XLA Ops:
  0.6 41.3 %copy-start = (bf16[16,1024]{1,0:T(8,128)(2,1)S(1)}, bf16[16,1024]{1,0:T(8,128)(2,1)}, u32[]{:S(2)}) copy-start(bf16[16,1024]{1,0:T(8,128)(2,1)} %param.9) | copy-start | bytes 98308
  4.0 8.4 %collective-permute-start.5 = (bf16[32,1152]{1,0:T(8,128)(2,1)S(1)}, bf16[32,1152]{1,0:T(8,128)(2,1)S(1)}, u32[]{:S(2)}, u32[]{:S(2)}) collective-permute-start(bf16[32,1152]{1,0:T(8,128)(2,1)S(1)} %concatenate.13), channel_id=1, source_target_pairs={{0,24},{4,28},{8,16},{12,20},{16,8},{20,12},{24,0},{28,4},{1,25},{... | collective-permute-start | bytes 221192 | tf_op jit(solution)/shard_map/ppermute | solution.py:84
  9.2 6.2 %collective-permute-start.3 = (bf16[32,1152]{1,0:T(8,128)(2,1)S(1)}, bf16[32,1152]{1,0:T(8,128)(2,1)S(1)}, u32[]{:S(2)}, u32[]{:S(2)}) collective-permute-start(bf16[32,1152]{1,0:T(8,128)(2,1)S(1)} %concatenate.13), channel_id=1, source_target_pairs={{0,16},{4,20},{8,24},{12,28},{16,0},{20,4},{24,8},{28,12},{1,17},{... | collective-permute-start | bytes 221192 | tf_op jit(solution)/shard_map/ppermute | solution.py:84
  9.2 7.7 %collective-permute-start.1 = (bf16[32,1152]{1,0:T(8,128)(2,1)S(1)}, bf16[32,1152]{1,0:T(8,128)(2,1)S(1)}, u32[]{:S(2)}, u32[]{:S(2)}) collective-permute-start(bf16[32,1152]{1,0:T(8,128)(2,1)S(1)} %concatenate.13), channel_id=1, source_target_pairs={{0,8},{4,12},{8,0},{12,4},{16,24},{20,28},{24,16},{28,20},{1,9},{5... | collective-permute-start | bytes 221192 | tf_op jit(solution)/shard_map/ppermute | solution.py:84
  9.8 7.6 %collective-permute-start = (bf16[32,1152]{1,0:T(8,128)(2,1)S(1)}, bf16[32,1152]{1,0:T(8,128)(2,1)S(1)}, u32[]{:S(2)}, u32[]{:S(2)}) collective-permute-start(bf16[32,1152]{1,0:T(8,128)(2,1)S(1)} %concatenate.13), channel_id=1, source_target_pairs={{0,4},{4,0},{8,12},{12,8},{16,20},{20,16},{24,28},{28,24},{1,5},{5... | collective-permute-start | bytes 221192 | tf_op jit(solution)/shard_map/ppermute | solution.py:84
  12.4 8.9 %collective-permute-start.6 = (bf16[32,1152]{1,0:T(8,128)(2,1)S(1)}, bf16[32,1152]{1,0:T(8,128)(2,1)S(1)}, u32[]{:S(2)}, u32[]{:S(2)}) collective-permute-start(bf16[32,1152]{1,0:T(8,128)(2,1)S(1)} %collective-permute-done.5), channel_id=1, source_target_pairs={{0,4},{4,0},{8,12},{12,8},{16,20},{20,16},{24,28},{28,24},{1,5},{5... | collective-permute-start | bytes 221192 | tf_op jit(solution)/shard_map/ppermute | solution.py:84
  15.4 5.9 %collective-permute-start.4 = (bf16[32,1152]{1,0:T(8,128)(2,1)S(1)}, bf16[32,1152]{1,0:T(8,128)(2,1)S(1)}, u32[]{:S(2)}, u32[]{:S(2)}) collective-permute-start(bf16[32,1152]{1,0:T(8,128)(2,1)S(1)} %collective-permute-done.3), channel_id=1, source_target_pairs={{0,4},{4,0},{8,12},{12,8},{16,20},{20,16},{24,28},{28,24},{1,5},{5... | collective-permute-start | bytes 221192 | tf_op jit(solution)/shard_map/ppermute | solution.py:84
  16.9 4.4 %collective-permute-start.2 = (bf16[32,1152]{1,0:T(8,128)(2,1)S(1)}, bf16[32,1152]{1,0:T(8,128)(2,1)S(1)}, u32[]{:S(2)}, u32[]{:S(2)}) collective-permute-start(bf16[32,1152]{1,0:T(8,128)(2,1)S(1)} %collective-permute-done.1), channel_id=1, source_target_pairs={{0,4},{4,0},{8,12},{12,8},{16,20},{20,16},{24,28},{28,24},{1,5},{5... | collective-permute-start | bytes 221192 | tf_op jit(solution)/shard_map/ppermute | solution.py:84
  22.4 3.5 %copy-start.1 = (bf16[1,512,1024]{2,1,0:T(8,128)(2,1)S(1)}, bf16[1,512,1024]{2,1,0:T(8,128)(2,1)}, u32[]{:S(2)}) copy-start(bf16[1,512,1024]{2,1,0:T(8,128)(2,1)} %param.11) | copy-start | bytes 3145732
  27.1 11.4 %all-to-all-start = ((f32[32,1,64]{2,1,0:T(1,128)}), f32[32,1,64]{2,1,0:T(1,128)S(1)}, u32[]{:S(2)}, u32[]{:S(2)}) async-start(f32[32,1,64]{2,1,0:T(1,128)} %all_to_all.6), calls=%async_computation | async-start | bytes 32768 | tf_op jit(solution)/shard_map/all_to_all | solution.py:159
  32.2 7.8 %copy-start.2 = (f32[32,16]{0,1:T(8,128)S(1)}, f32[32,16]{0,1:T(8,128)}, u32[]{:S(2)}) copy-start(f32[32,16]{0,1:T(8,128)} %param.8) | copy-start | bytes 6148
  32.2 7.8 %collective-permute-start.7 = (bf16[2,128,1024]{2,1,0:T(8,128)(2,1)}, bf16[2,128,1024]{2,1,0:T(8,128)(2,1)}, u32[]{:S(2)}, u32[]{:S(2)}) collective-permute-start(bf16[2,128,1024]{2,1,0:T(8,128)(2,1)} %dynamic-slice_bitcast_fusion), channel_id=1, source_target_pairs={{0,1},{1,0},{2,3},{3,2},{4,5},{5,4},{6,7},{7,6},{8,9},{9,8},{10,11... | collective-permute-start | bytes 1572872 | tf_op jit(solution)/shard_map/ppermute | solution.py:177
  41.3 8.1 %collective-permute-start.8 = (bf16[1,128,1024]{2,1,0:T(8,128)(2,1)S(1)}, bf16[1,128,1024]{2,1,0:T(8,128)(2,1)S(1)}, u32[]{:S(2)}, u32[]{:S(2)}) collective-permute-start(bf16[1,128,1024]{2,1,0:T(8,128)(2,1)S(1)} %constant_dynamic-slice_fusion), channel_id=1, source_target_pairs={{0,2},{1,3},{2,0},{3,1},{4,6},{5,7},{6,4},{7,5},{8,10},{9,11},{10,... | collective-permute-start | bytes 786440 | tf_op jit(solution)/shard_map/ppermute | solution.py:177

commit v2 on v0

--- a/solution.py
+++ b/solution.py
@@ -1,12 +1,18 @@
+import functools
+
 import jax
 import jax.numpy as jnp
 from jax import lax
+from jax.experimental import pallas as pl
+from jax.experimental.pallas import tpu as pltpu
 from jax.sharding import PartitionSpec as P
 
+
 route_scale = 2.5
-
-
-def body(out_grad, expert_ids, router_logits, router_weight, expert_weight, hidden_saved):
+LANES = 128
+
+
+def slot_plan(out_grad, expert_ids, router_logits, router_weight, expert_weight, hidden_saved):
     group_rows, features = out_grad.shape
     top_count = expert_ids.shape[1]
     experts = router_logits.shape[1]
@@ -37,22 +43,10 @@
     send_prob = jnp.sum(
         jnp.where(slot_match, route_probs.reshape(1, pair_count), 0.0), axis=1
     ).astype(jnp.bfloat16)
-    got_rows, got_prob = (
-        lax.all_to_all(
-            send_rows.reshape(local_experts, group_count, capacity, features),
-            "grp",
-            split_axis=1,
-            concat_axis=1,
-            tiled=True,
-        ),
-        lax.all_to_all(
-            send_prob.reshape(local_experts, group_count, capacity),
-            "grp",
-            split_axis=1,
-            concat_axis=1,
-            tiled=True,
-        ),
-    )
+    swap = dict(split_axis=1, concat_axis=1, tiled=True)
+    shape = (local_experts, group_count, capacity)
+    got_rows = lax.all_to_all(send_rows.reshape(shape + (features,)), "grp", **swap)
+    got_prob = lax.all_to_all(send_prob.reshape(shape), "grp", **swap)
     slot_grads = got_rows.reshape(local_experts, expert_span, features)
     prob_rows = got_prob.reshape(local_experts, expert_span).astype(jnp.float32)
     saved_rows = hidden_saved.reshape(local_experts, expert_span, hidden_width)
@@ -69,13 +63,7 @@
     ).reshape(slot_count, hidden_width)
     rounded_term = lax.optimization_barrier(partial_term.astype(jnp.bfloat16)).astype(jnp.float32)
     partial_score = jnp.sum(flat_saved.astype(jnp.float32) * rounded_term, axis=1)
-    moved_scores = lax.all_to_all(
-        partial_score.reshape(local_experts, group_count, capacity),
-        "grp",
-        split_axis=1,
-        concat_axis=1,
-        tiled=True,
-    )
+    moved_scores = lax.all_to_all(partial_score.reshape(shape), "grp", **swap)
     returned = lax.psum(moved_scores, "ep")
     summed = lax.psum_scatter(
         partial_term.astype(jnp.bfloat16), "ep", scatter_dimension=0, tiled=True
@@ -96,6 +84,371 @@
     return (weight_grad, hidden_grad, input_grad)
 
 
+def exchange(x, distance):
+    count = lax.axis_size("grp")
+    return lax.ppermute(x, "grp", [(i, i ^ distance) for i in range(count)])
+
+
+def gather_blocks(x):
+    count = lax.axis_size("grp")
+    blocks = {0: x}
+    far = sorted(range(2, count, 2), key=lambda d: (d != count // 2, -d))
+    for distance in far:
+        blocks[distance] = exchange(x, distance)
+    for distance in [0] + far:
+        blocks[distance ^ 1] = exchange(blocks[distance], 1)
+    return [blocks[d] for d in range(count)]
+
+
+def iota(shape, dim):
+    return lax.broadcasted_iota(jnp.int32, shape, dim)
+
+
+def contract_rows(a, b):
+    return lax.dot_general(a, b, (((0,), (0,)), ((), ())), preferred_element_type=jnp.float32)
+
+
+def pack_kernel(local, ids_hbm, logits_hbm, rows_hbm, packed_ref, meta_ref, ids_ref, logits_ref, sems):
+    top_count, tokens = ids_ref.shape
+    groups = logits_ref.shape[0] // local
+    features = rows_hbm.shape[1]
+    copies = [
+        pltpu.make_async_copy(ids_hbm, ids_ref, sems.at[0]),
+        pltpu.make_async_copy(logits_hbm, logits_ref, sems.at[1]),
+        pltpu.make_async_copy(rows_hbm, packed_ref.at[:, pl.ds(0, features)], sems.at[2]),
+    ]
+    for c in copies:
+        c.start()
+    copies[0].wait()
+    copies[1].wait()
+    ids = ids_ref[...]
+    upto = (iota((tokens, tokens), 0) <= iota((tokens, tokens), 1)).astype(jnp.bfloat16)
+    sig, chosen, ranks = [], [], []
+    for l in range(local):
+        expert = iota((groups, tokens), 0) * local + l
+        hit = jnp.zeros((groups, tokens), jnp.float32)
+        for i in range(top_count):
+            hit = hit + (ids[i : i + 1, :] == expert).astype(jnp.float32)
+        value = jax.nn.sigmoid(logits_ref[pl.ds(l, groups, stride=local), :])
+        sig.append(value)
+        chosen.append(hit * value)
+        count = jnp.dot(hit.astype(jnp.bfloat16), upto, preferred_element_type=jnp.float32)
+        ranks.append(hit * count)
+    total = sum(jnp.sum(c, axis=0, keepdims=True) for c in chosen)
+    probs = [route_scale * c / total for c in chosen]
+    stack = jnp.concatenate(probs + ranks, axis=0).astype(jnp.bfloat16)
+    lanes = packed_ref.shape[1] - features
+    spread = (iota((stack.shape[0], lanes), 0) == iota((stack.shape[0], lanes), 1)).astype(
+        jnp.bfloat16
+    )
+    packed_ref[:, features:] = contract_rows(stack, spread).astype(jnp.bfloat16)
+    for l in range(local):
+        for k, value in enumerate((sig[l], probs[l], ranks[l])):
+            meta_ref[l, k] = jnp.zeros(meta_ref.shape[2:], jnp.float32)
+            meta_ref[l, k, :, :tokens] = value
+    copies[2].wait()
+
+
+def load_kernel(parts, cue_ref, w_ref, h_ref, r_ref, w_out, h_out, r_out, sems):
+    rows = w_ref.shape[1] // parts
+    copies = [
+        pltpu.make_async_copy(
+            w_ref.at[l, pl.ds(i * rows, rows)],
+            w_out.at[l, pl.ds(i * rows, rows)],
+            sems.at[l * parts + i],
+        )
+        for l in range(w_ref.shape[0])
+        for i in range(parts)
+    ]
+    base = w_ref.shape[0] * parts
+    copies.append(pltpu.make_async_copy(h_ref, h_out, sems.at[base]))
+    copies.append(pltpu.make_async_copy(r_ref, r_out, sems.at[base + 1]))
+    for c in copies:
+        c.start()
+    for c in copies:
+        c.wait()
+
+
+def partial_kernel(local, groups, capacity, *refs):
+    blocks = refs[:groups]
+    w_ref, h_ref, keep_ref, send_ref, score_ref = refs[groups:]
+    features, width = w_ref.shape[1], w_ref.shape[2]
+    span = groups * capacity
+    tokens = groups * blocks[0].shape[0]
+    cols = 256 if width % 256 == 0 else LANES
+    own, half = lax.axis_index("grp"), lax.rem(lax.axis_index("ep"), 2)
+    rows = jnp.concatenate([b[:, :features] for b in blocks], axis=0)
+    aux = jnp.concatenate([b[:, features:] for b in blocks], axis=0).astype(jnp.float32)
+    aux = aux.T
+    source = (iota((1, tokens), 1) // blocks[0].shape[0]) ^ own
+    slot = iota((span, tokens), 0) + half * (span // 2)
+    slot = jnp.where(slot >= span, slot - span, slot)
+    part_row, part_lane = iota((span, LANES), 0), iota((span, LANES), 1)
+    near = pl.ds(pl.multiple_of(half * (span // 2), span // 2), span // 2)
+    away = pl.ds(pl.multiple_of((1 - half) * (span // 2), span // 2), span // 2)
+    sent = jnp.zeros((groups, LANES), jnp.float32)
+    for l in range(local):
+        lane = l * groups + own
+        prob = jnp.sum(jnp.where(iota(aux.shape, 0) == lane, aux, 0.0), axis=0, keepdims=True)
+        rank = jnp.sum(
+            jnp.where(iota(aux.shape, 0) == local * groups + lane, aux, 0.0),
+            axis=0,
+            keepdims=True,
+        ).astype(jnp.int32)
+        place = jnp.where(rank > 0, source * capacity + rank - 1, -1)
+        pick = slot == place
+        scale = jnp.sum(jnp.where(pick, prob, 0.0), axis=1, keepdims=True)
+        grads = jnp.dot(
+            pick.astype(jnp.float32).astype(jnp.bfloat16), rows, preferred_element_type=jnp.float32
+        ).astype(jnp.bfloat16)
+        score = jnp.zeros((span, LANES), jnp.float32)
+        for n in range(width // cols):
+            part = pl.ds(n * cols, cols)
+            term = jnp.dot(grads, w_ref[l, :, part], preferred_element_type=jnp.float32)
+            saved = jnp.concatenate([h_ref[l, near, part], h_ref[l, away, part]], axis=0)
+            product = term * saved.astype(jnp.float32)
+            for k in range(cols // LANES):
+                score = score + product[:, k * LANES : (k + 1) * LANES]
+            out = (term * scale).astype(jnp.bfloat16)
+            keep_ref[l, :, part] = out[: span // 2]
+            send_ref[l, :, part] = out[span // 2 :]
+        score = jnp.sum(score, axis=1, keepdims=True)
+        spread = jnp.where(lax.rem(part_row, capacity) + l * capacity == part_lane, score, 0.0)
+        sent = sent + jnp.sum(spread.reshape(groups, capacity, LANES), axis=1)
+    turned = jnp.concatenate([sent[groups // 2 :], sent[: groups // 2]], axis=0)
+    sent = jnp.where(half == 0, sent, turned)
+    score_ref[...] = jnp.broadcast_to(sent[:, None, :], score_ref.shape)
+
+
+def weight_kernel(local, groups, capacity, parts, *refs):
+    blocks = refs[:groups]
+    h_ref, out_hbm, turned_buf, scaled_buf, out_buf, sems = refs[groups:]
+    features = turned_buf.shape[0]
+    tile = features // parts
+    block_rows = blocks[0].shape[0]
+    span = groups * capacity
+    tokens = groups * block_rows
+    own = lax.axis_index("grp")
+    rows = jnp.concatenate([b[:, :features] for b in blocks], axis=0)
+    turned_buf[...] = rows.T
+    aux = jnp.concatenate([b[:, features:] for b in blocks], axis=0).astype(jnp.float32)
+    at = iota(aux.shape, 1)
+    source = (iota((tokens, 1), 0) // block_rows) ^ own
+    copies = []
+    for l in range(local):
+        lane = l * groups + own
+        prob = jnp.sum(jnp.where(at == lane, aux, 0.0), axis=1, keepdims=True)
+        rank = jnp.sum(jnp.where(at == local * groups + lane, aux, 0.0), axis=1, keepdims=True)
+        place = jnp.where(rank > 0, source * capacity + rank.astype(jnp.int32) - 1, -1)
+        pick = jnp.where(place == iota((tokens, span), 1), prob, 0.0).astype(jnp.bfloat16)
+        scaled_buf[...] = jnp.dot(
+            turned_buf[...], pick, preferred_element_type=jnp.float32
+        ).astype(jnp.bfloat16)
+        for d in range(parts):
+            part = pl.ds(d * tile, tile)
+            out_buf[l, part] = jnp.dot(
+                scaled_buf[part], h_ref[l], preferred_element_type=jnp.float32
+            ).astype(jnp.bfloat16)
+            copy = pltpu.make_async_copy(
+                out_buf.at[l, part], out_hbm.at[l, part], sems.at[l * parts + d]
+            )
+            copy.start()
+            copies.append(copy)
+    for copy in copies:
+        copy.wait()
+
+
+def pair_kernel(mine_ref, got_ref, keep_ref, send_ref):
+    bit = lax.axis_index("ep") // 2
+    keep_ref[...] = mine_ref[bit].astype(jnp.float32) + got_ref[bit].astype(jnp.float32)
+    send_ref[...] = (
+        mine_ref[1 - bit].astype(jnp.float32) + got_ref[1 - bit].astype(jnp.float32)
+    ).astype(jnp.bfloat16)
+
+
+def router_kernel(local, capacity, score_ref, meta_ref, w_ref, out_ref):
+    groups, tokens = meta_ref.shape[2], out_ref.shape[0]
+    found = jnp.sum(score_ref[...], axis=1)
+    scores = []
+    for l in range(local):
+        rank = meta_ref[l, 2].astype(jnp.int32)
+        at = jnp.maximum(rank + (l * capacity - 1), 0)
+        value = jnp.take_along_axis(found, at, axis=1, mode="promise_in_bounds")
+        scores.append(jnp.where(rank > 0, value, 0.0))
+    mean = sum(
+        jnp.sum(meta_ref[l, 1] * scores[l], axis=0, keepdims=True) for l in range(local)
+    ) * (1.0 / route_scale)
+    grads = jnp.concatenate(
+        [
+            meta_ref[l, 1] * (1.0 - meta_ref[l, 0]) * (scores[l] - mean)
+            for l in range(local)
+        ],
+        axis=0,
+    ).astype(jnp.bfloat16)
+    count = local * groups
+    row = iota((count, count), 0)
+    expert = lax.rem(row, groups) * local + row // groups
+    order = (expert == iota((count, count), 1)).astype(jnp.bfloat16)
+    turned = contract_rows(grads, order)[:tokens].astype(jnp.bfloat16)
+    out_ref[...] = jnp.dot(turned, w_ref[...], preferred_element_type=jnp.float32).astype(
+        jnp.bfloat16
+    )
+
+
+def cost(flops, nbytes):
+    return pl.CostEstimate(flops=flops, bytes_accessed=nbytes, transcendentals=0)
+
+
+def struct(shape, dtype):
+    return jax.ShapeDtypeStruct(shape, dtype)
+
+
+def held(x):
+    return pltpu.with_memory_space_constraint(x, pltpu.VMEM)
+
+
+def away_from_vmem(x):
+    return pltpu.with_memory_space_constraint(x, pltpu.HBM)
+
+
+def kept(shape, dtype):
+    return pltpu.VMEM(shape, dtype)
+
+
+def token_plan(out_grad, expert_ids, router_logits, router_weight, expert_weight, hidden_saved):
+    group_rows, features = out_grad.shape
+    groups, ep_count = lax.axis_size("grp"), lax.axis_size("ep")
+    local, _, width = expert_weight.shape
+    slot_count = hidden_saved.shape[1]
+    capacity = slot_count // (local * groups)
+    span = groups * capacity
+    tokens = groups * group_rows
+    bf16, f32 = jnp.bfloat16, jnp.float32
+    vmem = pl.BlockSpec(memory_space=pltpu.VMEM)
+    hbm = pl.BlockSpec(memory_space=pltpu.HBM)
+
+    def limit(mib):
+        return pltpu.CompilerParams(vmem_limit_bytes=mib * 2**20)
+
+    packed, meta = pl.pallas_call(
+        functools.partial(pack_kernel, local),
+        out_shape=(
+            pltpu.VMEM((group_rows, features + LANES), bf16),
+            pltpu.VMEM((local, 3, groups, LANES), f32),
+        ),
+        in_specs=[hbm] * 3,
+        out_specs=(vmem, vmem),
+        scratch_shapes=[
+            pltpu.VMEM(expert_ids.shape[::-1], jnp.int32),
+            pltpu.VMEM(router_logits.shape[::-1], f32),
+            pltpu.SemaphoreType.DMA((3,)),
+        ],
+        compiler_params=limit(2),
+        name="pack",
+    )(away_from_vmem(expert_ids.T), away_from_vmem(router_logits.T), away_from_vmem(out_grad))
+    blocks = [held(b) for b in gather_blocks(packed)]
+
+    weights, saved, projection = pl.pallas_call(
+        functools.partial(load_kernel, 2),
+        out_shape=(
+            pltpu.VMEM(expert_weight.shape, bf16),
+            pltpu.VMEM((local, span, width), bf16),
+            pltpu.VMEM(router_weight.shape, bf16),
+        ),
+        in_specs=[vmem] + [hbm] * 3,
+        out_specs=(vmem, vmem, vmem),
+        scratch_shapes=[pltpu.SemaphoreType.DMA((2 * local + 2,))],
+        compiler_params=limit(2),
+        cost_estimate=cost(2**27, 8 * 2**20),
+        name="load",
+    )(
+        blocks[2],
+        away_from_vmem(expert_weight),
+        away_from_vmem(hidden_saved.reshape(local, span, width)),
+        away_from_vmem(router_weight),
+    )
+    weights, saved, projection = held(weights), held(saved), held(projection)
+
+    keep, send, score = pl.pallas_call(
+        functools.partial(partial_kernel, local, groups, capacity),
+        out_shape=(
+            pltpu.VMEM((local, span // 2, width), bf16),
+            pltpu.VMEM((local, span // 2, width), bf16),
+            pltpu.VMEM((groups, ep_count, LANES), f32),
+        ),
+        in_specs=[vmem] * (groups + 2),
+        out_specs=(vmem, vmem, vmem),
+        compiler_params=limit(8),
+        cost_estimate=cost(2 * slot_count * features * width, 8 * 2**20),
+        name="partial",
+    )(*blocks, weights, saved)
+
+    core_pairs = [(i, i ^ 1) for i in range(ep_count)]
+    chip_pairs = [(i, i ^ 2) for i in range(ep_count)]
+    got = lax.ppermute(send, "ep", core_pairs)
+    from_all = lax.all_to_all(
+        score.reshape(groups * ep_count, 1, LANES), ("grp", "ep"), 0, 0, tiled=True
+    )
+    mine, away = pl.pallas_call(
+        pair_kernel,
+        out_shape=(kept((span // 2, width), f32), kept((span // 2, width), bf16)),
+        in_specs=[vmem, vmem],
+        out_specs=(vmem, vmem),
+        compiler_params=limit(2),
+        name="pair",
+    )(held(keep), held(got))
+    last = lax.ppermute(away, "ep", chip_pairs)
+
+    parts = 4
+    weight_grad = pl.pallas_call(
+        functools.partial(weight_kernel, local, groups, capacity, parts),
+        out_shape=struct((local, features, width), bf16),
+        in_specs=[vmem] * (groups + 1),
+        out_specs=hbm,
+        scratch_shapes=[
+            pltpu.VMEM((features, tokens), bf16),
+            pltpu.VMEM((features, span), bf16),
+            pltpu.VMEM((local, features, width), bf16),
+            pltpu.SemaphoreType.DMA((local * parts,)),
+        ],
+        compiler_params=limit(12),
+        cost_estimate=cost(2 * slot_count * features * width, 6 * 2**20),
+        name="weight",
+    )(*blocks, saved)
+
+    hidden_grad = (mine + last.astype(f32)).astype(bf16)[None]
+
+    input_grad = pl.pallas_call(
+        functools.partial(router_kernel, local, capacity),
+        out_shape=struct((group_rows, features), bf16),
+        in_specs=[vmem] * 3,
+        out_specs=vmem,
+        compiler_params=limit(2),
+        name="router",
+    )(held(from_all.reshape(groups, ep_count, LANES)), held(meta), projection)
+    return (weight_grad, hidden_grad, input_grad)
+
+
+def body(out_grad, expert_ids, router_logits, router_weight, expert_weight, hidden_saved):
+    groups, ep_count = lax.axis_size("grp"), lax.axis_size("ep")
+    rows, experts = router_logits.shape
+    slots = hidden_saved.shape[1]
+    local = expert_weight.shape[0]
+    fits = (
+        rows * groups <= slots
+        and groups % 8 == 0
+        and groups & (groups - 1) == 0
+        and (local, ep_count) == (2, 4)
+        and rows % 16 == 0
+        and slots // groups <= LANES
+        and 2 * experts <= LANES
+    )
+    plan = token_plan if fits else slot_plan
+    return plan(
+        out_grad, expert_ids, router_logits, router_weight, expert_weight, hidden_saved
+    )
+
+
 def solution(mesh):
     in_specs = (
         P("grp", "ep"),

time: 90 us -> 37.3 us (0.41)
  waiting for transfers between devices: 37.3 us -> 9.48 us
  between operations: 14.2 us -> 0.69 us
  Pallas kernels: 0 us -> 9.97 us
  matrix products: 9.16 us -> 0 us
  blocking collectives: 5.63 us -> 0 us
  local copies, waits for them, and re-layouts: 4.43 us -> 0 us
  other arithmetic: 4.71 us -> 0.76 us
  starting transfers between devices: 14.2 us -> 16.2 us
    all_to_all x3 -> x1, waiting for transfers between devices: 37.3 us -> 4.26 us  [token_plan(): lax.all_to_all(score.reshape(groups * ep_count, 1, LANES), ('grp', 'ep'),...]
    ppermute x0 -> x9, starting transfers between devices: none -> 12.9 us  [the longest x7 11.3 us: exchange(): return lax.ppermute(x, 'grp', [(i, i ^ distance) for i in range(count)])]
    all_to_all x3 -> x1, starting transfers between devices: 14.2 us -> 3.3 us  [token_plan(): lax.all_to_all(score.reshape(groups * ep_count, 1, LANES), ('grp', 'ep'),...]
    pallas_call x0 -> x6, Pallas kernels: none -> 9.97 us  [the longest x1 2.83 us: token_plan(): pl.pallas_call(functools.partial(weight_kernel, local, groups, capacity,...]
    dot_general x4 -> x0, matrix products: 9.16 us -> none  [the longest x1 4.52 us: body(): jnp.einsum('lmd,ldf->lmf', slot_grads, expert_weight, preferred_element_t...]
    psum x1 -> x0, blocking collectives: 5.63 us -> none  [body(): returned = lax.psum(moved_scores, 'ep')]
    ppermute x0 -> x9, waiting for transfers between devices: none -> 5.22 us  [the longest x7 3.31 us: exchange(): return lax.ppermute(x, 'grp', [(i, i ^ distance) for i in range(count)])]
    reduce_sum x7 -> x0, other arithmetic: 2.23 us -> none  [the longest x1 1.57 us: body(): jnp.sum(flat_saved.astype(jnp.float32) * rounded_term, axis=1)]
  transfers between devices with their start and end apart: 4 -> 10, of which waited for: 3 -> 6; matrix products, arithmetic and copies ran while one was open for 9% -> 0% of each run, Pallas kernels for 0% -> 17%
where the time goes in v2:
time: 37.3 us; the launch traced here: 37.1 us
  starting transfers between devices  16.2 us (43%)
  Pallas kernels  9.97 us (27%)
  waiting for transfers between devices  9.48 us (25%)
  other arithmetic  0.76 us (2%)
  between operations  0.69 us (2%)
    ppermute x7, starting transfers between devices, exchange(): return lax.ppermute(x, 'grp', [(i, i ^ distance) for i in range(count)])  11.3 us
    all_to_all x1, waiting for transfers between devices, token_plan(): lax.all_to_all(score.reshape(groups * ep_count, 1, LANES), ('grp', 'ep'),...  4.26 us
    ppermute x7, waiting for transfers between devices, exchange(): return lax.ppermute(x, 'grp', [(i, i ^ distance) for i in range(count)])  3.31 us
    all_to_all x1, starting transfers between devices, token_plan(): lax.all_to_all(score.reshape(groups * ep_count, 1, LANES), ('grp', 'ep'),...  3.3 us
    pallas_call x1, Pallas kernels, token_plan(): pl.pallas_call(functools.partial(weight_kernel, local, groups, capacity,...  2.83 us
    pallas_call x1, Pallas kernels, token_plan(): pl.pallas_call(functools.partial(load_kernel, 2), out_shape=(pltpu.VMEM(e...  2.54 us
    pallas_call x1, Pallas kernels, token_plan(): pl.pallas_call(functools.partial(partial_kernel, local, groups, capacity)...  2.4 us
    ppermute x1, waiting for transfers between devices, token_plan(): got = lax.ppermute(send, 'ep', core_pairs)  1.91 us
  transfers between devices with their start and end apart: 10, of which 6 were waited for; matrix products, arithmetic and copies ran while one was open for 0% of the time, Pallas kernels for 17%

profile of v2, /device:TPU:0, one launch (start us, length us, event | category | flops | bytes accessed | tf_op | source)
XLA Modules:
  0.0 37.1 jit_solution(2784768773735491857)
XLA Ops:
  0.6 1.0 %pack.1 = (bf16[32,1152]{1,0:T(8,128)(2,1)S(1)}, f32[2,3,8,128]{3,2,1,0:T(8,128)S(1)}) custom-call(s32[8,32]{1,0:T(8,128)} %bitcast.12, f32[16,32]{1,0:T(8,128)} %bitcast.11, bf16[32,1024]{1,0:T(8,128)(2,1)} %rows_hbm.1), custom_call_target="tpu_custom_call" | custom-call | tf_op jit(solution)/shard_map/pack/pallas_call | solution.py:333
  1.7 5.1 %collective-permute-start.5 = (bf16[32,1152]{1,0:T(8,128)(2,1)S(1)}, bf16[32,1152]{1,0:T(8,128)(2,1)S(1)}, u32[]{:S(2)}, u32[]{:S(2)}) collective-permute-start(bf16[32,1152]{1,0:T(8,128)(2,1)S(1)} %get-tuple-element.13.refs_0_), channel_id=1, source_target_pairs={{0,24},{4,28},{8,16},{12,20},{16,8},{20,12},{24,0},{28,4},{1,25},{... | collective-permute-start | bytes 221192 | tf_op jit(solution)/shard_map/ppermute | solution.py:89
  6.8 0.0 collective-permute-start.3
  6.8 0.6 %collective-permute-start.1 = (bf16[32,1152]{1,0:T(8,128)(2,1)S(1)}, bf16[32,1152]{1,0:T(8,128)(2,1)S(1)}, u32[]{:S(2)}, u32[]{:S(2)}) collective-permute-start(bf16[32,1152]{1,0:T(8,128)(2,1)S(1)} %get-tuple-element.13.refs_0_), channel_id=1, source_target_pairs={{0,8},{4,12},{8,0},{12,4},{16,24},{20,28},{24,16},{28,20},{1,9},{5... | collective-permute-start | bytes 221192 | tf_op jit(solution)/shard_map/ppermute | solution.py:89
  7.5 1.6 %collective-permute-start = (bf16[32,1152]{1,0:T(8,128)(2,1)S(1)}, bf16[32,1152]{1,0:T(8,128)(2,1)S(1)}, u32[]{:S(2)}, u32[]{:S(2)}) collective-permute-start(bf16[32,1152]{1,0:T(8,128)(2,1)S(1)} %get-tuple-element.13.refs_0_), channel_id=1, source_target_pairs={{0,4},{4,0},{8,12},{12,8},{16,20},{20,16},{24,28},{28,24},{1,5},{5... | collective-permute-start | bytes 221192 | tf_op jit(solution)/shard_map/ppermute | solution.py:89
  9.1 0.4 %collective-permute-done.5.refs_6_ = bf16[32,1152]{1,0:T(8,128)(2,1)S(1)} collective-permute-done((bf16[32,1152]{1,0:T(8,128)(2,1)S(1)}, bf16[32,1152]{1,0:T(8,128)(2,1)S(1)}, u32[]{:S(2)}, u32[]{:S(2)}) %collective-permute-start.5) | collective-permute-done | bytes 73760 | tf_op jit(solution)/shard_map/ppermute | solution.py:89
  9.5 1.9 %collective-permute-start.6 = (bf16[32,1152]{1,0:T(8,128)(2,1)S(1)}, bf16[32,1152]{1,0:T(8,128)(2,1)S(1)}, u32[]{:S(2)}, u32[]{:S(2)}) collective-permute-start(bf16[32,1152]{1,0:T(8,128)(2,1)S(1)} %collective-permute-done.5.refs_6_), channel_id=1, source_target_pairs={{0,4},{4,0},{8,12},{12,8},{16,20},{20,16},{24,28},{28,24},{1,5},{5... | collective-permute-start | bytes 221192 | tf_op jit(solution)/shard_map/ppermute | solution.py:89
  11.4 1.7 %collective-permute-done.3.refs_4_ = bf16[32,1152]{1,0:T(8,128)(2,1)S(1)} collective-permute-done((bf16[32,1152]{1,0:T(8,128)(2,1)S(1)}, bf16[32,1152]{1,0:T(8,128)(2,1)S(1)}, u32[]{:S(2)}, u32[]{:S(2)}) %collective-permute-start.3) | collective-permute-done | bytes 73760 | tf_op jit(solution)/shard_map/ppermute | solution.py:89
  13.0 1.5 %collective-permute-start.4 = (bf16[32,1152]{1,0:T(8,128)(2,1)S(1)}, bf16[32,1152]{1,0:T(8,128)(2,1)S(1)}, u32[]{:S(2)}, u32[]{:S(2)}) collective-permute-start(bf16[32,1152]{1,0:T(8,128)(2,1)S(1)} %collective-permute-done.3.refs_4_), channel_id=1, source_target_pairs={{0,4},{4,0},{8,12},{12,8},{16,20},{20,16},{24,28},{28,24},{1,5},{5... | collective-permute-start | bytes 221192 | tf_op jit(solution)/shard_map/ppermute | solution.py:89
  14.5 0.0 collective-permute-done.1.cue_ref.refs_2_
  14.5 0.5 %collective-permute-start.2 = (bf16[32,1152]{1,0:T(8,128)(2,1)S(1)}, bf16[32,1152]{1,0:T(8,128)(2,1)S(1)}, u32[]{:S(2)}, u32[]{:S(2)}) collective-permute-start(bf16[32,1152]{1,0:T(8,128)(2,1)S(1)} %collective-permute-done.1.cue_ref.refs_2_), channel_id=1, source_target_pairs={{0,4},{4,0},{8,12},{12,8},{16,20},{20,16},{24,28},{28,24},{1,5},{5... | collective-permute-start | bytes 221192 | tf_op jit(solution)/shard_map/ppermute | solution.py:89
  15.1 2.5 %load.1 = (bf16[2,1024,1024]{2,1,0:T(8,128)(2,1)S(1)}, bf16[2,256,1024]{2,1,0:T(8,128)(2,1)S(1)}, bf16[16,1024]{1,0:T(8,128)(2,1)S(1)}) custom-call(bf16[32,1152]{1,0:T(8,128)(2,1)S(1)} %collective-permute-done.1.cue_ref.refs_2_, bf16[2,1024,1024]{2,1,0:T(8,128)(2,1)} %w_ref.1, bf16[2,256,1024]{2,1,0:T(8,128)(2,1)} %bitcast.10, bf16[16,1024]{1,0:T(8,128)(2,1)} %r_ref.1), custom_call_target="tpu_custom_call" | custom-call | flops 134217728 | bytes 8388608 | tf_op jit(solution)/shard_map/load/pallas_call | solution.py:351
  17.6 0.0 collective-permute-done.refs_1_
  17.6 0.0 collective-permute-done.6.refs_7_
  17.6 0.4 %collective-permute-done.4.refs_5_ = bf16[32,1152]{1,0:T(8,128)(2,1)S(1)} collective-permute-done((bf16[32,1152]{1,0:T(8,128)(2,1)S(1)}, bf16[32,1152]{1,0:T(8,128)(2,1)S(1)}, u32[]{:S(2)}, u32[]{:S(2)}) %collective-permute-start.4) | collective-permute-done | bytes 73760 | tf_op jit(solution)/shard_map/ppermute | solution.py:89
  18.0 0.9 %collective-permute-done.2.refs_3_ = bf16[32,1152]{1,0:T(8,128)(2,1)S(1)} collective-permute-done((bf16[32,1152]{1,0:T(8,128)(2,1)S(1)}, bf16[32,1152]{1,0:T(8,128)(2,1)S(1)}, u32[]{:S(2)}, u32[]{:S(2)}) %collective-permute-start.2) | collective-permute-done | bytes 73760 | tf_op jit(solution)/shard_map/ppermute | solution.py:89
  18.9 2.4 %partial.1 = (bf16[2,128,1024]{2,1,0:T(8,128)(2,1)S(1)}, bf16[2,128,1024]{2,1,0:T(8,128)(2,1)S(1)}, f32[8,4,128]{2,1,0:T(4,128)}) custom-call(bf16[32,1152]{1,0:T(8,128)(2,1)S(1)} %get-tuple-element.13.refs_0_, bf16[32,1152]{1,0:T(8,128)(2,1)S(1)} %collective-permute-done.refs_1_, bf16[32,1152]{1,0:T(8,128)(2,1)S(1)} %collective-permute-done.1.cue_ref.refs_2_, ...), custom_call_target="tpu_custom_call" | custom-call | flops 1073741824 | bytes 8388608 | tf_op jit(solution)/shard_map/partial/pallas_call | solution.py:372
  21.3 0.0 collective-permute-start.7
  21.3 1.9 %collective-permute-done.7.got_ref = bf16[2,128,1024]{2,1,0:T(8,128)(2,1)S(1)} collective-permute-done((bf16[2,128,1024]{2,1,0:T(8,128)(2,1)S(1)}, bf16[2,128,1024]{2,1,0:T(8,128)(2,1)S(1)}, u32[]{:S(2)}, u32[]{:S(2)}) %collective-permute-start.7) | collective-permute-done | bytes 524320 | tf_op jit(solution)/shard_map/ppermute | solution.py:388
  23.2 0.1 pair.1
  23.3 1.6 %collective-permute-start.8 = (bf16[128,1024]{1,0:T(8,128)(2,1)S(1)}, bf16[128,1024]{1,0:T(8,128)(2,1)S(1)}, u32[]{:S(2)}, u32[]{:S(2)}) collective-permute-start(bf16[128,1024]{1,0:T(8,128)(2,1)S(1)} %get-tuple-element.19), channel_id=1, source_target_pairs={{0,2},{1,3},{2,0},{3,1},{4,6},{5,7},{6,4},{7,5},{8,10},{9,11},{10,... | collective-permute-start | bytes 786440 | tf_op jit(solution)/shard_map/ppermute | solution.py:400
  24.9 3.3 %all-to-all-start = ((f32[32,1,128]{2,1,0:T(1,128)}), f32[32,1,128]{2,1,0:T(1,128)S(1)}, u32[]{:S(2)}, u32[]{:S(2)}) async-start(f32[32,1,128]{2,1,0:T(1,128)} %bitcast.5), calls=%async_computation | async-start | bytes 32768 | tf_op jit(solution)/shard_map/all_to_all | solution.py:389
  28.2 2.8 %weight.1 = bf16[2,1024,1024]{2,1,0:T(8,128)(2,1)} custom-call(bf16[32,1152]{1,0:T(8,128)(2,1)S(1)} %get-tuple-element.13.refs_0_, bf16[32,1152]{1,0:T(8,128)(2,1)S(1)} %collective-permute-done.refs_1_, bf16[32,1152]{1,0:T(8,128)(2,1)S(1)} %collective-permute-done.1.cue_ref.refs_2_, bf16[32,1152]{1,0:T(8,128)(2,1)S(1)} %collective-permute-done.2.refs_3_, ...), custom_call_target="tpu_custom_call" | custom-call | flops 1073741824 | bytes 6291456 | tf_op jit(solution)/shard_map/weight/pallas_call | solution.py:403
  31.0 4.3 %all-to-all-done = f32[32,1,128]{2,1,0:T(1,128)S(1)} async-done(((f32[32,1,128]{2,1,0:T(1,128)}), f32[32,1,128]{2,1,0:T(1,128)S(1)}, u32[]{:S(2)}, u32[]{:S(2)}) %all-to-all-start) | async-done | bytes 16416 | tf_op jit(solution)/shard_map/all_to_all | solution.py:389
  35.3 1.0 %router.1 = bf16[32,1024]{1,0:T(8,128)(2,1)} custom-call(f32[8,4,128]{2,1,0:T(4,128)S(1)} %bitcast.9, f32[2,3,8,128]{3,2,1,0:T(8,128)S(1)} %get-tuple-element.21.meta_ref, bf16[16,1024]{1,0:T(8,128)(2,1)S(1)} %get-tuple-element.22.w_ref), custom_call_target="tpu_custom_call" | custom-call | tf_op jit(solution)/shard_map/router/pallas_call | solution.py:421
  36.4 0.0 collective-permute-done.8
  36.4 0.8 %fusion = bf16[1,128,1024]{2,1,0:T(8,128)(2,1)} fusion(f32[128,1024]{1,0:T(8,128)S(1)} %get-tuple-element.18, bf16[128,1024]{1,0:T(8,128)(2,1)S(1)} %collective-permute-done.8), kind=kLoop, calls=%fused_computation.1 | loop fusion | flops 393216 | bytes 1048576 | tf_op jit(solution)/shard_map/broadcast_in_dim | solution.py:419
Async XLA Ops:
  1.7 7.8 %collective-permute-start.5 = (bf16[32,1152]{1,0:T(8,128)(2,1)S(1)}, bf16[32,1152]{1,0:T(8,128)(2,1)S(1)}, u32[]{:S(2)}, u32[]{:S(2)}) collective-permute-start(bf16[32,1152]{1,0:T(8,128)(2,1)S(1)} %get-tuple-element.13.refs_0_), channel_id=1, source_target_pairs={{0,24},{4,28},{8,16},{12,20},{16,8},{20,12},{24,0},{28,4},{1,25},{... | collective-permute-start | bytes 221192 | tf_op jit(solution)/shard_map/ppermute | solution.py:89
  6.8 6.2 %collective-permute-start.3 = (bf16[32,1152]{1,0:T(8,128)(2,1)S(1)}, bf16[32,1152]{1,0:T(8,128)(2,1)S(1)}, u32[]{:S(2)}, u32[]{:S(2)}) collective-permute-start(bf16[32,1152]{1,0:T(8,128)(2,1)S(1)} %get-tuple-element.13.refs_0_), channel_id=1, source_target_pairs={{0,16},{4,20},{8,24},{12,28},{16,0},{20,4},{24,8},{28,12},{1,17},{... | collective-permute-start | bytes 221192 | tf_op jit(solution)/shard_map/ppermute | solution.py:89
  6.8 7.7 %collective-permute-start.1 = (bf16[32,1152]{1,0:T(8,128)(2,1)S(1)}, bf16[32,1152]{1,0:T(8,128)(2,1)S(1)}, u32[]{:S(2)}, u32[]{:S(2)}) collective-permute-start(bf16[32,1152]{1,0:T(8,128)(2,1)S(1)} %get-tuple-element.13.refs_0_), channel_id=1, source_target_pairs={{0,8},{4,12},{8,0},{12,4},{16,24},{20,28},{24,16},{28,20},{1,9},{5... | collective-permute-start | bytes 221192 | tf_op jit(solution)/shard_map/ppermute | solution.py:89
  7.5 10.2 %collective-permute-start = (bf16[32,1152]{1,0:T(8,128)(2,1)S(1)}, bf16[32,1152]{1,0:T(8,128)(2,1)S(1)}, u32[]{:S(2)}, u32[]{:S(2)}) collective-permute-start(bf16[32,1152]{1,0:T(8,128)(2,1)S(1)} %get-tuple-element.13.refs_0_), channel_id=1, source_target_pairs={{0,4},{4,0},{8,12},{12,8},{16,20},{20,16},{24,28},{28,24},{1,5},{5... | collective-permute-start | bytes 221192 | tf_op jit(solution)/shard_map/ppermute | solution.py:89
  9.5 8.1 %collective-permute-start.6 = (bf16[32,1152]{1,0:T(8,128)(2,1)S(1)}, bf16[32,1152]{1,0:T(8,128)(2,1)S(1)}, u32[]{:S(2)}, u32[]{:S(2)}) collective-permute-start(bf16[32,1152]{1,0:T(8,128)(2,1)S(1)} %collective-permute-done.5.refs_6_), channel_id=1, source_target_pairs={{0,4},{4,0},{8,12},{12,8},{16,20},{20,16},{24,28},{28,24},{1,5},{5... | collective-permute-start | bytes 221192 | tf_op jit(solution)/shard_map/ppermute | solution.py:89
  13.0 5.0 %collective-permute-start.4 = (bf16[32,1152]{1,0:T(8,128)(2,1)S(1)}, bf16[32,1152]{1,0:T(8,128)(2,1)S(1)}, u32[]{:S(2)}, u32[]{:S(2)}) collective-permute-start(bf16[32,1152]{1,0:T(8,128)(2,1)S(1)} %collective-permute-done.3.refs_4_), channel_id=1, source_target_pairs={{0,4},{4,0},{8,12},{12,8},{16,20},{20,16},{24,28},{28,24},{1,5},{5... | collective-permute-start | bytes 221192 | tf_op jit(solution)/shard_map/ppermute | solution.py:89
  14.5 4.4 %collective-permute-start.2 = (bf16[32,1152]{1,0:T(8,128)(2,1)S(1)}, bf16[32,1152]{1,0:T(8,128)(2,1)S(1)}, u32[]{:S(2)}, u32[]{:S(2)}) collective-permute-start(bf16[32,1152]{1,0:T(8,128)(2,1)S(1)} %collective-permute-done.1.cue_ref.refs_2_), channel_id=1, source_target_pairs={{0,4},{4,0},{8,12},{12,8},{16,20},{20,16},{24,28},{28,24},{1,5},{5... | collective-permute-start | bytes 221192 | tf_op jit(solution)/shard_map/ppermute | solution.py:89
  21.3 1.9 %collective-permute-start.7 = (bf16[2,128,1024]{2,1,0:T(8,128)(2,1)S(1)}, bf16[2,128,1024]{2,1,0:T(8,128)(2,1)S(1)}, u32[]{:S(2)}, u32[]{:S(2)}) collective-permute-start(bf16[2,128,1024]{2,1,0:T(8,128)(2,1)S(1)} %get-tuple-element.17), channel_id=1, source_target_pairs={{0,1},{1,0},{2,3},{3,2},{4,5},{5,4},{6,7},{7,6},{8,9},{9,8},{10,11... | collective-permute-start | bytes 1572872 | tf_op jit(solution)/shard_map/ppermute | solution.py:388
  23.3 13.1 %collective-permute-start.8 = (bf16[128,1024]{1,0:T(8,128)(2,1)S(1)}, bf16[128,1024]{1,0:T(8,128)(2,1)S(1)}, u32[]{:S(2)}, u32[]{:S(2)}) collective-permute-start(bf16[128,1024]{1,0:T(8,128)(2,1)S(1)} %get-tuple-element.19), channel_id=1, source_target_pairs={{0,2},{1,3},{2,0},{3,1},{4,6},{5,7},{6,4},{7,5},{8,10},{9,11},{10,... | collective-permute-start | bytes 786440 | tf_op jit(solution)/shard_map/ppermute | solution.py:400
  24.9 10.4 %all-to-all-start = ((f32[32,1,128]{2,1,0:T(1,128)}), f32[32,1,128]{2,1,0:T(1,128)S(1)}, u32[]{:S(2)}, u32[]{:S(2)}) async-start(f32[32,1,128]{2,1,0:T(1,128)} %bitcast.5), calls=%async_computation | async-start | bytes 32768 | tf_op jit(solution)/shard_map/all_to_all | solution.py:389

commit v3 on v2

--- a/solution.py
+++ b/solution.py
@@ -89,14 +89,20 @@
     return lax.ppermute(x, "grp", [(i, i ^ distance) for i in range(count)])
 
 
+def swap_order(count):
+    top, rest = count - 2, list(range(2, count - 2, 2))
+    return [top, 1] + rest + [top ^ 1, 3] + [d ^ 1 for d in rest if d != 2]
+
+
 def gather_blocks(x):
     count = lax.axis_size("grp")
     blocks = {0: x}
-    far = sorted(range(2, count, 2), key=lambda d: (d != count // 2, -d))
-    for distance in far:
-        blocks[distance] = exchange(x, distance)
-    for distance in [0] + far:
-        blocks[distance ^ 1] = exchange(blocks[distance], 1)
+    for distance in swap_order(count):
+        if distance == 3:
+            source, step = 1, 2
+        else:
+            source, step = (distance ^ 1, 1) if distance & 1 else (0, distance)
+        blocks[distance] = exchange(blocks[source], step)
     return [blocks[d] for d in range(count)]
 
 
@@ -149,53 +155,29 @@
     copies[2].wait()
 
 
-def load_kernel(parts, cue_ref, w_ref, h_ref, r_ref, w_out, h_out, r_out, sems):
-    rows = w_ref.shape[1] // parts
-    copies = [
-        pltpu.make_async_copy(
-            w_ref.at[l, pl.ds(i * rows, rows)],
-            w_out.at[l, pl.ds(i * rows, rows)],
-            sems.at[l * parts + i],
-        )
-        for l in range(w_ref.shape[0])
-        for i in range(parts)
-    ]
-    base = w_ref.shape[0] * parts
-    copies.append(pltpu.make_async_copy(h_ref, h_out, sems.at[base]))
-    copies.append(pltpu.make_async_copy(r_ref, r_out, sems.at[base + 1]))
-    for c in copies:
-        c.start()
-    for c in copies:
-        c.wait()
-
-
-def partial_kernel(local, groups, capacity, *refs):
-    blocks = refs[:groups]
-    w_ref, h_ref, keep_ref, send_ref, score_ref = refs[groups:]
-    features, width = w_ref.shape[1], w_ref.shape[2]
-    span = groups * capacity
-    tokens = groups * blocks[0].shape[0]
+def half_of(parity, local, groups, capacity, blocks, saved_ref, weight, outs):
+    keep_ref, send_ref = outs
+    block_rows, features = blocks[0].shape[0], blocks[0].shape[1] - LANES
+    width = keep_ref.shape[2]
+    count = groups // 2
+    span, tokens = count * capacity, count * block_rows
     cols = 256 if width % 256 == 0 else LANES
-    own, half = lax.axis_index("grp"), lax.rem(lax.axis_index("ep"), 2)
+    own, side = lax.axis_index("grp"), lax.rem(lax.axis_index("ep"), 2)
     rows = jnp.concatenate([b[:, :features] for b in blocks], axis=0)
-    aux = jnp.concatenate([b[:, features:] for b in blocks], axis=0).astype(jnp.float32)
-    aux = aux.T
-    source = (iota((1, tokens), 1) // blocks[0].shape[0]) ^ own
-    slot = iota((span, tokens), 0) + half * (span // 2)
+    aux = jnp.concatenate([b[:, features:] for b in blocks], axis=0).astype(jnp.float32).T
+    source = (iota((1, tokens), 1) // block_rows) ^ (own // 2)
+    slot = iota((span, tokens), 0) + side * (span // 2)
     slot = jnp.where(slot >= span, slot - span, slot)
+    near = pl.ds(side * (count // 2), count // 2)
+    away = pl.ds((1 - side) * (count // 2), count // 2)
     part_row, part_lane = iota((span, LANES), 0), iota((span, LANES), 1)
-    near = pl.ds(pl.multiple_of(half * (span // 2), span // 2), span // 2)
-    away = pl.ds(pl.multiple_of((1 - half) * (span // 2), span // 2), span // 2)
-    sent = jnp.zeros((groups, LANES), jnp.float32)
+    sent = jnp.zeros((count, LANES), jnp.float32)
     for l in range(local):
         lane = l * groups + own
-        prob = jnp.sum(jnp.where(iota(aux.shape, 0) == lane, aux, 0.0), axis=0, keepdims=True)
-        rank = jnp.sum(
-            jnp.where(iota(aux.shape, 0) == local * groups + lane, aux, 0.0),
-            axis=0,
-            keepdims=True,
-        ).astype(jnp.int32)
-        place = jnp.where(rank > 0, source * capacity + rank - 1, -1)
+        row = iota(aux.shape, 0)
+        prob = jnp.sum(jnp.where(row == lane, aux, 0.0), axis=0, keepdims=True)
+        rank = jnp.sum(jnp.where(row == local * groups + lane, aux, 0.0), axis=0, keepdims=True)
+        place = jnp.where(rank > 0, source * capacity + rank.astype(jnp.int32) - 1, -1)
         pick = slot == place
         scale = jnp.sum(jnp.where(pick, prob, 0.0), axis=1, keepdims=True)
         grads = jnp.dot(
@@ -204,8 +186,14 @@
         score = jnp.zeros((span, LANES), jnp.float32)
         for n in range(width // cols):
             part = pl.ds(n * cols, cols)
-            term = jnp.dot(grads, w_ref[l, :, part], preferred_element_type=jnp.float32)
-            saved = jnp.concatenate([h_ref[l, near, part], h_ref[l, away, part]], axis=0)
+            term = jnp.dot(grads, weight(l, n, cols), preferred_element_type=jnp.float32)
+            saved = jnp.concatenate(
+                [
+                    saved_ref[l, where, parity, :, part].reshape(span // 2, cols)
+                    for where in (near, away)
+                ],
+                axis=0,
+            )
             product = term * saved.astype(jnp.float32)
             for k in range(cols // LANES):
                 score = score + product[:, k * LANES : (k + 1) * LANES]
@@ -214,10 +202,74 @@
             send_ref[l, :, part] = out[span // 2 :]
         score = jnp.sum(score, axis=1, keepdims=True)
         spread = jnp.where(lax.rem(part_row, capacity) + l * capacity == part_lane, score, 0.0)
-        sent = sent + jnp.sum(spread.reshape(groups, capacity, LANES), axis=1)
-    turned = jnp.concatenate([sent[groups // 2 :], sent[: groups // 2]], axis=0)
-    sent = jnp.where(half == 0, sent, turned)
-    score_ref[...] = jnp.broadcast_to(sent[:, None, :], score_ref.shape)
+        sent = sent + jnp.sum(spread.reshape(count, capacity, LANES), axis=1)
+    turned = jnp.concatenate([sent[count // 2 :], sent[: count // 2]], axis=0)
+    return jnp.where(side == 0, sent, turned)
+
+
+def first_kernel(local, groups, capacity, *refs):
+    count = groups // 2
+    blocks, sources = refs[:count], refs[count : count + 3]
+    w_ref, h_ref, r_ref, keep_ref, send_ref, score_ref, w_sems, sems = refs[count + 3 :]
+    cols = w_ref.shape[2] // w_sems.shape[1]
+
+    def fetch(l, n):
+        part = pl.ds(n * cols, cols)
+        return pltpu.make_async_copy(
+            sources[0].at[l, :, part], w_ref.at[l, :, part], w_sems.at[l, n]
+        )
+
+    others = [
+        pltpu.make_async_copy(sources[1], h_ref, sems.at[0]),
+        pltpu.make_async_copy(sources[2], r_ref, sems.at[1]),
+    ]
+    fetch(0, 0).start()
+    others[0].start()
+    for i in range(1, local * w_sems.shape[1]):
+        fetch(i // w_sems.shape[1], i % w_sems.shape[1]).start()
+    others[1].start()
+    waited = set()
+
+    def weight(l, n, size):
+        piece = n * size // cols
+        if (l, piece) not in waited:
+            fetch(l, piece).wait()
+            if not waited:
+                others[0].wait()
+            waited.add((l, piece))
+        return w_ref[l, :, pl.ds(n * size, size)]
+
+    score_ref[...] = half_of(
+        lax.rem(lax.axis_index("grp"), 2),
+        local,
+        groups,
+        capacity,
+        blocks,
+        h_ref,
+        weight,
+        (keep_ref, send_ref),
+    )
+    others[1].wait()
+
+
+def second_kernel(local, groups, capacity, *refs):
+    count = groups // 2
+    blocks = refs[:count]
+    w_ref, h_ref, other_ref, keep_ref, send_ref, score_ref = refs[count:]
+    parity = 1 - lax.rem(lax.axis_index("grp"), 2)
+
+    def weight(l, n, size):
+        return w_ref[l, :, pl.ds(n * size, size)]
+
+    mine = half_of(
+        parity, local, groups, capacity, blocks, h_ref, weight, (keep_ref, send_ref)
+    )
+    other = other_ref[...]
+    for x in range(2):
+        value = jnp.where(parity == x, mine, other)
+        score_ref[:, x] = jnp.broadcast_to(
+            value[:, None, :], (count,) + score_ref.shape[2:]
+        )
 
 
 def weight_kernel(local, groups, capacity, parts, *refs):
@@ -258,12 +310,15 @@
         copy.wait()
 
 
-def pair_kernel(mine_ref, got_ref, keep_ref, send_ref):
+def pair_kernel(mine_a, got_a, mine_b, got_b, keep_ref, send_ref):
     bit = lax.axis_index("ep") // 2
-    keep_ref[...] = mine_ref[bit].astype(jnp.float32) + got_ref[bit].astype(jnp.float32)
-    send_ref[...] = (
-        mine_ref[1 - bit].astype(jnp.float32) + got_ref[1 - bit].astype(jnp.float32)
-    ).astype(jnp.bfloat16)
+    parity = lax.rem(lax.axis_index("grp"), 2)
+    shape = keep_ref.shape[:1] + keep_ref.shape[2:]
+    for at, mine, got in ((parity, mine_a, got_a), (1 - parity, mine_b, got_b)):
+        kept_sum = mine[bit].astype(jnp.float32) + got[bit].astype(jnp.float32)
+        sent_sum = mine[1 - bit].astype(jnp.float32) + got[1 - bit].astype(jnp.float32)
+        keep_ref[:, at] = kept_sum.reshape(shape)
+        send_ref[:, at] = sent_sum.astype(jnp.bfloat16).reshape(shape)
 
 
 def router_kernel(local, capacity, score_ref, meta_ref, w_ref, out_ref):
@@ -348,55 +403,56 @@
     )(away_from_vmem(expert_ids.T), away_from_vmem(router_logits.T), away_from_vmem(out_grad))
     blocks = [held(b) for b in gather_blocks(packed)]
 
-    weights, saved, projection = pl.pallas_call(
-        functools.partial(load_kernel, 2),
+    saved_shape = (local, groups // 2, 2, capacity, width)
+    sums = [kept((local, span // 4, width), bf16)] * 2
+    work = slot_count * features * width
+    weights, saved, projection, keep_a, send_a, score_a = pl.pallas_call(
+        functools.partial(first_kernel, local, groups, capacity),
         out_shape=(
-            pltpu.VMEM(expert_weight.shape, bf16),
-            pltpu.VMEM((local, span, width), bf16),
-            pltpu.VMEM(router_weight.shape, bf16),
+            kept(expert_weight.shape, bf16),
+            kept(saved_shape, bf16),
+            kept(router_weight.shape, bf16),
+            *sums,
+            kept((groups // 2, LANES), f32),
         ),
-        in_specs=[vmem] + [hbm] * 3,
-        out_specs=(vmem, vmem, vmem),
-        scratch_shapes=[pltpu.SemaphoreType.DMA((2 * local + 2,))],
-        compiler_params=limit(2),
-        cost_estimate=cost(2**27, 8 * 2**20),
-        name="load",
+        in_specs=[vmem] * (groups // 2) + [hbm] * 3,
+        out_specs=(vmem,) * 6,
+        scratch_shapes=[pltpu.SemaphoreType.DMA((local, 1)), pltpu.SemaphoreType.DMA((2,))],
+        compiler_params=limit(8),
+        cost_estimate=cost(work, 8 * 2**20),
+        name="first",
     )(
-        blocks[2],
+        *blocks[0::2],
         away_from_vmem(expert_weight),
-        away_from_vmem(hidden_saved.reshape(local, span, width)),
+        away_from_vmem(hidden_saved.reshape(saved_shape)),
         away_from_vmem(router_weight),
     )
-    weights, saved, projection = held(weights), held(saved), held(projection)
-
-    keep, send, score = pl.pallas_call(
-        functools.partial(partial_kernel, local, groups, capacity),
-        out_shape=(
-            pltpu.VMEM((local, span // 2, width), bf16),
-            pltpu.VMEM((local, span // 2, width), bf16),
-            pltpu.VMEM((groups, ep_count, LANES), f32),
-        ),
-        in_specs=[vmem] * (groups + 2),
-        out_specs=(vmem, vmem, vmem),
-        compiler_params=limit(8),
-        cost_estimate=cost(2 * slot_count * features * width, 8 * 2**20),
-        name="partial",
-    )(*blocks, weights, saved)
-
     core_pairs = [(i, i ^ 1) for i in range(ep_count)]
     chip_pairs = [(i, i ^ 2) for i in range(ep_count)]
-    got = lax.ppermute(send, "ep", core_pairs)
+    got_a = lax.ppermute(send_a, "ep", core_pairs)
+
+    keep_b, send_b, score = pl.pallas_call(
+        functools.partial(second_kernel, local, groups, capacity),
+        out_shape=(*sums, kept((groups // 2, 2, ep_count, LANES), f32)),
+        in_specs=[vmem] * (groups // 2 + 3),
+        out_specs=(vmem,) * 3,
+        compiler_params=limit(8),
+        cost_estimate=cost(work, 4 * 2**20),
+        name="second",
+    )(*blocks[1::2], held(weights), held(saved), held(score_a))
+    got_b = lax.ppermute(send_b, "ep", core_pairs)
     from_all = lax.all_to_all(
         score.reshape(groups * ep_count, 1, LANES), ("grp", "ep"), 0, 0, tiled=True
     )
+    order = (groups // 4, 2, capacity, width)
     mine, away = pl.pallas_call(
         pair_kernel,
-        out_shape=(kept((span // 2, width), f32), kept((span // 2, width), bf16)),
-        in_specs=[vmem, vmem],
+        out_shape=(kept(order, f32), kept(order, bf16)),
+        in_specs=[vmem] * 4,
         out_specs=(vmem, vmem),
         compiler_params=limit(2),
         name="pair",
-    )(held(keep), held(got))
+    )(held(keep_a), held(got_a), held(keep_b), held(got_b))
     last = lax.ppermute(away, "ep", chip_pairs)
 
     parts = 4
@@ -414,9 +470,9 @@
         compiler_params=limit(12),
         cost_estimate=cost(2 * slot_count * features * width, 6 * 2**20),
         name="weight",
-    )(*blocks, saved)
-
-    hidden_grad = (mine + last.astype(f32)).astype(bf16)[None]
+    )(*blocks, held(saved.reshape(local, span, width)))
+
+    hidden_grad = (mine + last.astype(f32)).astype(bf16).reshape(1, span // 2, width)
 
     input_grad = pl.pallas_call(
         functools.partial(router_kernel, local, capacity),
@@ -425,7 +481,7 @@
         out_specs=vmem,
         compiler_params=limit(2),
         name="router",
-    )(held(from_all.reshape(groups, ep_count, LANES)), held(meta), projection)
+    )(held(from_all.reshape(groups, ep_count, LANES)), held(meta), held(projection))
     return (weight_grad, hidden_grad, input_grad)
 
 

time: 37.3 us -> 36.2 us (0.971)
  waiting for transfers between devices: 9.48 us -> 8.86 us
  starting transfers between devices: 16.2 us -> 15.6 us
    convert_element_type x0 -> x1, other arithmetic: none -> 0.78 us  [token_plan(): (mine + last.astype(f32)).astype(bf16).reshape(1, span // 2, width)]
    broadcast_in_dim x1 -> x0, other arithmetic: 0.76 us -> none  [token_plan(): hidden_grad = (mine + last.astype(f32)).astype(bf16)[None]]
    ppermute x7, starting transfers between devices: 11.3 us -> 10.9 us  [exchange(): return lax.ppermute(x, 'grp', [(i, i ^ distance) for i in range(count)])]
    ppermute x1 -> x2, waiting for transfers between devices: 1.91 us -> 1.53 us  [the longest x1 1.53 us: token_plan(): got_b = lax.ppermute(send_b, 'ep', core_pairs)]
  transfers between devices with their start and end apart: 10 -> 11, of which waited for: 6 -> 5; matrix products, arithmetic and copies ran while one was open for 0% -> 0% of each run, Pallas kernels for 17% -> 25%
where the time goes in v3:
time: 36.2 us; the launch traced here: 36 us
  starting transfers between devices  15.6 us (43%)
  Pallas kernels  10.1 us (28%)
  waiting for transfers between devices  8.86 us (24%)
  other arithmetic  0.78 us (2%)
  between operations  0.7 us (2%)
    ppermute x7, starting transfers between devices, exchange(): return lax.ppermute(x, 'grp', [(i, i ^ distance) for i in range(count)])  10.9 us
    all_to_all x1, waiting for transfers between devices, token_plan(): lax.all_to_all(score.reshape(groups * ep_count, 1, LANES), ('grp', 'ep'),...  4.27 us
    pallas_call x1, Pallas kernels, token_plan(): pl.pallas_call(functools.partial(first_kernel, local, groups, capacity),...  3.22 us
    ppermute x7, waiting for transfers between devices, exchange(): return lax.ppermute(x, 'grp', [(i, i ^ distance) for i in range(count)])  3.06 us
    all_to_all x1, starting transfers between devices, token_plan(): lax.all_to_all(score.reshape(groups * ep_count, 1, LANES), ('grp', 'ep'),...  2.98 us
    pallas_call x1, Pallas kernels, token_plan(): pl.pallas_call(functools.partial(weight_kernel, local, groups, capacity,...  2.83 us
    pallas_call x1, Pallas kernels, token_plan(): pl.pallas_call(functools.partial(second_kernel, local, groups, capacity),...  1.82 us
    ppermute x1, starting transfers between devices, token_plan(): last = lax.ppermute(away, 'ep', chip_pairs)  1.58 us
  transfers between devices with their start and end apart: 11, of which 5 were waited for; matrix products, arithmetic and copies ran while one was open for 0% of the time, Pallas kernels for 25%

profile of v3, /device:TPU:0, one launch (start us, length us, event | category | flops | bytes accessed | tf_op | source)
XLA Modules:
  0.0 36.0 jit_solution(17624650616830244277)
XLA Ops:
  0.6 1.0 %pack.1 = (bf16[32,1152]{1,0:T(8,128)(2,1)S(1)}, f32[2,3,8,128]{3,2,1,0:T(8,128)S(1)}) custom-call(s32[8,32]{1,0:T(8,128)} %bitcast.14, f32[16,32]{1,0:T(8,128)} %bitcast.13, bf16[32,1024]{1,0:T(8,128)(2,1)} %rows_hbm.1), custom_call_target="tpu_custom_call" | custom-call | tf_op jit(solution)/shard_map/pack/pallas_call | solution.py:388
  1.7 5.1 %collective-permute-start.5 = (bf16[32,1152]{1,0:T(8,128)(2,1)S(1)}, bf16[32,1152]{1,0:T(8,128)(2,1)S(1)}, u32[]{:S(2)}, u32[]{:S(2)}) collective-permute-start(bf16[32,1152]{1,0:T(8,128)(2,1)S(1)} %get-tuple-element.16.refs_0_), channel_id=1, source_target_pairs={{0,24},{4,28},{8,16},{12,20},{16,8},{20,12},{24,0},{28,4},{1,25},{... | collective-permute-start | bytes 221192 | tf_op jit(solution)/shard_map/ppermute | solution.py:89
  6.8 0.0 collective-permute-start.3
  6.8 1.5 %collective-permute-start = (bf16[32,1152]{1,0:T(8,128)(2,1)S(1)}, bf16[32,1152]{1,0:T(8,128)(2,1)S(1)}, u32[]{:S(2)}, u32[]{:S(2)}) collective-permute-start(bf16[32,1152]{1,0:T(8,128)(2,1)S(1)} %get-tuple-element.16.refs_0_), channel_id=1, source_target_pairs={{0,4},{4,0},{8,12},{12,8},{16,20},{20,16},{24,28},{28,24},{1,5},{5... | collective-permute-start | bytes 221192 | tf_op jit(solution)/shard_map/ppermute | solution.py:89
  8.3 0.8 %collective-permute-start.1 = (bf16[32,1152]{1,0:T(8,128)(2,1)S(1)}, bf16[32,1152]{1,0:T(8,128)(2,1)S(1)}, u32[]{:S(2)}, u32[]{:S(2)}) collective-permute-start(bf16[32,1152]{1,0:T(8,128)(2,1)S(1)} %get-tuple-element.16.refs_0_), channel_id=1, source_target_pairs={{0,8},{4,12},{8,0},{12,4},{16,24},{20,28},{24,16},{28,20},{1,9},{5... | collective-permute-start | bytes 221192 | tf_op jit(solution)/shard_map/ppermute | solution.py:89
  9.1 0.4 %collective-permute-done.5.refs_3_.refs_6_ = bf16[32,1152]{1,0:T(8,128)(2,1)S(1)} collective-permute-done((bf16[32,1152]{1,0:T(8,128)(2,1)S(1)}, bf16[32,1152]{1,0:T(8,128)(2,1)S(1)}, u32[]{:S(2)}, u32[]{:S(2)}) %collective-permute-start.5) | collective-permute-done | bytes 73760 | tf_op jit(solution)/shard_map/ppermute | solution.py:89
  9.5 1.9 %collective-permute-start.6 = (bf16[32,1152]{1,0:T(8,128)(2,1)S(1)}, bf16[32,1152]{1,0:T(8,128)(2,1)S(1)}, u32[]{:S(2)}, u32[]{:S(2)}) collective-permute-start(bf16[32,1152]{1,0:T(8,128)(2,1)S(1)} %collective-permute-done.5.refs_3_.refs_6_), channel_id=1, source_target_pairs={{0,4},{4,0},{8,12},{12,8},{16,20},{20,16},{24,28},{28,24},{1,5},{5... | collective-permute-start | bytes 221192 | tf_op jit(solution)/shard_map/ppermute | solution.py:89
  11.4 1.8 %collective-permute-done.3.refs_2_.refs_4_ = bf16[32,1152]{1,0:T(8,128)(2,1)S(1)} collective-permute-done((bf16[32,1152]{1,0:T(8,128)(2,1)S(1)}, bf16[32,1152]{1,0:T(8,128)(2,1)S(1)}, u32[]{:S(2)}, u32[]{:S(2)}) %collective-permute-start.3) | collective-permute-done | bytes 73760 | tf_op jit(solution)/shard_map/ppermute | solution.py:89
  13.1 1.5 %collective-permute-start.4 = (bf16[32,1152]{1,0:T(8,128)(2,1)S(1)}, bf16[32,1152]{1,0:T(8,128)(2,1)S(1)}, u32[]{:S(2)}, u32[]{:S(2)}) collective-permute-start(bf16[32,1152]{1,0:T(8,128)(2,1)S(1)} %collective-permute-done.3.refs_2_.refs_4_), channel_id=1, source_target_pairs={{0,4},{4,0},{8,12},{12,8},{16,20},{20,16},{24,28},{28,24},{1,5},{5... | collective-permute-start | bytes 221192 | tf_op jit(solution)/shard_map/ppermute | solution.py:89
  14.6 0.0 collective-permute-done.refs_1_.refs_0_
  14.6 0.1 collective-permute-start.2
  14.8 0.0 collective-permute-done.1.refs_1_.refs_2_
  14.8 3.2 %first.1 = (bf16[2,1024,1024]{2,1,0:T(8,128)(2,1)S(1)}, bf16[2,4,2,32,1024]{4,3,2,1,0:T(8,128)(2,1)S(1)}, bf16[16,1024]{1,0:T(8,128)(2,1)S(1)}, bf16[2,64,1024]{...) custom-call(bf16[32,1152]{1,0:T(8,128)(2,1)S(1)} %get-tuple-element.16.refs_0_, ...), custom_call_target="tpu_custom_call" | custom-call | flops 536870912 | bytes 8388608 | tf_op jit(solution)/shard_map/first/pallas_call | solution.py:409
  18.0 0.1 collective-permute-start.7
  18.1 0.0 collective-permute-done.6.refs_7_.refs_3_
  18.1 0.0 collective-permute-done.4.refs_5_.refs_2_
  18.1 0.9 %collective-permute-done.2.refs_3_.refs_1_ = bf16[32,1152]{1,0:T(8,128)(2,1)S(1)} collective-permute-done((bf16[32,1152]{1,0:T(8,128)(2,1)S(1)}, bf16[32,1152]{1,0:T(8,128)(2,1)S(1)}, u32[]{:S(2)}, u32[]{:S(2)}) %collective-permute-start.2) | collective-permute-done | bytes 73760 | tf_op jit(solution)/shard_map/ppermute | solution.py:89
  19.0 1.8 %second.1 = (bf16[2,64,1024]{2,1,0:T(8,128)(2,1)S(1)}, bf16[2,64,1024]{2,1,0:T(8,128)(2,1)S(1)}, f32[4,2,4,128]{3,2,1,0:T(4,128)}) custom-call(bf16[32,1152]{1,0:T(8,128)(2,1)S(1)} %collective-permute-done.refs_1_.refs_0_, bf16[32,1152]{1,0:T(8,128)(2,1)S(1)} %collective-permute-done.2.refs_3_.refs_1_, ...), custom_call_target="tpu_custom_call" | custom-call | flops 536870912 | bytes 4194304 | tf_op jit(solution)/shard_map/second/pallas_call | solution.py:434
  20.8 0.0 collective-permute-start.8
  20.8 0.0 collective-permute-done.7.got_a
  20.8 1.5 %collective-permute-done.8.got_b = bf16[2,64,1024]{2,1,0:T(8,128)(2,1)S(1)} collective-permute-done((bf16[2,64,1024]{2,1,0:T(8,128)(2,1)S(1)}, bf16[2,64,1024]{2,1,0:T(8,128)(2,1)S(1)}, u32[]{:S(2)}, u32[]{:S(2)}) %collective-permute-start.8) | collective-permute-done | bytes 262176 | tf_op jit(solution)/shard_map/ppermute | solution.py:443
  22.3 0.1 pair.1
  22.5 1.6 %collective-permute-start.9 = (bf16[2,2,32,1024]{3,2,1,0:T(8,128)(2,1)S(1)}, bf16[2,2,32,1024]{3,2,1,0:T(8,128)(2,1)S(1)}, u32[]{:S(2)}, u32[]{:S(2)}) collective-permute-start(bf16[2,2,32,1024]{3,2,1,0:T(8,128)(2,1)S(1)} %get-tuple-element.25), channel_id=1, source_target_pairs={{0,2},{1,3},{2,0},{3,1},{4,6},{5,7},{6,4},{7,5},{8,10},{9,11},{10,... | collective-permute-start | bytes 786440 | tf_op jit(solution)/shard_map/ppermute | solution.py:456
  24.0 3.0 %all-to-all-start = ((f32[32,1,128]{2,1,0:T(1,128)}), f32[32,1,128]{2,1,0:T(1,128)S(1)}, u32[]{:S(2)}, u32[]{:S(2)}) async-start(f32[32,1,128]{2,1,0:T(1,128)} %bitcast.6), calls=%async_computation | async-start | bytes 32768 | tf_op jit(solution)/shard_map/all_to_all | solution.py:444
  27.0 2.8 %weight.1 = bf16[2,1024,1024]{2,1,0:T(8,128)(2,1)} custom-call(bf16[32,1152]{1,0:T(8,128)(2,1)S(1)} %get-tuple-element.16.refs_0_, bf16[32,1152]{1,0:T(8,128)(2,1)S(1)} %collective-permute-done.refs_1_.refs_0_, bf16[32,1152]{1,0:T(8,128)(2,1)S(1)} %collective-permute-done.1.refs_1_.refs_2_, bf16[32,1152]{1,0:T(8,128)(2,1)S(1)} %collective-permute-done.2.refs_3_.refs_1_, ...), custom_call_target="tpu_custom_call" | custom-call | flops 1073741824 | bytes 6291456 | tf_op jit(solution)/shard_map/weight/pallas_call | solution.py:459
  29.9 4.3 %all-to-all-done = f32[32,1,128]{2,1,0:T(1,128)S(1)} async-done(((f32[32,1,128]{2,1,0:T(1,128)}), f32[32,1,128]{2,1,0:T(1,128)S(1)}, u32[]{:S(2)}, u32[]{:S(2)}) %all-to-all-start) | async-done | bytes 16416 | tf_op jit(solution)/shard_map/all_to_all | solution.py:444
  34.1 1.0 %router.1 = bf16[32,1024]{1,0:T(8,128)(2,1)} custom-call(f32[8,4,128]{2,1,0:T(4,128)S(1)} %bitcast.10, f32[2,3,8,128]{3,2,1,0:T(8,128)S(1)} %get-tuple-element.27.meta_ref, bf16[16,1024]{1,0:T(8,128)(2,1)S(1)} %get-tuple-element.28.w_ref), custom_call_target="tpu_custom_call" | custom-call | tf_op jit(solution)/shard_map/router/pallas_call | solution.py:477
  35.2 0.0 collective-permute-done.9
  35.2 0.8 %add_convert_fusion = bf16[2,2,32,1024]{3,2,1,0:T(8,128)(2,1)} fusion(f32[2,2,32,1024]{3,2,1,0:T(8,128)S(1)} %get-tuple-element.24, bf16[2,2,32,1024]{3,2,1,0:T(8,128)(2,1)S(1)} %collective-permute-done.9), kind=kLoop, calls=%fused_computation | loop fusion | flops 393216 | bytes 1048576 | tf_op jit(solution)/shard_map/convert_element_type | solution.py:475
Async XLA Ops:
  1.7 7.8 %collective-permute-start.5 = (bf16[32,1152]{1,0:T(8,128)(2,1)S(1)}, bf16[32,1152]{1,0:T(8,128)(2,1)S(1)}, u32[]{:S(2)}, u32[]{:S(2)}) collective-permute-start(bf16[32,1152]{1,0:T(8,128)(2,1)S(1)} %get-tuple-element.16.refs_0_), channel_id=1, source_target_pairs={{0,24},{4,28},{8,16},{12,20},{16,8},{20,12},{24,0},{28,4},{1,25},{... | collective-permute-start | bytes 221192 | tf_op jit(solution)/shard_map/ppermute | solution.py:89
  6.8 6.3 %collective-permute-start.3 = (bf16[32,1152]{1,0:T(8,128)(2,1)S(1)}, bf16[32,1152]{1,0:T(8,128)(2,1)S(1)}, u32[]{:S(2)}, u32[]{:S(2)}) collective-permute-start(bf16[32,1152]{1,0:T(8,128)(2,1)S(1)} %get-tuple-element.16.refs_0_), channel_id=1, source_target_pairs={{0,16},{4,20},{8,24},{12,28},{16,0},{20,4},{24,8},{28,12},{1,17},{... | collective-permute-start | bytes 221192 | tf_op jit(solution)/shard_map/ppermute | solution.py:89
  6.8 7.8 %collective-permute-start = (bf16[32,1152]{1,0:T(8,128)(2,1)S(1)}, bf16[32,1152]{1,0:T(8,128)(2,1)S(1)}, u32[]{:S(2)}, u32[]{:S(2)}) collective-permute-start(bf16[32,1152]{1,0:T(8,128)(2,1)S(1)} %get-tuple-element.16.refs_0_), channel_id=1, source_target_pairs={{0,4},{4,0},{8,12},{12,8},{16,20},{20,16},{24,28},{28,24},{1,5},{5... | collective-permute-start | bytes 221192 | tf_op jit(solution)/shard_map/ppermute | solution.py:89
  8.3 6.4 %collective-permute-start.1 = (bf16[32,1152]{1,0:T(8,128)(2,1)S(1)}, bf16[32,1152]{1,0:T(8,128)(2,1)S(1)}, u32[]{:S(2)}, u32[]{:S(2)}) collective-permute-start(bf16[32,1152]{1,0:T(8,128)(2,1)S(1)} %get-tuple-element.16.refs_0_), channel_id=1, source_target_pairs={{0,8},{4,12},{8,0},{12,4},{16,24},{20,28},{24,16},{28,20},{1,9},{5... | collective-permute-start | bytes 221192 | tf_op jit(solution)/shard_map/ppermute | solution.py:89
  9.5 8.6 %collective-permute-start.6 = (bf16[32,1152]{1,0:T(8,128)(2,1)S(1)}, bf16[32,1152]{1,0:T(8,128)(2,1)S(1)}, u32[]{:S(2)}, u32[]{:S(2)}) collective-permute-start(bf16[32,1152]{1,0:T(8,128)(2,1)S(1)} %collective-permute-done.5.refs_3_.refs_6_), channel_id=1, source_target_pairs={{0,4},{4,0},{8,12},{12,8},{16,20},{20,16},{24,28},{28,24},{1,5},{5... | collective-permute-start | bytes 221192 | tf_op jit(solution)/shard_map/ppermute | solution.py:89
  13.1 4.9 %collective-permute-start.4 = (bf16[32,1152]{1,0:T(8,128)(2,1)S(1)}, bf16[32,1152]{1,0:T(8,128)(2,1)S(1)}, u32[]{:S(2)}, u32[]{:S(2)}) collective-permute-start(bf16[32,1152]{1,0:T(8,128)(2,1)S(1)} %collective-permute-done.3.refs_2_.refs_4_), channel_id=1, source_target_pairs={{0,4},{4,0},{8,12},{12,8},{16,20},{20,16},{24,28},{28,24},{1,5},{5... | collective-permute-start | bytes 221192 | tf_op jit(solution)/shard_map/ppermute | solution.py:89
  14.6 4.4 %collective-permute-start.2 = (bf16[32,1152]{1,0:T(8,128)(2,1)S(1)}, bf16[32,1152]{1,0:T(8,128)(2,1)S(1)}, u32[]{:S(2)}, u32[]{:S(2)}) collective-permute-start(bf16[32,1152]{1,0:T(8,128)(2,1)S(1)} %collective-permute-done.refs_1_.refs_0_), channel_id=1, source_target_pairs={{0,8},{4,12},{8,0},{12,4},{16,24},{20,28},{24,16},{28,20},{1,9},{5... | collective-permute-start | bytes 221192 | tf_op jit(solution)/shard_map/ppermute | solution.py:89
  18.0 2.8 %collective-permute-start.7 = (bf16[2,64,1024]{2,1,0:T(8,128)(2,1)S(1)}, bf16[2,64,1024]{2,1,0:T(8,128)(2,1)S(1)}, u32[]{:S(2)}, u32[]{:S(2)}) collective-permute-start(bf16[2,64,1024]{2,1,0:T(8,128)(2,1)S(1)} %get-tuple-element.19), channel_id=1, source_target_pairs={{0,1},{1,0},{2,3},{3,2},{4,5},{5,4},{6,7},{7,6},{8,9},{9,8},{10,11... | collective-permute-start | bytes 786440 | tf_op jit(solution)/shard_map/ppermute | solution.py:432
  20.8 1.5 %collective-permute-start.8 = (bf16[2,64,1024]{2,1,0:T(8,128)(2,1)S(1)}, bf16[2,64,1024]{2,1,0:T(8,128)(2,1)S(1)}, u32[]{:S(2)}, u32[]{:S(2)}) collective-permute-start(bf16[2,64,1024]{2,1,0:T(8,128)(2,1)S(1)} %get-tuple-element.23), channel_id=1, source_target_pairs={{0,1},{1,0},{2,3},{3,2},{4,5},{5,4},{6,7},{7,6},{8,9},{9,8},{10,11... | collective-permute-start | bytes 786440 | tf_op jit(solution)/shard_map/ppermute | solution.py:443
  22.5 12.7 %collective-permute-start.9 = (bf16[2,2,32,1024]{3,2,1,0:T(8,128)(2,1)S(1)}, bf16[2,2,32,1024]{3,2,1,0:T(8,128)(2,1)S(1)}, u32[]{:S(2)}, u32[]{:S(2)}) collective-permute-start(bf16[2,2,32,1024]{3,2,1,0:T(8,128)(2,1)S(1)} %get-tuple-element.25), channel_id=1, source_target_pairs={{0,2},{1,3},{2,0},{3,1},{4,6},{5,7},{6,4},{7,5},{8,10},{9,11},{10,... | collective-permute-start | bytes 786440 | tf_op jit(solution)/shard_map/ppermute | solution.py:456
  24.0 10.1 %all-to-all-start = ((f32[32,1,128]{2,1,0:T(1,128)}), f32[32,1,128]{2,1,0:T(1,128)S(1)}, u32[]{:S(2)}, u32[]{:S(2)}) async-start(f32[32,1,128]{2,1,0:T(1,128)} %bitcast.6), calls=%async_computation | async-start | bytes 32768 | tf_op jit(solution)/shard_map/all_to_all | solution.py:444

commit v4 on v3

--- a/solution.py
+++ b/solution.py
@@ -310,15 +310,20 @@
         copy.wait()
 
 
-def pair_kernel(mine_a, got_a, mine_b, got_b, keep_ref, send_ref):
+def pair_kernel(mine_ref, got_ref, keep_ref, send_ref):
     bit = lax.axis_index("ep") // 2
+    keep_ref[...] = mine_ref[bit].astype(jnp.float32) + got_ref[bit].astype(jnp.float32)
+    send_ref[...] = (
+        mine_ref[1 - bit].astype(jnp.float32) + got_ref[1 - bit].astype(jnp.float32)
+    ).astype(jnp.bfloat16)
+
+
+def last_kernel(mine_a, got_a, mine_b, got_b, out_ref):
     parity = lax.rem(lax.axis_index("grp"), 2)
-    shape = keep_ref.shape[:1] + keep_ref.shape[2:]
+    shape = out_ref.shape[:1] + out_ref.shape[2:]
     for at, mine, got in ((parity, mine_a, got_a), (1 - parity, mine_b, got_b)):
-        kept_sum = mine[bit].astype(jnp.float32) + got[bit].astype(jnp.float32)
-        sent_sum = mine[1 - bit].astype(jnp.float32) + got[1 - bit].astype(jnp.float32)
-        keep_ref[:, at] = kept_sum.reshape(shape)
-        send_ref[:, at] = sent_sum.astype(jnp.bfloat16).reshape(shape)
+        total = mine[...] + got[...].astype(jnp.float32)
+        out_ref[:, at] = total.astype(jnp.bfloat16).reshape(shape)
 
 
 def router_kernel(local, capacity, score_ref, meta_ref, w_ref, out_ref):
@@ -406,6 +411,19 @@
     saved_shape = (local, groups // 2, 2, capacity, width)
     sums = [kept((local, span // 4, width), bf16)] * 2
     work = slot_count * features * width
+    core_pairs = [(i, i ^ 1) for i in range(ep_count)]
+    chip_pairs = [(i, i ^ 2) for i in range(ep_count)]
+
+    def both_cores(keep, send):
+        got = lax.ppermute(send, "ep", core_pairs)
+        return pl.pallas_call(
+            pair_kernel,
+            out_shape=(kept((span // 4, width), f32), kept((span // 4, width), bf16)),
+            in_specs=[vmem] * 2,
+            out_specs=(vmem,) * 2,
+            compiler_params=limit(2),
+        )(held(keep), held(got))
+
     weights, saved, projection, keep_a, send_a, score_a = pl.pallas_call(
         functools.partial(first_kernel, local, groups, capacity),
         out_shape=(
@@ -427,9 +445,8 @@
         away_from_vmem(hidden_saved.reshape(saved_shape)),
         away_from_vmem(router_weight),
     )
-    core_pairs = [(i, i ^ 1) for i in range(ep_count)]
-    chip_pairs = [(i, i ^ 2) for i in range(ep_count)]
-    got_a = lax.ppermute(send_a, "ep", core_pairs)
+    mine_a, away_a = both_cores(keep_a, send_a)
+    last_a = lax.ppermute(away_a, "ep", chip_pairs)
 
     keep_b, send_b, score = pl.pallas_call(
         functools.partial(second_kernel, local, groups, capacity),
@@ -440,20 +457,11 @@
         cost_estimate=cost(work, 4 * 2**20),
         name="second",
     )(*blocks[1::2], held(weights), held(saved), held(score_a))
-    got_b = lax.ppermute(send_b, "ep", core_pairs)
+    mine_b, away_b = both_cores(keep_b, send_b)
     from_all = lax.all_to_all(
         score.reshape(groups * ep_count, 1, LANES), ("grp", "ep"), 0, 0, tiled=True
     )
-    order = (groups // 4, 2, capacity, width)
-    mine, away = pl.pallas_call(
-        pair_kernel,
-        out_shape=(kept(order, f32), kept(order, bf16)),
-        in_specs=[vmem] * 4,
-        out_specs=(vmem, vmem),
-        compiler_params=limit(2),
-        name="pair",
-    )(held(keep_a), held(got_a), held(keep_b), held(got_b))
-    last = lax.ppermute(away, "ep", chip_pairs)
+    last_b = lax.ppermute(away_b, "ep", chip_pairs)
 
     parts = 4
     weight_grad = pl.pallas_call(
@@ -472,7 +480,14 @@
         name="weight",
     )(*blocks, held(saved.reshape(local, span, width)))
 
-    hidden_grad = (mine + last.astype(f32)).astype(bf16).reshape(1, span // 2, width)
+    hidden_grad = pl.pallas_call(
+        last_kernel,
+        out_shape=struct((groups // 4, 2, capacity, width), bf16),
+        in_specs=[vmem] * 4,
+        out_specs=vmem,
+        compiler_params=limit(2),
+        name="last",
+    )(held(mine_a), held(last_a), held(mine_b), held(last_b)).reshape(1, span // 2, width)
 
     input_grad = pl.pallas_call(
         functools.partial(router_kernel, local, capacity),

time: 36.2 us -> 36.5 us (level)
  starting transfers between devices: 15.6 us -> 17.4 us
  waiting for transfers between devices: 8.86 us -> 7.34 us
  other arithmetic: 0.78 us -> 0 us
  Pallas kernels: 10.1 us -> 10.8 us
    ppermute x3 -> x4, waiting for transfers between devices: 1.53 us -> 0.01 us  [the longest x2 0.01 us: both_cores(): got = lax.ppermute(send, 'ep', core_pairs)]
    ppermute x3 -> x4, starting transfers between devices: 1.66 us -> 3.13 us  [the longest x1 1.59 us: token_plan(): last_a = lax.ppermute(away_a, 'ep', chip_pairs)]
    convert_element_type x1 -> x0, other arithmetic: 0.78 us -> none  [token_plan(): (mine + last.astype(f32)).astype(bf16).reshape(1, span // 2, width)]
    pallas_call x1 -> x3, Pallas kernels: 0.11 us -> 0.87 us  [the longest x1 0.75 us: token_plan(): pl.pallas_call(last_kernel, out_shape=struct((groups // 4, 2, capacity, w...]
    all_to_all x1, starting transfers between devices: 2.98 us -> 3.36 us  [token_plan(): lax.all_to_all(score.reshape(groups * ep_count, 1, LANES), ('grp', 'ep'),...]
  transfers between devices with their start and end apart: 11 -> 12, of which waited for: 5 -> 4; matrix products, arithmetic and copies ran while one was open for 0% -> 0% of each run, Pallas kernels for 25% -> 25%
where the time goes in v4:
time: 36.5 us; the launch traced here: 36.3 us
  starting transfers between devices  17.4 us (48%)
  Pallas kernels  10.8 us (30%)
  waiting for transfers between devices  7.34 us (20%)
  between operations  0.7 us (2%)
    ppermute x7, starting transfers between devices, exchange(): return lax.ppermute(x, 'grp', [(i, i ^ distance) for i in range(count)])  10.9 us
    all_to_all x1, waiting for transfers between devices, token_plan(): lax.all_to_all(score.reshape(groups * ep_count, 1, LANES), ('grp', 'ep'),...  4.27 us
    all_to_all x1, starting transfers between devices, token_plan(): lax.all_to_all(score.reshape(groups * ep_count, 1, LANES), ('grp', 'ep'),...  3.36 us
    pallas_call x1, Pallas kernels, token_plan(): pl.pallas_call(functools.partial(first_kernel, local, groups, capacity),...  3.22 us
    ppermute x7, waiting for transfers between devices, exchange(): return lax.ppermute(x, 'grp', [(i, i ^ distance) for i in range(count)])  3.06 us
    pallas_call x1, Pallas kernels, token_plan(): pl.pallas_call(functools.partial(weight_kernel, local, groups, capacity,...  2.82 us
    pallas_call x1, Pallas kernels, token_plan(): pl.pallas_call(functools.partial(second_kernel, local, groups, capacity),...  1.81 us
    ppermute x1, starting transfers between devices, token_plan(): last_a = lax.ppermute(away_a, 'ep', chip_pairs)  1.59 us
  transfers between devices with their start and end apart: 12, of which 4 were waited for; matrix products, arithmetic and copies ran while one was open for 0% of the time, Pallas kernels for 25%

profile of v4, /device:TPU:0, one launch (start us, length us, event | category | flops | bytes accessed | tf_op | source)
XLA Modules:
  0.0 36.3 jit_solution(1433343191428207181)
XLA Ops:
  0.6 1.0 %pack.1 = (bf16[32,1152]{1,0:T(8,128)(2,1)S(1)}, f32[2,3,8,128]{3,2,1,0:T(8,128)S(1)}) custom-call(s32[8,32]{1,0:T(8,128)} %bitcast.14, f32[16,32]{1,0:T(8,128)} %bitcast.13, bf16[32,1024]{1,0:T(8,128)(2,1)} %rows_hbm.1), custom_call_target="tpu_custom_call" | custom-call | tf_op jit(solution)/shard_map/pack/pallas_call | solution.py:393
  1.7 5.1 %collective-permute-start.5 = (bf16[32,1152]{1,0:T(8,128)(2,1)S(1)}, bf16[32,1152]{1,0:T(8,128)(2,1)S(1)}, u32[]{:S(2)}, u32[]{:S(2)}) collective-permute-start(bf16[32,1152]{1,0:T(8,128)(2,1)S(1)} %get-tuple-element.18.refs_0_), channel_id=1, source_target_pairs={{0,24},{4,28},{8,16},{12,20},{16,8},{20,12},{24,0},{28,4},{1,25},{... | collective-permute-start | bytes 221192 | tf_op jit(solution)/shard_map/ppermute | solution.py:89
  6.8 0.0 collective-permute-start.3
  6.8 1.5 %collective-permute-start = (bf16[32,1152]{1,0:T(8,128)(2,1)S(1)}, bf16[32,1152]{1,0:T(8,128)(2,1)S(1)}, u32[]{:S(2)}, u32[]{:S(2)}) collective-permute-start(bf16[32,1152]{1,0:T(8,128)(2,1)S(1)} %get-tuple-element.18.refs_0_), channel_id=1, source_target_pairs={{0,4},{4,0},{8,12},{12,8},{16,20},{20,16},{24,28},{28,24},{1,5},{5... | collective-permute-start | bytes 221192 | tf_op jit(solution)/shard_map/ppermute | solution.py:89
  8.3 0.8 %collective-permute-start.1 = (bf16[32,1152]{1,0:T(8,128)(2,1)S(1)}, bf16[32,1152]{1,0:T(8,128)(2,1)S(1)}, u32[]{:S(2)}, u32[]{:S(2)}) collective-permute-start(bf16[32,1152]{1,0:T(8,128)(2,1)S(1)} %get-tuple-element.18.refs_0_), channel_id=1, source_target_pairs={{0,8},{4,12},{8,0},{12,4},{16,24},{20,28},{24,16},{28,20},{1,9},{5... | collective-permute-start | bytes 221192 | tf_op jit(solution)/shard_map/ppermute | solution.py:89
  9.1 0.4 %collective-permute-done.5.refs_3_.refs_6_ = bf16[32,1152]{1,0:T(8,128)(2,1)S(1)} collective-permute-done((bf16[32,1152]{1,0:T(8,128)(2,1)S(1)}, bf16[32,1152]{1,0:T(8,128)(2,1)S(1)}, u32[]{:S(2)}, u32[]{:S(2)}) %collective-permute-start.5) | collective-permute-done | bytes 73760 | tf_op jit(solution)/shard_map/ppermute | solution.py:89
  9.5 1.9 %collective-permute-start.6 = (bf16[32,1152]{1,0:T(8,128)(2,1)S(1)}, bf16[32,1152]{1,0:T(8,128)(2,1)S(1)}, u32[]{:S(2)}, u32[]{:S(2)}) collective-permute-start(bf16[32,1152]{1,0:T(8,128)(2,1)S(1)} %collective-permute-done.5.refs_3_.refs_6_), channel_id=1, source_target_pairs={{0,4},{4,0},{8,12},{12,8},{16,20},{20,16},{24,28},{28,24},{1,5},{5... | collective-permute-start | bytes 221192 | tf_op jit(solution)/shard_map/ppermute | solution.py:89
  11.4 1.8 %collective-permute-done.3.refs_2_.refs_4_ = bf16[32,1152]{1,0:T(8,128)(2,1)S(1)} collective-permute-done((bf16[32,1152]{1,0:T(8,128)(2,1)S(1)}, bf16[32,1152]{1,0:T(8,128)(2,1)S(1)}, u32[]{:S(2)}, u32[]{:S(2)}) %collective-permute-start.3) | collective-permute-done | bytes 73760 | tf_op jit(solution)/shard_map/ppermute | solution.py:89
  13.1 1.5 %collective-permute-start.4 = (bf16[32,1152]{1,0:T(8,128)(2,1)S(1)}, bf16[32,1152]{1,0:T(8,128)(2,1)S(1)}, u32[]{:S(2)}, u32[]{:S(2)}) collective-permute-start(bf16[32,1152]{1,0:T(8,128)(2,1)S(1)} %collective-permute-done.3.refs_2_.refs_4_), channel_id=1, source_target_pairs={{0,4},{4,0},{8,12},{12,8},{16,20},{20,16},{24,28},{28,24},{1,5},{5... | collective-permute-start | bytes 221192 | tf_op jit(solution)/shard_map/ppermute | solution.py:89
  14.6 0.0 collective-permute-done.refs_1_.refs_0_
  14.6 0.1 collective-permute-start.2
  14.8 0.0 collective-permute-done.1.refs_1_.refs_2_
  14.8 3.2 %first.1 = (bf16[2,1024,1024]{2,1,0:T(8,128)(2,1)S(1)}, bf16[2,4,2,32,1024]{4,3,2,1,0:T(8,128)(2,1)S(1)}, bf16[16,1024]{1,0:T(8,128)(2,1)S(1)}, bf16[2,64,1024]{...) custom-call(bf16[32,1152]{1,0:T(8,128)(2,1)S(1)} %get-tuple-element.18.refs_0_, ...), custom_call_target="tpu_custom_call" | custom-call | flops 536870912 | bytes 8388608 | tf_op jit(solution)/shard_map/first/pallas_call | solution.py:427
  18.0 0.1 collective-permute-start.7
  18.1 0.0 collective-permute-done.6.refs_7_.refs_3_
  18.1 0.0 collective-permute-done.4.refs_5_.refs_2_
  18.1 0.9 %collective-permute-done.2.refs_3_.refs_1_ = bf16[32,1152]{1,0:T(8,128)(2,1)S(1)} collective-permute-done((bf16[32,1152]{1,0:T(8,128)(2,1)S(1)}, bf16[32,1152]{1,0:T(8,128)(2,1)S(1)}, u32[]{:S(2)}, u32[]{:S(2)}) %collective-permute-start.2) | collective-permute-done | bytes 73760 | tf_op jit(solution)/shard_map/ppermute | solution.py:89
  19.0 1.8 %second.1 = (bf16[2,64,1024]{2,1,0:T(8,128)(2,1)S(1)}, bf16[2,64,1024]{2,1,0:T(8,128)(2,1)S(1)}, f32[4,2,4,128]{3,2,1,0:T(4,128)}) custom-call(bf16[32,1152]{1,0:T(8,128)(2,1)S(1)} %collective-permute-done.refs_1_.refs_0_, bf16[32,1152]{1,0:T(8,128)(2,1)S(1)} %collective-permute-done.2.refs_3_.refs_1_, ...), custom_call_target="tpu_custom_call" | custom-call | flops 536870912 | bytes 4194304 | tf_op jit(solution)/shard_map/second/pallas_call | solution.py:451
  20.8 0.0 collective-permute-start.9
  20.8 0.0 collective-permute-done.7.got_ref
  20.8 0.1 shard_map.85
  20.9 1.6 %collective-permute-start.8 = (bf16[64,1024]{1,0:T(8,128)(2,1)S(1)}, bf16[64,1024]{1,0:T(8,128)(2,1)S(1)}, u32[]{:S(2)}, u32[]{:S(2)}) collective-permute-start(bf16[64,1024]{1,0:T(8,128)(2,1)S(1)} %get-tuple-element.23), channel_id=1, source_target_pairs={{0,2},{1,3},{2,0},{3,1},{4,6},{5,7},{6,4},{7,5},{8,10},{9,11},{10,... | collective-permute-start | bytes 393224 | tf_op jit(solution)/shard_map/ppermute | solution.py:449
  22.5 0.0 collective-permute-done.9.got_ref
  22.5 0.1 shard_map.86
  22.5 1.5 %collective-permute-start.10 = (bf16[64,1024]{1,0:T(8,128)(2,1)S(1)}, bf16[64,1024]{1,0:T(8,128)(2,1)S(1)}, u32[]{:S(2)}, u32[]{:S(2)}) collective-permute-start(bf16[64,1024]{1,0:T(8,128)(2,1)S(1)} %get-tuple-element.29), channel_id=1, source_target_pairs={{0,2},{1,3},{2,0},{3,1},{4,6},{5,7},{6,4},{7,5},{8,10},{9,11},{10,... | collective-permute-start | bytes 393224 | tf_op jit(solution)/shard_map/ppermute | solution.py:464
  24.0 3.4 %all-to-all-start = ((f32[32,1,128]{2,1,0:T(1,128)}), f32[32,1,128]{2,1,0:T(1,128)S(1)}, u32[]{:S(2)}, u32[]{:S(2)}) async-start(f32[32,1,128]{2,1,0:T(1,128)} %bitcast.6), calls=%async_computation | async-start | bytes 32768 | tf_op jit(solution)/shard_map/all_to_all | solution.py:461
  27.4 2.8 %weight.1 = bf16[2,1024,1024]{2,1,0:T(8,128)(2,1)} custom-call(bf16[32,1152]{1,0:T(8,128)(2,1)S(1)} %get-tuple-element.18.refs_0_, bf16[32,1152]{1,0:T(8,128)(2,1)S(1)} %collective-permute-done.refs_1_.refs_0_, bf16[32,1152]{1,0:T(8,128)(2,1)S(1)} %collective-permute-done.1.refs_1_.refs_2_, bf16[32,1152]{1,0:T(8,128)(2,1)S(1)} %collective-permute-done.2.refs_3_.refs_1_, ...), custom_call_target="tpu_custom_call" | custom-call | flops 1073741824 | bytes 6291456 | tf_op jit(solution)/shard_map/weight/pallas_call | solution.py:467
  30.2 4.3 %all-to-all-done = f32[32,1,128]{2,1,0:T(1,128)S(1)} async-done(((f32[32,1,128]{2,1,0:T(1,128)}), f32[32,1,128]{2,1,0:T(1,128)S(1)}, u32[]{:S(2)}, u32[]{:S(2)}) %all-to-all-start) | async-done | bytes 16416 | tf_op jit(solution)/shard_map/all_to_all | solution.py:461
  34.5 1.0 %router.1 = bf16[32,1024]{1,0:T(8,128)(2,1)} custom-call(f32[8,4,128]{2,1,0:T(4,128)S(1)} %bitcast.10, f32[2,3,8,128]{3,2,1,0:T(8,128)S(1)} %get-tuple-element.31.meta_ref, bf16[16,1024]{1,0:T(8,128)(2,1)S(1)} %get-tuple-element.32.w_ref), custom_call_target="tpu_custom_call" | custom-call | tf_op jit(solution)/shard_map/router/pallas_call | solution.py:492
  35.5 0.0 collective-permute-done.8.got_a
  35.5 0.0 collective-permute-done.10.got_b
  35.5 0.7 %last.1 = bf16[2,2,32,1024]{3,2,1,0:T(8,128)(2,1)} custom-call(f32[64,1024]{1,0:T(8,128)S(1)} %get-tuple-element.22.mine_a, bf16[64,1024]{1,0:T(8,128)(2,1)S(1)} %collective-permute-done.8.got_a, f32[64,1024]{1,0:T(8,128)S(1)} %get-tuple-element.28.mine_b, bf16[64,1024]{1,0:T(8,128)(2,1)S(1)} %collective-permute-done.10.got_b), custom_call_target="tpu_custom_call" | custom-call | tf_op jit(solution)/shard_map/last/pallas_call | solution.py:483
Async XLA Ops:
  1.7 7.8 %collective-permute-start.5 = (bf16[32,1152]{1,0:T(8,128)(2,1)S(1)}, bf16[32,1152]{1,0:T(8,128)(2,1)S(1)}, u32[]{:S(2)}, u32[]{:S(2)}) collective-permute-start(bf16[32,1152]{1,0:T(8,128)(2,1)S(1)} %get-tuple-element.18.refs_0_), channel_id=1, source_target_pairs={{0,24},{4,28},{8,16},{12,20},{16,8},{20,12},{24,0},{28,4},{1,25},{... | collective-permute-start | bytes 221192 | tf_op jit(solution)/shard_map/ppermute | solution.py:89
  6.8 6.3 %collective-permute-start.3 = (bf16[32,1152]{1,0:T(8,128)(2,1)S(1)}, bf16[32,1152]{1,0:T(8,128)(2,1)S(1)}, u32[]{:S(2)}, u32[]{:S(2)}) collective-permute-start(bf16[32,1152]{1,0:T(8,128)(2,1)S(1)} %get-tuple-element.18.refs_0_), channel_id=1, source_target_pairs={{0,16},{4,20},{8,24},{12,28},{16,0},{20,4},{24,8},{28,12},{1,17},{... | collective-permute-start | bytes 221192 | tf_op jit(solution)/shard_map/ppermute | solution.py:89
  6.8 7.8 %collective-permute-start = (bf16[32,1152]{1,0:T(8,128)(2,1)S(1)}, bf16[32,1152]{1,0:T(8,128)(2,1)S(1)}, u32[]{:S(2)}, u32[]{:S(2)}) collective-permute-start(bf16[32,1152]{1,0:T(8,128)(2,1)S(1)} %get-tuple-element.18.refs_0_), channel_id=1, source_target_pairs={{0,4},{4,0},{8,12},{12,8},{16,20},{20,16},{24,28},{28,24},{1,5},{5... | collective-permute-start | bytes 221192 | tf_op jit(solution)/shard_map/ppermute | solution.py:89
  8.3 6.4 %collective-permute-start.1 = (bf16[32,1152]{1,0:T(8,128)(2,1)S(1)}, bf16[32,1152]{1,0:T(8,128)(2,1)S(1)}, u32[]{:S(2)}, u32[]{:S(2)}) collective-permute-start(bf16[32,1152]{1,0:T(8,128)(2,1)S(1)} %get-tuple-element.18.refs_0_), channel_id=1, source_target_pairs={{0,8},{4,12},{8,0},{12,4},{16,24},{20,28},{24,16},{28,20},{1,9},{5... | collective-permute-start | bytes 221192 | tf_op jit(solution)/shard_map/ppermute | solution.py:89
  9.5 8.6 %collective-permute-start.6 = (bf16[32,1152]{1,0:T(8,128)(2,1)S(1)}, bf16[32,1152]{1,0:T(8,128)(2,1)S(1)}, u32[]{:S(2)}, u32[]{:S(2)}) collective-permute-start(bf16[32,1152]{1,0:T(8,128)(2,1)S(1)} %collective-permute-done.5.refs_3_.refs_6_), channel_id=1, source_target_pairs={{0,4},{4,0},{8,12},{12,8},{16,20},{20,16},{24,28},{28,24},{1,5},{5... | collective-permute-start | bytes 221192 | tf_op jit(solution)/shard_map/ppermute | solution.py:89
  13.1 4.9 %collective-permute-start.4 = (bf16[32,1152]{1,0:T(8,128)(2,1)S(1)}, bf16[32,1152]{1,0:T(8,128)(2,1)S(1)}, u32[]{:S(2)}, u32[]{:S(2)}) collective-permute-start(bf16[32,1152]{1,0:T(8,128)(2,1)S(1)} %collective-permute-done.3.refs_2_.refs_4_), channel_id=1, source_target_pairs={{0,4},{4,0},{8,12},{12,8},{16,20},{20,16},{24,28},{28,24},{1,5},{5... | collective-permute-start | bytes 221192 | tf_op jit(solution)/shard_map/ppermute | solution.py:89
  14.6 4.4 %collective-permute-start.2 = (bf16[32,1152]{1,0:T(8,128)(2,1)S(1)}, bf16[32,1152]{1,0:T(8,128)(2,1)S(1)}, u32[]{:S(2)}, u32[]{:S(2)}) collective-permute-start(bf16[32,1152]{1,0:T(8,128)(2,1)S(1)} %collective-permute-done.refs_1_.refs_0_), channel_id=1, source_target_pairs={{0,8},{4,12},{8,0},{12,4},{16,24},{20,28},{24,16},{28,20},{1,9},{5... | collective-permute-start | bytes 221192 | tf_op jit(solution)/shard_map/ppermute | solution.py:89
  18.0 2.8 %collective-permute-start.7 = (bf16[2,64,1024]{2,1,0:T(8,128)(2,1)S(1)}, bf16[2,64,1024]{2,1,0:T(8,128)(2,1)S(1)}, u32[]{:S(2)}, u32[]{:S(2)}) collective-permute-start(bf16[2,64,1024]{2,1,0:T(8,128)(2,1)S(1)} %get-tuple-element.21), channel_id=1, source_target_pairs={{0,1},{1,0},{2,3},{3,2},{4,5},{5,4},{6,7},{7,6},{8,9},{9,8},{10,11... | collective-permute-start | bytes 786440 | tf_op jit(solution)/shard_map/ppermute | solution.py:418
  20.8 1.7 %collective-permute-start.9 = (bf16[2,64,1024]{2,1,0:T(8,128)(2,1)S(1)}, bf16[2,64,1024]{2,1,0:T(8,128)(2,1)S(1)}, u32[]{:S(2)}, u32[]{:S(2)}) collective-permute-start(bf16[2,64,1024]{2,1,0:T(8,128)(2,1)S(1)} %get-tuple-element.27), channel_id=1, source_target_pairs={{0,1},{1,0},{2,3},{3,2},{4,5},{5,4},{6,7},{7,6},{8,9},{9,8},{10,11... | collective-permute-start | bytes 786440 | tf_op jit(solution)/shard_map/ppermute | solution.py:418
  20.9 14.6 %collective-permute-start.8 = (bf16[64,1024]{1,0:T(8,128)(2,1)S(1)}, bf16[64,1024]{1,0:T(8,128)(2,1)S(1)}, u32[]{:S(2)}, u32[]{:S(2)}) collective-permute-start(bf16[64,1024]{1,0:T(8,128)(2,1)S(1)} %get-tuple-element.23), channel_id=1, source_target_pairs={{0,2},{1,3},{2,0},{3,1},{4,6},{5,7},{6,4},{7,5},{8,10},{9,11},{10,... | collective-permute-start | bytes 393224 | tf_op jit(solution)/shard_map/ppermute | solution.py:449
  22.5 13.0 %collective-permute-start.10 = (bf16[64,1024]{1,0:T(8,128)(2,1)S(1)}, bf16[64,1024]{1,0:T(8,128)(2,1)S(1)}, u32[]{:S(2)}, u32[]{:S(2)}) collective-permute-start(bf16[64,1024]{1,0:T(8,128)(2,1)S(1)} %get-tuple-element.29), channel_id=1, source_target_pairs={{0,2},{1,3},{2,0},{3,1},{4,6},{5,7},{6,4},{7,5},{8,10},{9,11},{10,... | collective-permute-start | bytes 393224 | tf_op jit(solution)/shard_map/ppermute | solution.py:464
  24.0 10.5 %all-to-all-start = ((f32[32,1,128]{2,1,0:T(1,128)}), f32[32,1,128]{2,1,0:T(1,128)S(1)}, u32[]{:S(2)}, u32[]{:S(2)}) async-start(f32[32,1,128]{2,1,0:T(1,128)} %bitcast.6), calls=%async_computation | async-start | bytes 32768 | tf_op jit(solution)/shard_map/all_to_all | solution.py:461

commit v5 on v4

--- a/solution.py
+++ b/solution.py
@@ -91,7 +91,7 @@
 
 def swap_order(count):
     top, rest = count - 2, list(range(2, count - 2, 2))
-    return [top, 1] + rest + [top ^ 1, 3] + [d ^ 1 for d in rest if d != 2]
+    return [top, 1] + rest + [3, top ^ 1] + [d ^ 1 for d in rest if d != 2]
 
 
 def gather_blocks(x):
@@ -155,10 +155,10 @@
     copies[2].wait()
 
 
-def half_of(parity, local, groups, capacity, blocks, saved_ref, weight, outs):
-    keep_ref, send_ref = outs
+def half_of(parity, experts, groups, capacity, blocks, saved_ref, w_ref, store):
+    local = len(experts)
     block_rows, features = blocks[0].shape[0], blocks[0].shape[1] - LANES
-    width = keep_ref.shape[2]
+    width = w_ref.shape[2]
     count = groups // 2
     span, tokens = count * capacity, count * block_rows
     cols = 256 if width % 256 == 0 else LANES
@@ -172,21 +172,28 @@
     away = pl.ds((1 - side) * (count // 2), count // 2)
     part_row, part_lane = iota((span, LANES), 0), iota((span, LANES), 1)
     sent = jnp.zeros((count, LANES), jnp.float32)
-    for l in range(local):
+    row = iota(aux.shape, 0)
+    picks, scales = [], []
+    for l in experts:
         lane = l * groups + own
-        row = iota(aux.shape, 0)
         prob = jnp.sum(jnp.where(row == lane, aux, 0.0), axis=0, keepdims=True)
         rank = jnp.sum(jnp.where(row == local * groups + lane, aux, 0.0), axis=0, keepdims=True)
         place = jnp.where(rank > 0, source * capacity + rank.astype(jnp.int32) - 1, -1)
         pick = slot == place
-        scale = jnp.sum(jnp.where(pick, prob, 0.0), axis=1, keepdims=True)
-        grads = jnp.dot(
-            pick.astype(jnp.float32).astype(jnp.bfloat16), rows, preferred_element_type=jnp.float32
-        ).astype(jnp.bfloat16)
+        picks.append(pick.astype(jnp.float32).astype(jnp.bfloat16))
+        scales.append(jnp.sum(jnp.where(pick, prob, 0.0), axis=1, keepdims=True))
+    grads = jnp.dot(
+        jnp.concatenate(picks, axis=0), rows, preferred_element_type=jnp.float32
+    ).astype(jnp.bfloat16)
+    for i, l in enumerate(experts):
         score = jnp.zeros((span, LANES), jnp.float32)
         for n in range(width // cols):
             part = pl.ds(n * cols, cols)
-            term = jnp.dot(grads, weight(l, n, cols), preferred_element_type=jnp.float32)
+            term = jnp.dot(
+                grads[i * span : (i + 1) * span],
+                w_ref[l, :, part],
+                preferred_element_type=jnp.float32,
+            )
             saved = jnp.concatenate(
                 [
                     saved_ref[l, where, parity, :, part].reshape(span // 2, cols)
@@ -197,9 +204,7 @@
             product = term * saved.astype(jnp.float32)
             for k in range(cols // LANES):
                 score = score + product[:, k * LANES : (k + 1) * LANES]
-            out = (term * scale).astype(jnp.bfloat16)
-            keep_ref[l, :, part] = out[: span // 2]
-            send_ref[l, :, part] = out[span // 2 :]
+            store(i, part, (term * scales[i]).astype(jnp.bfloat16))
         score = jnp.sum(score, axis=1, keepdims=True)
         spread = jnp.where(lax.rem(part_row, capacity) + l * capacity == part_lane, score, 0.0)
         sent = sent + jnp.sum(spread.reshape(count, capacity, LANES), axis=1)
@@ -207,49 +212,37 @@
     return jnp.where(side == 0, sent, turned)
 
 
-def first_kernel(local, groups, capacity, *refs):
+def load_kernel(cue_ref, *refs):
+    sources, targets, sems = refs[:3], refs[3:6], refs[6]
+    copies = [
+        pltpu.make_async_copy(source, target, sems.at[i])
+        for i, (source, target) in enumerate(zip(sources, targets))
+    ]
+    for copy in copies:
+        copy.start()
+    for copy in copies:
+        copy.wait()
+
+
+def first_kernel(groups, capacity, *refs):
     count = groups // 2
-    blocks, sources = refs[:count], refs[count : count + 3]
-    w_ref, h_ref, r_ref, keep_ref, send_ref, score_ref, w_sems, sems = refs[count + 3 :]
-    cols = w_ref.shape[2] // w_sems.shape[1]
-
-    def fetch(l, n):
-        part = pl.ds(n * cols, cols)
-        return pltpu.make_async_copy(
-            sources[0].at[l, :, part], w_ref.at[l, :, part], w_sems.at[l, n]
-        )
-
-    others = [
-        pltpu.make_async_copy(sources[1], h_ref, sems.at[0]),
-        pltpu.make_async_copy(sources[2], r_ref, sems.at[1]),
-    ]
-    fetch(0, 0).start()
-    others[0].start()
-    for i in range(1, local * w_sems.shape[1]):
-        fetch(i // w_sems.shape[1], i % w_sems.shape[1]).start()
-    others[1].start()
-    waited = set()
-
-    def weight(l, n, size):
-        piece = n * size // cols
-        if (l, piece) not in waited:
-            fetch(l, piece).wait()
-            if not waited:
-                others[0].wait()
-            waited.add((l, piece))
-        return w_ref[l, :, pl.ds(n * size, size)]
+    blocks = refs[:count]
+    w_ref, h_ref, keep_ref, send_ref, score_ref = refs[count:]
+    bit = lax.axis_index("ep") // 2
+
+    def store(i, part, value):
+        (send_ref, keep_ref)[i][:, part] = value
 
     score_ref[...] = half_of(
         lax.rem(lax.axis_index("grp"), 2),
-        local,
+        (1 - bit, bit),
         groups,
         capacity,
         blocks,
         h_ref,
-        weight,
-        (keep_ref, send_ref),
-    )
-    others[1].wait()
+        w_ref,
+        store,
+    )
 
 
 def second_kernel(local, groups, capacity, *refs):
@@ -257,12 +250,14 @@
     blocks = refs[:count]
     w_ref, h_ref, other_ref, keep_ref, send_ref, score_ref = refs[count:]
     parity = 1 - lax.rem(lax.axis_index("grp"), 2)
-
-    def weight(l, n, size):
-        return w_ref[l, :, pl.ds(n * size, size)]
+    rows = keep_ref.shape[1]
+
+    def store(l, part, value):
+        keep_ref[l, :, part] = value[:rows]
+        send_ref[l, :, part] = value[rows:]
 
     mine = half_of(
-        parity, local, groups, capacity, blocks, h_ref, weight, (keep_ref, send_ref)
+        parity, tuple(range(local)), groups, capacity, blocks, h_ref, w_ref, store
     )
     other = other_ref[...]
     for x in range(2):
@@ -274,7 +269,13 @@
 
 def weight_kernel(local, groups, capacity, parts, *refs):
     blocks = refs[:groups]
-    h_ref, out_hbm, turned_buf, scaled_buf, out_buf, sems = refs[groups:]
+    h_ref, r_ref, out_hbm, sorted_ref, turned_buf, scaled_buf, out_buf, sems = refs[groups:]
+    experts = r_ref.shape[0]
+    at = iota((experts, experts), 0)
+    order = lax.rem(at, groups) * local + at // groups == iota((experts, experts), 1)
+    sorted_ref[...] = jnp.dot(
+        order.astype(jnp.float32).astype(jnp.bfloat16), r_ref[...], preferred_element_type=jnp.float32
+    ).astype(jnp.bfloat16)
     features = turned_buf.shape[0]
     tile = features // parts
     block_rows = blocks[0].shape[0]
@@ -318,6 +319,13 @@
     ).astype(jnp.bfloat16)
 
 
+def split_kernel(mine_ref, got_ref, keep_ref, send_ref):
+    rows = keep_ref.shape[0]
+    total = mine_ref[...].astype(jnp.float32) + got_ref[...].astype(jnp.float32)
+    keep_ref[...] = total[:rows]
+    send_ref[...] = total[rows:].astype(jnp.bfloat16)
+
+
 def last_kernel(mine_a, got_a, mine_b, got_b, out_ref):
     parity = lax.rem(lax.axis_index("grp"), 2)
     shape = out_ref.shape[:1] + out_ref.shape[2:]
@@ -327,7 +335,7 @@
 
 
 def router_kernel(local, capacity, score_ref, meta_ref, w_ref, out_ref):
-    groups, tokens = meta_ref.shape[2], out_ref.shape[0]
+    tokens = out_ref.shape[0]
     found = jnp.sum(score_ref[...], axis=1)
     scores = []
     for l in range(local):
@@ -345,14 +353,7 @@
         ],
         axis=0,
     ).astype(jnp.bfloat16)
-    count = local * groups
-    row = iota((count, count), 0)
-    expert = lax.rem(row, groups) * local + row // groups
-    order = (expert == iota((count, count), 1)).astype(jnp.bfloat16)
-    turned = contract_rows(grads, order)[:tokens].astype(jnp.bfloat16)
-    out_ref[...] = jnp.dot(turned, w_ref[...], preferred_element_type=jnp.float32).astype(
-        jnp.bfloat16
-    )
+    out_ref[...] = contract_rows(grads, w_ref[...])[:tokens].astype(jnp.bfloat16)
 
 
 def cost(flops, nbytes):
@@ -411,42 +412,52 @@
     saved_shape = (local, groups // 2, 2, capacity, width)
     sums = [kept((local, span // 4, width), bf16)] * 2
     work = slot_count * features * width
+    weights, saved, projection = pl.pallas_call(
+        load_kernel,
+        out_shape=(
+            kept(expert_weight.shape, bf16),
+            kept(saved_shape, bf16),
+            kept(router_weight.shape, bf16),
+        ),
+        in_specs=[vmem] + [hbm] * 3,
+        out_specs=(vmem,) * 3,
+        scratch_shapes=[pltpu.SemaphoreType.DMA((3,))],
+        compiler_params=limit(2),
+        cost_estimate=cost(work // 2, 8 * 2**20),
+        name="load",
+    )(
+        blocks[0],
+        away_from_vmem(expert_weight),
+        away_from_vmem(hidden_saved.reshape(saved_shape)),
+        away_from_vmem(router_weight),
+    )
+
     core_pairs = [(i, i ^ 1) for i in range(ep_count)]
     chip_pairs = [(i, i ^ 2) for i in range(ep_count)]
 
-    def both_cores(keep, send):
-        got = lax.ppermute(send, "ep", core_pairs)
+    def summed(kernel, keep, got):
         return pl.pallas_call(
-            pair_kernel,
+            kernel,
             out_shape=(kept((span // 4, width), f32), kept((span // 4, width), bf16)),
             in_specs=[vmem] * 2,
             out_specs=(vmem,) * 2,
             compiler_params=limit(2),
         )(held(keep), held(got))
 
-    weights, saved, projection, keep_a, send_a, score_a = pl.pallas_call(
-        functools.partial(first_kernel, local, groups, capacity),
+    keep_a, send_a, score_a = pl.pallas_call(
+        functools.partial(first_kernel, groups, capacity),
         out_shape=(
-            kept(expert_weight.shape, bf16),
-            kept(saved_shape, bf16),
-            kept(router_weight.shape, bf16),
-            *sums,
+            kept((span // 2, width), bf16),
+            kept((span // 2, width), bf16),
             kept((groups // 2, LANES), f32),
         ),
-        in_specs=[vmem] * (groups // 2) + [hbm] * 3,
-        out_specs=(vmem,) * 6,
-        scratch_shapes=[pltpu.SemaphoreType.DMA((local, 1)), pltpu.SemaphoreType.DMA((2,))],
+        in_specs=[vmem] * (groups // 2 + 2),
+        out_specs=(vmem,) * 3,
         compiler_params=limit(8),
-        cost_estimate=cost(work, 8 * 2**20),
+        cost_estimate=cost(work, 4 * 2**20),
         name="first",
-    )(
-        *blocks[0::2],
-        away_from_vmem(expert_weight),
-        away_from_vmem(hidden_saved.reshape(saved_shape)),
-        away_from_vmem(router_weight),
-    )
-    mine_a, away_a = both_cores(keep_a, send_a)
-    last_a = lax.ppermute(away_a, "ep", chip_pairs)
+    )(*blocks[0::2], held(weights), held(saved))
+    got_a = lax.ppermute(send_a, "ep", chip_pairs)
 
     keep_b, send_b, score = pl.pallas_call(
         functools.partial(second_kernel, local, groups, capacity),
@@ -457,18 +468,21 @@
         cost_estimate=cost(work, 4 * 2**20),
         name="second",
     )(*blocks[1::2], held(weights), held(saved), held(score_a))
-    mine_b, away_b = both_cores(keep_b, send_b)
+    got_b = lax.ppermute(send_b, "ep", core_pairs)
     from_all = lax.all_to_all(
         score.reshape(groups * ep_count, 1, LANES), ("grp", "ep"), 0, 0, tiled=True
     )
+    mine_b, away_b = summed(pair_kernel, keep_b, got_b)
     last_b = lax.ppermute(away_b, "ep", chip_pairs)
+    mine_a, away_a = summed(split_kernel, keep_a, got_a)
+    last_a = lax.ppermute(away_a, "ep", core_pairs)
 
     parts = 4
-    weight_grad = pl.pallas_call(
+    weight_grad, projection = pl.pallas_call(
         functools.partial(weight_kernel, local, groups, capacity, parts),
-        out_shape=struct((local, features, width), bf16),
-        in_specs=[vmem] * (groups + 1),
-        out_specs=hbm,
+        out_shape=(struct((local, features, width), bf16), kept(router_weight.shape, bf16)),
+        in_specs=[vmem] * (groups + 2),
+        out_specs=(hbm, vmem),
         scratch_shapes=[
             pltpu.VMEM((features, tokens), bf16),
             pltpu.VMEM((features, span), bf16),
@@ -478,7 +492,7 @@
         compiler_params=limit(12),
         cost_estimate=cost(2 * slot_count * features * width, 6 * 2**20),
         name="weight",
-    )(*blocks, held(saved.reshape(local, span, width)))
+    )(*blocks, held(saved.reshape(local, span, width)), held(projection))
 
     hidden_grad = pl.pallas_call(
         last_kernel,

time: 36.5 us -> 39.4 us (1.079)
  waiting for transfers between devices: 7.34 us -> 10.6 us
  starting transfers between devices: 17.4 us -> 16.8 us
    ppermute x3, waiting for transfers between devices: 0.01 us -> 4.21 us  [the longest x1 4.2 us: token_plan(): got_a = lax.ppermute(send_a, 'ep', chip_pairs)]
    ppermute x7, waiting for transfers between devices: 3.06 us -> 2.16 us  [exchange(): return lax.ppermute(x, 'grp', [(i, i ^ distance) for i in range(count)])]
    all_to_all x1, starting transfers between devices: 3.36 us -> 2.78 us  [token_plan(): lax.all_to_all(score.reshape(groups * ep_count, 1, LANES), ('grp', 'ep'),...]
    pallas_call x3 -> x4, Pallas kernels: 3.34 us -> 3.74 us  [the longest x1 2.51 us: token_plan(): pl.pallas_call(load_kernel, out_shape=(kept(expert_weight.shape, bf16), k...]
  transfers between devices with their start and end apart: 12 -> 12, of which waited for: 4 -> 4; matrix products, arithmetic and copies ran while one was open for 0% -> 0% of each run, Pallas kernels for 25% -> 24%
where the time goes in v5:
time: 39.4 us; the launch traced here: 39.2 us
  starting transfers between devices  16.8 us (43%)
  Pallas kernels  11 us (28%)
  waiting for transfers between devices  10.6 us (27%)
  between operations  0.72 us (2%)
    ppermute x7, starting transfers between devices, exchange(): return lax.ppermute(x, 'grp', [(i, i ^ distance) for i in range(count)])  10.9 us
    all_to_all x1, waiting for transfers between devices, token_plan(): lax.all_to_all(score.reshape(groups * ep_count, 1, LANES), ('grp', 'ep'),...  4.25 us
    ppermute x1, waiting for transfers between devices, token_plan(): got_a = lax.ppermute(send_a, 'ep', chip_pairs)  4.2 us
    pallas_call x1, Pallas kernels, token_plan(): pl.pallas_call(functools.partial(weight_kernel, local, groups, capacity,...  2.84 us
    all_to_all x1, starting transfers between devices, token_plan(): lax.all_to_all(score.reshape(groups * ep_count, 1, LANES), ('grp', 'ep'),...  2.78 us
    pallas_call x1, Pallas kernels, token_plan(): pl.pallas_call(load_kernel, out_shape=(kept(expert_weight.shape, bf16), k...  2.51 us
    ppermute x7, waiting for transfers between devices, exchange(): return lax.ppermute(x, 'grp', [(i, i ^ distance) for i in range(count)])  2.16 us
    pallas_call x1, Pallas kernels, token_plan(): pl.pallas_call(functools.partial(second_kernel, local, groups, capacity),...  1.7 us
  transfers between devices with their start and end apart: 12, of which 4 were waited for; matrix products, arithmetic and copies ran while one was open for 0% of the time, Pallas kernels for 24%

profile of v5, /device:TPU:0, one launch (start us, length us, event | category | flops | bytes accessed | tf_op | source)
XLA Modules:
  0.0 39.2 jit_solution(18308388690298031387)
XLA Ops:
  0.6 1.0 %pack.1 = (bf16[32,1152]{1,0:T(8,128)(2,1)S(1)}, f32[2,3,8,128]{3,2,1,0:T(8,128)S(1)}) custom-call(s32[8,32]{1,0:T(8,128)} %bitcast.14, f32[16,32]{1,0:T(8,128)} %bitcast.13, bf16[32,1024]{1,0:T(8,128)(2,1)} %rows_hbm.1), custom_call_target="tpu_custom_call" | custom-call | tf_op jit(solution)/shard_map/pack/pallas_call | solution.py:394
  1.7 5.1 %collective-permute-start.5 = (bf16[32,1152]{1,0:T(8,128)(2,1)S(1)}, bf16[32,1152]{1,0:T(8,128)(2,1)S(1)}, u32[]{:S(2)}, u32[]{:S(2)}) collective-permute-start(bf16[32,1152]{1,0:T(8,128)(2,1)S(1)} %get-tuple-element.20.cue_ref.refs_0_), channel_id=1, source_target_pairs={{0,24},{4,28},{8,16},{12,20},{16,8},{20,12},{24,0},{28,4},{1,25},{... | collective-permute-start | bytes 221192 | tf_op jit(solution)/shard_map/ppermute | solution.py:89
  6.8 0.0 collective-permute-start.3
  6.8 1.5 %collective-permute-start = (bf16[32,1152]{1,0:T(8,128)(2,1)S(1)}, bf16[32,1152]{1,0:T(8,128)(2,1)S(1)}, u32[]{:S(2)}, u32[]{:S(2)}) collective-permute-start(bf16[32,1152]{1,0:T(8,128)(2,1)S(1)} %get-tuple-element.20.cue_ref.refs_0_), channel_id=1, source_target_pairs={{0,4},{4,0},{8,12},{12,8},{16,20},{20,16},{24,28},{28,24},{1,5},{5... | collective-permute-start | bytes 221192 | tf_op jit(solution)/shard_map/ppermute | solution.py:89
  8.3 0.8 %collective-permute-start.1 = (bf16[32,1152]{1,0:T(8,128)(2,1)S(1)}, bf16[32,1152]{1,0:T(8,128)(2,1)S(1)}, u32[]{:S(2)}, u32[]{:S(2)}) collective-permute-start(bf16[32,1152]{1,0:T(8,128)(2,1)S(1)} %get-tuple-element.20.cue_ref.refs_0_), channel_id=1, source_target_pairs={{0,8},{4,12},{8,0},{12,4},{16,24},{20,28},{24,16},{28,20},{1,9},{5... | collective-permute-start | bytes 221192 | tf_op jit(solution)/shard_map/ppermute | solution.py:89
  9.1 0.4 collective-permute-done.5.refs_6_.refs_3_
  9.5 1.9 %collective-permute-start.6 = (bf16[32,1152]{1,0:T(8,128)(2,1)S(1)}, bf16[32,1152]{1,0:T(8,128)(2,1)S(1)}, u32[]{:S(2)}, u32[]{:S(2)}) collective-permute-start(bf16[32,1152]{1,0:T(8,128)(2,1)S(1)} %collective-permute-done.5.refs_6_.refs_3_), channel_id=1, source_target_pairs={{0,4},{4,0},{8,12},{12,8},{16,20},{20,16},{24,28},{28,24},{1,5},{5... | collective-permute-start | bytes 221192 | tf_op jit(solution)/shard_map/ppermute | solution.py:89
  11.4 1.8 %collective-permute-done.3.refs_4_.refs_2_ = bf16[32,1152]{1,0:T(8,128)(2,1)S(1)} collective-permute-done((bf16[32,1152]{1,0:T(8,128)(2,1)S(1)}, bf16[32,1152]{1,0:T(8,128)(2,1)S(1)}, u32[]{:S(2)}, u32[]{:S(2)}) %collective-permute-start.3) | collective-permute-done | bytes 73760 | tf_op jit(solution)/shard_map/ppermute | solution.py:89
  13.1 1.5 %collective-permute-start.4 = (bf16[32,1152]{1,0:T(8,128)(2,1)S(1)}, bf16[32,1152]{1,0:T(8,128)(2,1)S(1)}, u32[]{:S(2)}, u32[]{:S(2)}) collective-permute-start(bf16[32,1152]{1,0:T(8,128)(2,1)S(1)} %collective-permute-done.3.refs_4_.refs_2_), channel_id=1, source_target_pairs={{0,4},{4,0},{8,12},{12,8},{16,20},{20,16},{24,28},{28,24},{1,5},{5... | collective-permute-start | bytes 221192 | tf_op jit(solution)/shard_map/ppermute | solution.py:89
  14.6 0.0 collective-permute-done.refs_1_.refs_0_
  14.6 0.1 collective-permute-start.2
  14.8 2.5 %load.1 = (bf16[2,1024,1024]{2,1,0:T(8,128)(2,1)S(1)}, bf16[2,4,2,32,1024]{4,3,2,1,0:T(8,128)(2,1)S(1)}, bf16[16,1024]{1,0:T(8,128)(2,1)S(1)}) custom-call(bf16[32,1152]{1,0:T(8,128)(2,1)S(1)} %get-tuple-element.20.cue_ref.refs_0_, bf16[2,1024,1024]{2,1,0:T(8,128)(2,1)} %refs_0_.1, bf16[2,4,2,32,1024]{4,3,2,1,0:T(8,128)(2,1)} %bitcast.11, ...), custom_call_target="tpu_custom_call" | custom-call | flops 268435456 | bytes 8388608 | tf_op jit(solution)/shard_map/load/pallas_call | solution.py:415
  17.3 0.0 collective-permute-done.1.refs_2_.refs_1_
  17.3 1.1 %first.1 = (bf16[128,1024]{1,0:T(8,128)(2,1)S(1)}, bf16[128,1024]{1,0:T(8,128)(2,1)S(1)}, f32[4,128]{1,0:T(4,128)S(1)}) custom-call(bf16[32,1152]{1,0:T(8,128)(2,1)S(1)} %get-tuple-element.20.cue_ref.refs_0_, bf16[32,1152]{1,0:T(8,128)(2,1)S(1)} %collective-permute-done.1.refs_2_.refs_1_, bf16[32,1152]{1,0:T(8,128)(2,1)S(1)} %collective-permute-done.3.refs_4_.refs_2_, ...), custom_call_target="tpu_custom_call" | custom-call | flops 536870912 | bytes 4194304 | tf_op jit(solution)/shard_map/first/pallas_call | solution.py:447
  18.4 1.5 %collective-permute-start.7 = (bf16[128,1024]{1,0:T(8,128)(2,1)S(1)}, bf16[128,1024]{1,0:T(8,128)(2,1)S(1)}, u32[]{:S(2)}, u32[]{:S(2)}) collective-permute-start(bf16[128,1024]{1,0:T(8,128)(2,1)S(1)} %get-tuple-element.26), channel_id=1, source_target_pairs={{0,2},{1,3},{2,0},{3,1},{4,6},{5,7},{6,4},{7,5},{8,10},{9,11},{10,... | collective-permute-start | bytes 786440 | tf_op jit(solution)/shard_map/ppermute | solution.py:460
  19.9 0.0 collective-permute-done.6.refs_7_.refs_3_
  19.9 0.0 collective-permute-done.4.refs_5_.refs_2_
  19.9 0.0 collective-permute-done.2.refs_3_.refs_1_
  19.9 1.7 %second.1 = (bf16[2,64,1024]{2,1,0:T(8,128)(2,1)S(1)}, bf16[2,64,1024]{2,1,0:T(8,128)(2,1)S(1)}, f32[4,2,4,128]{3,2,1,0:T(4,128)}) custom-call(bf16[32,1152]{1,0:T(8,128)(2,1)S(1)} %collective-permute-done.refs_1_.refs_0_, bf16[32,1152]{1,0:T(8,128)(2,1)S(1)} %collective-permute-done.2.refs_3_.refs_1_, ...), custom_call_target="tpu_custom_call" | custom-call | flops 536870912 | bytes 4194304 | tf_op jit(solution)/shard_map/second/pallas_call | solution.py:462
  21.6 0.0 collective-permute-start.9
  21.6 4.2 %collective-permute-done.7.got_ref = bf16[128,1024]{1,0:T(8,128)(2,1)S(1)} collective-permute-done((bf16[128,1024]{1,0:T(8,128)(2,1)S(1)}, bf16[128,1024]{1,0:T(8,128)(2,1)S(1)}, u32[]{:S(2)}, u32[]{:S(2)}) %collective-permute-start.7) | collective-permute-done | bytes 262176 | tf_op jit(solution)/shard_map/ppermute | solution.py:460
  25.8 0.1 shard_map.85
  25.8 0.1 collective-permute-start.8
  25.9 0.0 collective-permute-done.9.got_ref
  25.9 0.1 shard_map.86
  26.0 1.6 %collective-permute-start.10 = (bf16[64,1024]{1,0:T(8,128)(2,1)S(1)}, bf16[64,1024]{1,0:T(8,128)(2,1)S(1)}, u32[]{:S(2)}, u32[]{:S(2)}) collective-permute-start(bf16[64,1024]{1,0:T(8,128)(2,1)S(1)} %get-tuple-element.33), channel_id=1, source_target_pairs={{0,2},{1,3},{2,0},{3,1},{4,6},{5,7},{6,4},{7,5},{8,10},{9,11},{10,... | collective-permute-start | bytes 393224 | tf_op jit(solution)/shard_map/ppermute | solution.py:476
  27.6 2.8 %all-to-all-start = ((f32[32,1,128]{2,1,0:T(1,128)}), f32[32,1,128]{2,1,0:T(1,128)S(1)}, u32[]{:S(2)}, u32[]{:S(2)}) async-start(f32[32,1,128]{2,1,0:T(1,128)} %bitcast.6), calls=%async_computation | async-start | bytes 32768 | tf_op jit(solution)/shard_map/all_to_all | solution.py:472
  30.4 2.8 %weight.1 = (bf16[2,1024,1024]{2,1,0:T(8,128)(2,1)}, bf16[16,1024]{1,0:T(8,128)(2,1)S(1)}) custom-call(bf16[32,1152]{1,0:T(8,128)(2,1)S(1)} %get-tuple-element.20.cue_ref.refs_0_, bf16[32,1152]{1,0:T(8,128)(2,1)S(1)} %collective-permute-done.refs_1_.refs_0_, bf16[32,1152]{1,0:T(8,128)(2,1)S(1)} %collective-permute-done.1.refs_2_.refs_1_, ...), custom_call_target="tpu_custom_call" | custom-call | flops 1073741824 | bytes 6291456 | tf_op jit(solution)/shard_map/weight/pallas_call | solution.py:481
  33.2 4.3 %all-to-all-done = f32[32,1,128]{2,1,0:T(1,128)S(1)} async-done(((f32[32,1,128]{2,1,0:T(1,128)}), f32[32,1,128]{2,1,0:T(1,128)S(1)}, u32[]{:S(2)}, u32[]{:S(2)}) %all-to-all-start) | async-done | bytes 16416 | tf_op jit(solution)/shard_map/all_to_all | solution.py:472
  37.5 1.0 %router.1 = bf16[32,1024]{1,0:T(8,128)(2,1)} custom-call(f32[8,4,128]{2,1,0:T(4,128)S(1)} %bitcast.10, f32[2,3,8,128]{3,2,1,0:T(8,128)S(1)} %get-tuple-element.35.meta_ref, bf16[16,1024]{1,0:T(8,128)(2,1)S(1)} %get-tuple-element.36.w_ref), custom_call_target="tpu_custom_call" | custom-call | tf_op jit(solution)/shard_map/router/pallas_call | solution.py:506
  38.4 0.0 collective-permute-done.8.got_a
  38.4 0.0 collective-permute-done.10.got_b
  38.4 0.7 %last.1 = bf16[2,2,32,1024]{3,2,1,0:T(8,128)(2,1)} custom-call(f32[64,1024]{1,0:T(8,128)S(1)} %get-tuple-element.27.mine_a, bf16[64,1024]{1,0:T(8,128)(2,1)S(1)} %collective-permute-done.8.got_a, f32[64,1024]{1,0:T(8,128)S(1)} %get-tuple-element.32.mine_b, bf16[64,1024]{1,0:T(8,128)(2,1)S(1)} %collective-permute-done.10.got_b), custom_call_target="tpu_custom_call" | custom-call | tf_op jit(solution)/shard_map/last/pallas_call | solution.py:497
Async XLA Ops:
  1.7 7.8 %collective-permute-start.5 = (bf16[32,1152]{1,0:T(8,128)(2,1)S(1)}, bf16[32,1152]{1,0:T(8,128)(2,1)S(1)}, u32[]{:S(2)}, u32[]{:S(2)}) collective-permute-start(bf16[32,1152]{1,0:T(8,128)(2,1)S(1)} %get-tuple-element.20.cue_ref.refs_0_), channel_id=1, source_target_pairs={{0,24},{4,28},{8,16},{12,20},{16,8},{20,12},{24,0},{28,4},{1,25},{... | collective-permute-start | bytes 221192 | tf_op jit(solution)/shard_map/ppermute | solution.py:89
  6.8 6.3 %collective-permute-start.3 = (bf16[32,1152]{1,0:T(8,128)(2,1)S(1)}, bf16[32,1152]{1,0:T(8,128)(2,1)S(1)}, u32[]{:S(2)}, u32[]{:S(2)}) collective-permute-start(bf16[32,1152]{1,0:T(8,128)(2,1)S(1)} %get-tuple-element.20.cue_ref.refs_0_), channel_id=1, source_target_pairs={{0,16},{4,20},{8,24},{12,28},{16,0},{20,4},{24,8},{28,12},{1,17},{... | collective-permute-start | bytes 221192 | tf_op jit(solution)/shard_map/ppermute | solution.py:89
  6.8 7.8 %collective-permute-start = (bf16[32,1152]{1,0:T(8,128)(2,1)S(1)}, bf16[32,1152]{1,0:T(8,128)(2,1)S(1)}, u32[]{:S(2)}, u32[]{:S(2)}) collective-permute-start(bf16[32,1152]{1,0:T(8,128)(2,1)S(1)} %get-tuple-element.20.cue_ref.refs_0_), channel_id=1, source_target_pairs={{0,4},{4,0},{8,12},{12,8},{16,20},{20,16},{24,28},{28,24},{1,5},{5... | collective-permute-start | bytes 221192 | tf_op jit(solution)/shard_map/ppermute | solution.py:89
  8.3 9.0 %collective-permute-start.1 = (bf16[32,1152]{1,0:T(8,128)(2,1)S(1)}, bf16[32,1152]{1,0:T(8,128)(2,1)S(1)}, u32[]{:S(2)}, u32[]{:S(2)}) collective-permute-start(bf16[32,1152]{1,0:T(8,128)(2,1)S(1)} %get-tuple-element.20.cue_ref.refs_0_), channel_id=1, source_target_pairs={{0,8},{4,12},{8,0},{12,4},{16,24},{20,28},{24,16},{28,20},{1,9},{5... | collective-permute-start | bytes 221192 | tf_op jit(solution)/shard_map/ppermute | solution.py:89
  9.5 10.4 %collective-permute-start.6 = (bf16[32,1152]{1,0:T(8,128)(2,1)S(1)}, bf16[32,1152]{1,0:T(8,128)(2,1)S(1)}, u32[]{:S(2)}, u32[]{:S(2)}) collective-permute-start(bf16[32,1152]{1,0:T(8,128)(2,1)S(1)} %collective-permute-done.5.refs_6_.refs_3_), channel_id=1, source_target_pairs={{0,4},{4,0},{8,12},{12,8},{16,20},{20,16},{24,28},{28,24},{1,5},{5... | collective-permute-start | bytes 221192 | tf_op jit(solution)/shard_map/ppermute | solution.py:89
  13.1 6.7 %collective-permute-start.4 = (bf16[32,1152]{1,0:T(8,128)(2,1)S(1)}, bf16[32,1152]{1,0:T(8,128)(2,1)S(1)}, u32[]{:S(2)}, u32[]{:S(2)}) collective-permute-start(bf16[32,1152]{1,0:T(8,128)(2,1)S(1)} %collective-permute-done.3.refs_4_.refs_2_), channel_id=1, source_target_pairs={{0,4},{4,0},{8,12},{12,8},{16,20},{20,16},{24,28},{28,24},{1,5},{5... | collective-permute-start | bytes 221192 | tf_op jit(solution)/shard_map/ppermute | solution.py:89
  14.6 5.2 %collective-permute-start.2 = (bf16[32,1152]{1,0:T(8,128)(2,1)S(1)}, bf16[32,1152]{1,0:T(8,128)(2,1)S(1)}, u32[]{:S(2)}, u32[]{:S(2)}) collective-permute-start(bf16[32,1152]{1,0:T(8,128)(2,1)S(1)} %collective-permute-done.refs_1_.refs_0_), channel_id=1, source_target_pairs={{0,8},{4,12},{8,0},{12,4},{16,24},{20,28},{24,16},{28,20},{1,9},{5... | collective-permute-start | bytes 221192 | tf_op jit(solution)/shard_map/ppermute | solution.py:89
  18.4 7.4 %collective-permute-start.7 = (bf16[128,1024]{1,0:T(8,128)(2,1)S(1)}, bf16[128,1024]{1,0:T(8,128)(2,1)S(1)}, u32[]{:S(2)}, u32[]{:S(2)}) collective-permute-start(bf16[128,1024]{1,0:T(8,128)(2,1)S(1)} %get-tuple-element.26), channel_id=1, source_target_pairs={{0,2},{1,3},{2,0},{3,1},{4,6},{5,7},{6,4},{7,5},{8,10},{9,11},{10,... | collective-permute-start | bytes 786440 | tf_op jit(solution)/shard_map/ppermute | solution.py:460
  21.6 4.3 %collective-permute-start.9 = (bf16[2,64,1024]{2,1,0:T(8,128)(2,1)S(1)}, bf16[2,64,1024]{2,1,0:T(8,128)(2,1)S(1)}, u32[]{:S(2)}, u32[]{:S(2)}) collective-permute-start(bf16[2,64,1024]{2,1,0:T(8,128)(2,1)S(1)} %get-tuple-element.31), channel_id=1, source_target_pairs={{0,1},{1,0},{2,3},{3,2},{4,5},{5,4},{6,7},{7,6},{8,9},{9,8},{10,11... | collective-permute-start | bytes 786440 | tf_op jit(solution)/shard_map/ppermute | solution.py:471
  25.8 12.6 %collective-permute-start.8 = (bf16[64,1024]{1,0:T(8,128)(2,1)S(1)}, bf16[64,1024]{1,0:T(8,128)(2,1)S(1)}, u32[]{:S(2)}, u32[]{:S(2)}) collective-permute-start(bf16[64,1024]{1,0:T(8,128)(2,1)S(1)} %get-tuple-element.28), channel_id=1, source_target_pairs={{0,1},{1,0},{2,3},{3,2},{4,5},{5,4},{6,7},{7,6},{8,9},{9,8},{10,11... | collective-permute-start | bytes 393224 | tf_op jit(solution)/shard_map/ppermute | solution.py:478
  26.0 12.4 %collective-permute-start.10 = (bf16[64,1024]{1,0:T(8,128)(2,1)S(1)}, bf16[64,1024]{1,0:T(8,128)(2,1)S(1)}, u32[]{:S(2)}, u32[]{:S(2)}) collective-permute-start(bf16[64,1024]{1,0:T(8,128)(2,1)S(1)} %get-tuple-element.33), channel_id=1, source_target_pairs={{0,2},{1,3},{2,0},{3,1},{4,6},{5,7},{6,4},{7,5},{8,10},{9,11},{10,... | collective-permute-start | bytes 393224 | tf_op jit(solution)/shard_map/ppermute | solution.py:476
  27.6 9.9 %all-to-all-start = ((f32[32,1,128]{2,1,0:T(1,128)}), f32[32,1,128]{2,1,0:T(1,128)S(1)}, u32[]{:S(2)}, u32[]{:S(2)}) async-start(f32[32,1,128]{2,1,0:T(1,128)} %bitcast.6), calls=%async_computation | async-start | bytes 32768 | tf_op jit(solution)/shard_map/all_to_all | solution.py:472

commit v6 on v5

--- a/solution.py
+++ b/solution.py
@@ -90,8 +90,8 @@
 
 
 def swap_order(count):
-    top, rest = count - 2, list(range(2, count - 2, 2))
-    return [top, 1] + rest + [3, top ^ 1] + [d ^ 1 for d in rest if d != 2]
+    far = list(range(count - 2, 0, -2))
+    return far[:-1] + [1, 2, far[0] ^ 1, 3] + [d ^ 1 for d in far[1:-1]]
 
 
 def gather_blocks(x):
@@ -129,25 +129,36 @@
     copies[1].wait()
     ids = ids_ref[...]
     upto = (iota((tokens, tokens), 0) <= iota((tokens, tokens), 1)).astype(jnp.bfloat16)
-    sig, chosen, ranks = [], [], []
+    named, sig, chosen, ranks = [], [], [], []
     for l in range(local):
         expert = iota((groups, tokens), 0) * local + l
         hit = jnp.zeros((groups, tokens), jnp.float32)
         for i in range(top_count):
             hit = hit + (ids[i : i + 1, :] == expert).astype(jnp.float32)
         value = jax.nn.sigmoid(logits_ref[pl.ds(l, groups, stride=local), :])
+        named.append(hit)
         sig.append(value)
         chosen.append(hit * value)
         count = jnp.dot(hit.astype(jnp.bfloat16), upto, preferred_element_type=jnp.float32)
         ranks.append(hit * count)
     total = sum(jnp.sum(c, axis=0, keepdims=True) for c in chosen)
     probs = [route_scale * c / total for c in chosen]
-    stack = jnp.concatenate(probs + ranks, axis=0).astype(jnp.bfloat16)
     lanes = packed_ref.shape[1] - features
-    spread = (iota((stack.shape[0], lanes), 0) == iota((stack.shape[0], lanes), 1)).astype(
-        jnp.bfloat16
-    )
-    packed_ref[:, features:] = contract_rows(stack, spread).astype(jnp.bfloat16)
+    count = local * groups
+    rest = jnp.zeros((lanes - 2 * count, tokens), jnp.float32)
+    none = jnp.zeros((count, tokens), jnp.float32)
+    table = jnp.concatenate(
+        [
+            jnp.concatenate(probs + [none, rest], axis=0),
+            jnp.concatenate([none] + named + [rest], axis=0),
+        ],
+        axis=1,
+    ).astype(jnp.bfloat16)
+    at, of = iota((tokens, 2 * tokens), 0), iota((tokens, 2 * tokens), 1)
+    weigh = ((of == at) | ((of >= tokens) & (of - tokens <= at))).astype(jnp.bfloat16)
+    packed_ref[:, features:] = lax.dot_general(
+        weigh, table, (((1,), (1,)), ((), ())), preferred_element_type=jnp.float32
+    ).astype(jnp.bfloat16)
     for l in range(local):
         for k, value in enumerate((sig[l], probs[l], ranks[l])):
             meta_ref[l, k] = jnp.zeros(meta_ref.shape[2:], jnp.float32)
@@ -155,7 +166,7 @@
     copies[2].wait()
 
 
-def half_of(parity, experts, groups, capacity, blocks, saved_ref, w_ref, store):
+def half_of(parity, experts, groups, capacity, blocks, saved_ref, w_ref, store, ready=None):
     local = len(experts)
     block_rows, features = blocks[0].shape[0], blocks[0].shape[1] - LANES
     width = w_ref.shape[2]
@@ -178,13 +189,15 @@
         lane = l * groups + own
         prob = jnp.sum(jnp.where(row == lane, aux, 0.0), axis=0, keepdims=True)
         rank = jnp.sum(jnp.where(row == local * groups + lane, aux, 0.0), axis=0, keepdims=True)
-        place = jnp.where(rank > 0, source * capacity + rank.astype(jnp.int32) - 1, -1)
+        place = jnp.where(prob > 0, source * capacity + rank.astype(jnp.int32) - 1, -1)
         pick = slot == place
         picks.append(pick.astype(jnp.float32).astype(jnp.bfloat16))
         scales.append(jnp.sum(jnp.where(pick, prob, 0.0), axis=1, keepdims=True))
     grads = jnp.dot(
         jnp.concatenate(picks, axis=0), rows, preferred_element_type=jnp.float32
     ).astype(jnp.bfloat16)
+    if ready is not None:
+        ready()
     for i, l in enumerate(experts):
         score = jnp.zeros((span, LANES), jnp.float32)
         for n in range(width // cols):
@@ -212,11 +225,10 @@
     return jnp.where(side == 0, sent, turned)
 
 
-def load_kernel(cue_ref, *refs):
-    sources, targets, sems = refs[:3], refs[3:6], refs[6]
+def load_kernel(cue_ref, source_ref, out_ref, sems):
     copies = [
-        pltpu.make_async_copy(source, target, sems.at[i])
-        for i, (source, target) in enumerate(zip(sources, targets))
+        pltpu.make_async_copy(source_ref.at[i], out_ref.at[i], sems.at[i])
+        for i in range(source_ref.shape[0])
     ]
     for copy in copies:
         copy.start()
@@ -227,8 +239,15 @@
 def first_kernel(groups, capacity, *refs):
     count = groups // 2
     blocks = refs[:count]
-    w_ref, h_ref, keep_ref, send_ref, score_ref = refs[count:]
+    w_ref, *sources = refs[count : count + 3]
+    h_ref, r_ref, keep_ref, send_ref, score_ref, sems = refs[count + 3 :]
     bit = lax.axis_index("ep") // 2
+    copies = [
+        pltpu.make_async_copy(source, target, sems.at[i])
+        for i, (source, target) in enumerate(zip(sources, (h_ref, r_ref)))
+    ]
+    for copy in copies:
+        copy.start()
 
     def store(i, part, value):
         (send_ref, keep_ref)[i][:, part] = value
@@ -242,7 +261,9 @@
         h_ref,
         w_ref,
         store,
-    )
+        copies[0].wait,
+    )
+    copies[1].wait()
 
 
 def second_kernel(local, groups, capacity, *refs):
@@ -292,7 +313,7 @@
         lane = l * groups + own
         prob = jnp.sum(jnp.where(at == lane, aux, 0.0), axis=1, keepdims=True)
         rank = jnp.sum(jnp.where(at == local * groups + lane, aux, 0.0), axis=1, keepdims=True)
-        place = jnp.where(rank > 0, source * capacity + rank.astype(jnp.int32) - 1, -1)
+        place = jnp.where(prob > 0, source * capacity + rank.astype(jnp.int32) - 1, -1)
         pick = jnp.where(place == iota((tokens, span), 1), prob, 0.0).astype(jnp.bfloat16)
         scaled_buf[...] = jnp.dot(
             turned_buf[...], pick, preferred_element_type=jnp.float32
@@ -412,25 +433,16 @@
     saved_shape = (local, groups // 2, 2, capacity, width)
     sums = [kept((local, span // 4, width), bf16)] * 2
     work = slot_count * features * width
-    weights, saved, projection = pl.pallas_call(
+    weights = pl.pallas_call(
         load_kernel,
-        out_shape=(
-            kept(expert_weight.shape, bf16),
-            kept(saved_shape, bf16),
-            kept(router_weight.shape, bf16),
-        ),
-        in_specs=[vmem] + [hbm] * 3,
-        out_specs=(vmem,) * 3,
-        scratch_shapes=[pltpu.SemaphoreType.DMA((3,))],
+        out_shape=kept(expert_weight.shape, bf16),
+        in_specs=[vmem, hbm],
+        out_specs=vmem,
+        scratch_shapes=[pltpu.SemaphoreType.DMA((local,))],
         compiler_params=limit(2),
         cost_estimate=cost(work // 2, 8 * 2**20),
         name="load",
-    )(
-        blocks[0],
-        away_from_vmem(expert_weight),
-        away_from_vmem(hidden_saved.reshape(saved_shape)),
-        away_from_vmem(router_weight),
-    )
+    )(blocks[0], away_from_vmem(expert_weight))
 
     core_pairs = [(i, i ^ 1) for i in range(ep_count)]
     chip_pairs = [(i, i ^ 2) for i in range(ep_count)]
@@ -444,19 +456,27 @@
             compiler_params=limit(2),
         )(held(keep), held(got))
 
-    keep_a, send_a, score_a = pl.pallas_call(
+    saved, projection, keep_a, send_a, score_a = pl.pallas_call(
         functools.partial(first_kernel, groups, capacity),
         out_shape=(
+            kept(saved_shape, bf16),
+            kept(router_weight.shape, bf16),
             kept((span // 2, width), bf16),
             kept((span // 2, width), bf16),
             kept((groups // 2, LANES), f32),
         ),
-        in_specs=[vmem] * (groups // 2 + 2),
-        out_specs=(vmem,) * 3,
+        in_specs=[vmem] * (groups // 2 + 1) + [hbm] * 2,
+        out_specs=(vmem,) * 5,
+        scratch_shapes=[pltpu.SemaphoreType.DMA((2,))],
         compiler_params=limit(8),
         cost_estimate=cost(work, 4 * 2**20),
         name="first",
-    )(*blocks[0::2], held(weights), held(saved))
+    )(
+        *blocks[0::2],
+        held(weights),
+        away_from_vmem(hidden_saved.reshape(saved_shape)),
+        away_from_vmem(router_weight),
+    )
     got_a = lax.ppermute(send_a, "ep", chip_pairs)
 
     keep_b, send_b, score = pl.pallas_call(

time: 39.4 us -> 40.2 us (1.020)
  Pallas kernels: 11 us -> 11.8 us
    pallas_call x1, Pallas kernels: 1.1 us -> 2.24 us  [token_plan(): pl.pallas_call(functools.partial(first_kernel, groups, capacity), out_sha...]
  transfers between devices with their start and end apart: 12 -> 12, of which waited for: 4 -> 4; matrix products, arithmetic and copies ran while one was open for 0% -> 0% of each run, Pallas kernels for 24% -> 25%
where the time goes in v6:
time: 40.2 us; the launch traced here: 40 us
  starting transfers between devices  16.8 us (42%)
  Pallas kernels  11.8 us (29%)
  waiting for transfers between devices  10.6 us (26%)
  between operations  0.72 us (2%)
    ppermute x7, starting transfers between devices, exchange(): return lax.ppermute(x, 'grp', [(i, i ^ distance) for i in range(count)])  10.9 us
    all_to_all x1, waiting for transfers between devices, token_plan(): lax.all_to_all(score.reshape(groups * ep_count, 1, LANES), ('grp', 'ep'),...  4.24 us
    ppermute x1, waiting for transfers between devices, token_plan(): got_a = lax.ppermute(send_a, 'ep', chip_pairs)  4.21 us
    pallas_call x1, Pallas kernels, token_plan(): pl.pallas_call(functools.partial(weight_kernel, local, groups, capacity,...  2.85 us
    all_to_all x1, starting transfers between devices, token_plan(): lax.all_to_all(score.reshape(groups * ep_count, 1, LANES), ('grp', 'ep'),...  2.78 us
    pallas_call x1, Pallas kernels, token_plan(): pl.pallas_call(functools.partial(first_kernel, groups, capacity), out_sha...  2.24 us
    pallas_call x1, Pallas kernels, token_plan(): pl.pallas_call(load_kernel, out_shape=kept(expert_weight.shape, bf16), in...  2.24 us
    ppermute x7, waiting for transfers between devices, exchange(): return lax.ppermute(x, 'grp', [(i, i ^ distance) for i in range(count)])  2.16 us
  transfers between devices with their start and end apart: 12, of which 4 were waited for; matrix products, arithmetic and copies ran while one was open for 0% of the time, Pallas kernels for 25%

profile of v6, /device:TPU:0, one launch (start us, length us, event | category | flops | bytes accessed | tf_op | source)
XLA Modules:
  0.0 40.0 jit_solution(6390752186380541443)
XLA Ops:
  0.6 1.0 %pack.1 = (bf16[32,1152]{1,0:T(8,128)(2,1)S(1)}, f32[2,3,8,128]{3,2,1,0:T(8,128)S(1)}) custom-call(s32[8,32]{1,0:T(8,128)} %bitcast.14, f32[16,32]{1,0:T(8,128)} %bitcast.13, bf16[32,1024]{1,0:T(8,128)(2,1)} %rows_hbm.1), custom_call_target="tpu_custom_call" | custom-call | tf_op jit(solution)/shard_map/pack/pallas_call | solution.py:415
  1.6 5.1 %collective-permute-start.5 = (bf16[32,1152]{1,0:T(8,128)(2,1)S(1)}, bf16[32,1152]{1,0:T(8,128)(2,1)S(1)}, u32[]{:S(2)}, u32[]{:S(2)}) collective-permute-start(bf16[32,1152]{1,0:T(8,128)(2,1)S(1)} %get-tuple-element.19.cue_ref.refs_0_), channel_id=1, source_target_pairs={{0,24},{4,28},{8,16},{12,20},{16,8},{20,12},{24,0},{28,4},{1,25},{... | collective-permute-start | bytes 221192 | tf_op jit(solution)/shard_map/ppermute | solution.py:89
  6.8 0.0 collective-permute-start.3
  6.8 1.5 %collective-permute-start = (bf16[32,1152]{1,0:T(8,128)(2,1)S(1)}, bf16[32,1152]{1,0:T(8,128)(2,1)S(1)}, u32[]{:S(2)}, u32[]{:S(2)}) collective-permute-start(bf16[32,1152]{1,0:T(8,128)(2,1)S(1)} %get-tuple-element.19.cue_ref.refs_0_), channel_id=1, source_target_pairs={{0,4},{4,0},{8,12},{12,8},{16,20},{20,16},{24,28},{28,24},{1,5},{5... | collective-permute-start | bytes 221192 | tf_op jit(solution)/shard_map/ppermute | solution.py:89
  8.2 0.8 %collective-permute-start.1 = (bf16[32,1152]{1,0:T(8,128)(2,1)S(1)}, bf16[32,1152]{1,0:T(8,128)(2,1)S(1)}, u32[]{:S(2)}, u32[]{:S(2)}) collective-permute-start(bf16[32,1152]{1,0:T(8,128)(2,1)S(1)} %get-tuple-element.19.cue_ref.refs_0_), channel_id=1, source_target_pairs={{0,8},{4,12},{8,0},{12,4},{16,24},{20,28},{24,16},{28,20},{1,9},{5... | collective-permute-start | bytes 221192 | tf_op jit(solution)/shard_map/ppermute | solution.py:89
  9.0 0.4 collective-permute-done.5.refs_3_.refs_6_
  9.4 1.9 %collective-permute-start.6 = (bf16[32,1152]{1,0:T(8,128)(2,1)S(1)}, bf16[32,1152]{1,0:T(8,128)(2,1)S(1)}, u32[]{:S(2)}, u32[]{:S(2)}) collective-permute-start(bf16[32,1152]{1,0:T(8,128)(2,1)S(1)} %collective-permute-done.5.refs_3_.refs_6_), channel_id=1, source_target_pairs={{0,4},{4,0},{8,12},{12,8},{16,20},{20,16},{24,28},{28,24},{1,5},{5... | collective-permute-start | bytes 221192 | tf_op jit(solution)/shard_map/ppermute | solution.py:89
  11.3 1.8 %collective-permute-done.3.refs_2_.refs_4_ = bf16[32,1152]{1,0:T(8,128)(2,1)S(1)} collective-permute-done((bf16[32,1152]{1,0:T(8,128)(2,1)S(1)}, bf16[32,1152]{1,0:T(8,128)(2,1)S(1)}, u32[]{:S(2)}, u32[]{:S(2)}) %collective-permute-start.3) | collective-permute-done | bytes 73760 | tf_op jit(solution)/shard_map/ppermute | solution.py:89
  13.1 1.5 %collective-permute-start.4 = (bf16[32,1152]{1,0:T(8,128)(2,1)S(1)}, bf16[32,1152]{1,0:T(8,128)(2,1)S(1)}, u32[]{:S(2)}, u32[]{:S(2)}) collective-permute-start(bf16[32,1152]{1,0:T(8,128)(2,1)S(1)} %collective-permute-done.3.refs_2_.refs_4_), channel_id=1, source_target_pairs={{0,4},{4,0},{8,12},{12,8},{16,20},{20,16},{24,28},{28,24},{1,5},{5... | collective-permute-start | bytes 221192 | tf_op jit(solution)/shard_map/ppermute | solution.py:89
  14.6 0.0 collective-permute-done.refs_1_.refs_0_
  14.6 0.1 collective-permute-start.2
  14.7 2.2 %load.1.refs_4_ = bf16[2,1024,1024]{2,1,0:T(8,128)(2,1)S(1)} custom-call(bf16[32,1152]{1,0:T(8,128)(2,1)S(1)} %get-tuple-element.19.cue_ref.refs_0_, bf16[2,1024,1024]{2,1,0:T(8,128)(2,1)} %source_ref.1), custom_call_target="tpu_custom_call" | custom-call | flops 268435456 | bytes 8388608 | tf_op jit(solution)/shard_map/load/pallas_call | solution.py:436
  16.9 0.0 collective-permute-done.1.refs_1_.refs_2_
  16.9 2.2 %first.1 = (bf16[2,4,2,32,1024]{4,3,2,1,0:T(8,128)(2,1)S(1)}, bf16[16,1024]{1,0:T(8,128)(2,1)S(1)}, bf16[128,1024]{1,0:T(8,128)(2,1)S(1)}, bf16[128,1024]{1,0:T(8,128)(2,1)S(1)}, f32[4,128]{1,0:T(4,128)S(1)}) custom-call(bf16[32,1152]{1,0:T(8,128)(2,1)S(1)} %get-tuple-element.19.cue_ref.refs_0_, bf16[32,1152]{1,0:T(8,128)(2,1)S(1)} %collective-permute-done.1.refs_1_.refs_2_, ...), custom_call_target="tpu_custom_call" | custom-call | flops 536870912 | bytes 4194304 | tf_op jit(solution)/shard_map/first/pallas_call | solution.py:459
  19.2 1.5 %collective-permute-start.7 = (bf16[128,1024]{1,0:T(8,128)(2,1)S(1)}, bf16[128,1024]{1,0:T(8,128)(2,1)S(1)}, u32[]{:S(2)}, u32[]{:S(2)}) collective-permute-start(bf16[128,1024]{1,0:T(8,128)(2,1)S(1)} %get-tuple-element.24), channel_id=1, source_target_pairs={{0,2},{1,3},{2,0},{3,1},{4,6},{5,7},{6,4},{7,5},{8,10},{9,11},{10,... | collective-permute-start | bytes 786440 | tf_op jit(solution)/shard_map/ppermute | solution.py:480
  20.7 0.0 collective-permute-done.6.refs_7_.refs_3_
  20.7 0.0 collective-permute-done.4.refs_5_.refs_2_
  20.7 0.0 collective-permute-done.2.refs_3_.refs_1_
  20.7 1.7 %second.1 = (bf16[2,64,1024]{2,1,0:T(8,128)(2,1)S(1)}, bf16[2,64,1024]{2,1,0:T(8,128)(2,1)S(1)}, f32[4,2,4,128]{3,2,1,0:T(4,128)}) custom-call(bf16[32,1152]{1,0:T(8,128)(2,1)S(1)} %collective-permute-done.refs_1_.refs_0_, bf16[32,1152]{1,0:T(8,128)(2,1)S(1)} %collective-permute-done.2.refs_3_.refs_1_, ...), custom_call_target="tpu_custom_call" | custom-call | flops 536870912 | bytes 4194304 | tf_op jit(solution)/shard_map/second/pallas_call | solution.py:482
  22.4 0.0 collective-permute-start.9
  22.4 4.2 %collective-permute-done.7.got_ref = bf16[128,1024]{1,0:T(8,128)(2,1)S(1)} collective-permute-done((bf16[128,1024]{1,0:T(8,128)(2,1)S(1)}, bf16[128,1024]{1,0:T(8,128)(2,1)S(1)}, u32[]{:S(2)}, u32[]{:S(2)}) %collective-permute-start.7) | collective-permute-done | bytes 262176 | tf_op jit(solution)/shard_map/ppermute | solution.py:480
  26.6 0.1 shard_map.85
  26.6 0.1 collective-permute-start.8
  26.7 0.0 collective-permute-done.9.got_ref
  26.7 0.1 shard_map.86
  26.8 1.6 %collective-permute-start.10 = (bf16[64,1024]{1,0:T(8,128)(2,1)S(1)}, bf16[64,1024]{1,0:T(8,128)(2,1)S(1)}, u32[]{:S(2)}, u32[]{:S(2)}) collective-permute-start(bf16[64,1024]{1,0:T(8,128)(2,1)S(1)} %get-tuple-element.31), channel_id=1, source_target_pairs={{0,2},{1,3},{2,0},{3,1},{4,6},{5,7},{6,4},{7,5},{8,10},{9,11},{10,... | collective-permute-start | bytes 393224 | tf_op jit(solution)/shard_map/ppermute | solution.py:496
  28.4 2.8 %all-to-all-start = ((f32[32,1,128]{2,1,0:T(1,128)}), f32[32,1,128]{2,1,0:T(1,128)S(1)}, u32[]{:S(2)}, u32[]{:S(2)}) async-start(f32[32,1,128]{2,1,0:T(1,128)} %bitcast.6), calls=%async_computation | async-start | bytes 32768 | tf_op jit(solution)/shard_map/all_to_all | solution.py:492
  31.2 2.8 %weight.1 = (bf16[2,1024,1024]{2,1,0:T(8,128)(2,1)}, bf16[16,1024]{1,0:T(8,128)(2,1)S(1)}) custom-call(bf16[32,1152]{1,0:T(8,128)(2,1)S(1)} %get-tuple-element.19.cue_ref.refs_0_, bf16[32,1152]{1,0:T(8,128)(2,1)S(1)} %collective-permute-done.refs_1_.refs_0_, bf16[32,1152]{1,0:T(8,128)(2,1)S(1)} %collective-permute-done.1.refs_1_.refs_2_, ...), custom_call_target="tpu_custom_call" | custom-call | flops 1073741824 | bytes 6291456 | tf_op jit(solution)/shard_map/weight/pallas_call | solution.py:501
  34.0 4.2 %all-to-all-done = f32[32,1,128]{2,1,0:T(1,128)S(1)} async-done(((f32[32,1,128]{2,1,0:T(1,128)}), f32[32,1,128]{2,1,0:T(1,128)S(1)}, u32[]{:S(2)}, u32[]{:S(2)}) %all-to-all-start) | async-done | bytes 16416 | tf_op jit(solution)/shard_map/all_to_all | solution.py:492
  38.3 1.0 %router.1 = bf16[32,1024]{1,0:T(8,128)(2,1)} custom-call(f32[8,4,128]{2,1,0:T(4,128)S(1)} %bitcast.10, f32[2,3,8,128]{3,2,1,0:T(8,128)S(1)} %get-tuple-element.33.meta_ref, bf16[16,1024]{1,0:T(8,128)(2,1)S(1)} %get-tuple-element.34.w_ref), custom_call_target="tpu_custom_call" | custom-call | tf_op jit(solution)/shard_map/router/pallas_call | solution.py:526
  39.2 0.0 collective-permute-done.8.got_a
  39.2 0.0 collective-permute-done.10.got_b
  39.2 0.7 %last.1 = bf16[2,2,32,1024]{3,2,1,0:T(8,128)(2,1)} custom-call(f32[64,1024]{1,0:T(8,128)S(1)} %get-tuple-element.25.mine_a, bf16[64,1024]{1,0:T(8,128)(2,1)S(1)} %collective-permute-done.8.got_a, f32[64,1024]{1,0:T(8,128)S(1)} %get-tuple-element.30.mine_b, bf16[64,1024]{1,0:T(8,128)(2,1)S(1)} %collective-permute-done.10.got_b), custom_call_target="tpu_custom_call" | custom-call | tf_op jit(solution)/shard_map/last/pallas_call | solution.py:517
Async XLA Ops:
  1.6 7.8 %collective-permute-start.5 = (bf16[32,1152]{1,0:T(8,128)(2,1)S(1)}, bf16[32,1152]{1,0:T(8,128)(2,1)S(1)}, u32[]{:S(2)}, u32[]{:S(2)}) collective-permute-start(bf16[32,1152]{1,0:T(8,128)(2,1)S(1)} %get-tuple-element.19.cue_ref.refs_0_), channel_id=1, source_target_pairs={{0,24},{4,28},{8,16},{12,20},{16,8},{20,12},{24,0},{28,4},{1,25},{... | collective-permute-start | bytes 221192 | tf_op jit(solution)/shard_map/ppermute | solution.py:89
  6.8 6.3 %collective-permute-start.3 = (bf16[32,1152]{1,0:T(8,128)(2,1)S(1)}, bf16[32,1152]{1,0:T(8,128)(2,1)S(1)}, u32[]{:S(2)}, u32[]{:S(2)}) collective-permute-start(bf16[32,1152]{1,0:T(8,128)(2,1)S(1)} %get-tuple-element.19.cue_ref.refs_0_), channel_id=1, source_target_pairs={{0,16},{4,20},{8,24},{12,28},{16,0},{20,4},{24,8},{28,12},{1,17},{... | collective-permute-start | bytes 221192 | tf_op jit(solution)/shard_map/ppermute | solution.py:89
  6.8 7.8 %collective-permute-start = (bf16[32,1152]{1,0:T(8,128)(2,1)S(1)}, bf16[32,1152]{1,0:T(8,128)(2,1)S(1)}, u32[]{:S(2)}, u32[]{:S(2)}) collective-permute-start(bf16[32,1152]{1,0:T(8,128)(2,1)S(1)} %get-tuple-element.19.cue_ref.refs_0_), channel_id=1, source_target_pairs={{0,4},{4,0},{8,12},{12,8},{16,20},{20,16},{24,28},{28,24},{1,5},{5... | collective-permute-start | bytes 221192 | tf_op jit(solution)/shard_map/ppermute | solution.py:89
  8.2 8.7 %collective-permute-start.1 = (bf16[32,1152]{1,0:T(8,128)(2,1)S(1)}, bf16[32,1152]{1,0:T(8,128)(2,1)S(1)}, u32[]{:S(2)}, u32[]{:S(2)}) collective-permute-start(bf16[32,1152]{1,0:T(8,128)(2,1)S(1)} %get-tuple-element.19.cue_ref.refs_0_), channel_id=1, source_target_pairs={{0,8},{4,12},{8,0},{12,4},{16,24},{20,28},{24,16},{28,20},{1,9},{5... | collective-permute-start | bytes 221192 | tf_op jit(solution)/shard_map/ppermute | solution.py:89
  9.4 11.2 %collective-permute-start.6 = (bf16[32,1152]{1,0:T(8,128)(2,1)S(1)}, bf16[32,1152]{1,0:T(8,128)(2,1)S(1)}, u32[]{:S(2)}, u32[]{:S(2)}) collective-permute-start(bf16[32,1152]{1,0:T(8,128)(2,1)S(1)} %collective-permute-done.5.refs_3_.refs_6_), channel_id=1, source_target_pairs={{0,4},{4,0},{8,12},{12,8},{16,20},{20,16},{24,28},{28,24},{1,5},{5... | collective-permute-start | bytes 221192 | tf_op jit(solution)/shard_map/ppermute | solution.py:89
  13.1 7.6 %collective-permute-start.4 = (bf16[32,1152]{1,0:T(8,128)(2,1)S(1)}, bf16[32,1152]{1,0:T(8,128)(2,1)S(1)}, u32[]{:S(2)}, u32[]{:S(2)}) collective-permute-start(bf16[32,1152]{1,0:T(8,128)(2,1)S(1)} %collective-permute-done.3.refs_2_.refs_4_), channel_id=1, source_target_pairs={{0,4},{4,0},{8,12},{12,8},{16,20},{20,16},{24,28},{28,24},{1,5},{5... | collective-permute-start | bytes 221192 | tf_op jit(solution)/shard_map/ppermute | solution.py:89
  14.6 6.1 %collective-permute-start.2 = (bf16[32,1152]{1,0:T(8,128)(2,1)S(1)}, bf16[32,1152]{1,0:T(8,128)(2,1)S(1)}, u32[]{:S(2)}, u32[]{:S(2)}) collective-permute-start(bf16[32,1152]{1,0:T(8,128)(2,1)S(1)} %collective-permute-done.refs_1_.refs_0_), channel_id=1, source_target_pairs={{0,8},{4,12},{8,0},{12,4},{16,24},{20,28},{24,16},{28,20},{1,9},{5... | collective-permute-start | bytes 221192 | tf_op jit(solution)/shard_map/ppermute | solution.py:89
  19.2 7.4 %collective-permute-start.7 = (bf16[128,1024]{1,0:T(8,128)(2,1)S(1)}, bf16[128,1024]{1,0:T(8,128)(2,1)S(1)}, u32[]{:S(2)}, u32[]{:S(2)}) collective-permute-start(bf16[128,1024]{1,0:T(8,128)(2,1)S(1)} %get-tuple-element.24), channel_id=1, source_target_pairs={{0,2},{1,3},{2,0},{3,1},{4,6},{5,7},{6,4},{7,5},{8,10},{9,11},{10,... | collective-permute-start | bytes 786440 | tf_op jit(solution)/shard_map/ppermute | solution.py:480
  22.4 4.4 %collective-permute-start.9 = (bf16[2,64,1024]{2,1,0:T(8,128)(2,1)S(1)}, bf16[2,64,1024]{2,1,0:T(8,128)(2,1)S(1)}, u32[]{:S(2)}, u32[]{:S(2)}) collective-permute-start(bf16[2,64,1024]{2,1,0:T(8,128)(2,1)S(1)} %get-tuple-element.29), channel_id=1, source_target_pairs={{0,1},{1,0},{2,3},{3,2},{4,5},{5,4},{6,7},{7,6},{8,9},{9,8},{10,11... | collective-permute-start | bytes 786440 | tf_op jit(solution)/shard_map/ppermute | solution.py:491
  26.6 12.6 %collective-permute-start.8 = (bf16[64,1024]{1,0:T(8,128)(2,1)S(1)}, bf16[64,1024]{1,0:T(8,128)(2,1)S(1)}, u32[]{:S(2)}, u32[]{:S(2)}) collective-permute-start(bf16[64,1024]{1,0:T(8,128)(2,1)S(1)} %get-tuple-element.26), channel_id=1, source_target_pairs={{0,1},{1,0},{2,3},{3,2},{4,5},{5,4},{6,7},{7,6},{8,9},{9,8},{10,11... | collective-permute-start | bytes 393224 | tf_op jit(solution)/shard_map/ppermute | solution.py:498
  26.8 12.4 %collective-permute-start.10 = (bf16[64,1024]{1,0:T(8,128)(2,1)S(1)}, bf16[64,1024]{1,0:T(8,128)(2,1)S(1)}, u32[]{:S(2)}, u32[]{:S(2)}) collective-permute-start(bf16[64,1024]{1,0:T(8,128)(2,1)S(1)} %get-tuple-element.31), channel_id=1, source_target_pairs={{0,2},{1,3},{2,0},{3,1},{4,6},{5,7},{6,4},{7,5},{8,10},{9,11},{10,... | collective-permute-start | bytes 393224 | tf_op jit(solution)/shard_map/ppermute | solution.py:496
  28.4 9.9 %all-to-all-start = ((f32[32,1,128]{2,1,0:T(1,128)}), f32[32,1,128]{2,1,0:T(1,128)S(1)}, u32[]{:S(2)}, u32[]{:S(2)}) async-start(f32[32,1,128]{2,1,0:T(1,128)} %bitcast.6), calls=%async_computation | async-start | bytes 32768 | tf_op jit(solution)/shard_map/all_to_all | solution.py:492
